TPU v7x, 512 devices: a whole 4x8x8 slice. The times are simulated.
512 devices in a mesh: replica: 64 (over z, x, core), spatial: 8 (over y).
Axes of the slice: x: 4, y: 8, z: 8, core: 2. Of those that a mesh axis runs over, the one named last changes fastest.
Arguments:
- grads: bfloat16 [64, 8, 852992], P('replica', 'spatial'), may hold values from -16 to 16
- master: float32 [852992], P(('replica', 'spatial')), may hold values from -0.06 to 0.06
- velocity: float32 [852992], P(('replica', 'spatial')), may hold values from -0.3 to 0.3
- layer_offsets: int32 [6], replicated, may hold values from 0 to 852736, as said below
- layer_sizes: int32 [6], replicated, may hold values from 256 to 589824
- lars_skip: int32 [6], replicated, may hold values from 0 to 1
Outputs:
- new_weights: bfloat16 [852992], replicated
- new_master: float32 [852992], P(('replica', 'spatial'))
- new_velocity: float32 [852992], P(('replica', 'spatial'))
Inputs may be any that keep to these rules, and one draw needn't show every extreme that they name: layer_offsets, layer_sizes and lars_skip describe the six tensors (a 256 x 1024 convolution, a 256 x 256 x 9 convolution, and two gains and two shifts of 256 entries) laid end to end in some order without gaps, the last of them always a gain or a shift; lars_skip is 1 exactly for the gains and shifts.
All inputs are finite; a program needn't handle non-finite values.
Results may differ from a plain program's by a relative error of at most 0.001.
Values may be sent and summed in bfloat16 or wider, within the bound.
No kernel may reach another device: no remote copies, remote signals or barrier semaphores. Data moves between devices by JAX's collectives and lax.ppermute only.
A program may use at most 64 MiB of HBM per device.

v0:
```python
import jax
import jax.numpy as jnp
from jax import lax
from jax.sharding import Mesh
from jax.sharding import PartitionSpec as P

REPLICA = ("replica_0", "replica_1", "replica_2")
REPLICA_SPATIAL = ("replica_0", "replica_1", "replica_2", "spatial")


def in_blocks(shard, dim, count):
    before, after = (shard.shape[:dim], shard.shape[dim + 1 :])
    return jnp.moveaxis(shard.reshape(*before, count, -1, *after), dim, 0)


def sent_and_summed(shard, axis, dim):
    count = lax.axis_size(axis)
    blocks = lax.all_to_all(in_blocks(shard, dim, count), axis, 0, 0, tiled=True)
    return jnp.sum(blocks, axis=0)


def copy_for_each(shard, axis):
    copies = jnp.broadcast_to(shard, (lax.axis_size(axis), *shard.shape))
    return lax.all_to_all(copies, axis, split_axis=0, concat_axis=0, tiled=True)


def over_copies(shard, axis):
    return copy_for_each(shard, axis).sum(axis=0)


def over_axes(shard, axes):
    far, near = axes
    nearer = over_copies(shard, near)
    return over_copies(nearer, far)


def in_one(arrays, axis):
    ends = [0]
    for a in arrays:
        ends.append(ends[-1] + a.size)
    running = over_axes(jnp.concatenate([a.ravel() for a in arrays]), axis)
    return tuple((running[b:e].reshape(a.shape) for a, b, e in zip(arrays, ends, ends[1:])))


def laid_out(blocks, dim):
    blocks = jnp.moveaxis(blocks, 0, dim)
    shape = blocks.shape
    return blocks.reshape(*shape[:dim], shape[dim] * shape[dim + 1], *shape[dim + 2 :])


def gathered_by_axis(shard, axes, dim):
    far, near = axes
    blocks = copy_for_each(copy_for_each(shard, far), near)
    return laid_out(blocks.swapaxes(0, 1).reshape(-1, *shard.shape), dim)


def shards(grads, master, velocity, layer_offsets, layer_sizes, lars_skip):
    n_rep = lax.axis_size(REPLICA)
    n_spa = lax.axis_size("spatial")
    shard = master.shape[0]
    position = lax.axis_index(REPLICA_SPATIAL) * shard + jnp.arange(shard, dtype=jnp.int32)
    inside = (position[None, :] >= layer_offsets[:, None]) & (
        position[None, :] < (layer_offsets + layer_sizes)[:, None]
    )
    onehot = inside.astype(jnp.float32)
    received = lax.all_to_all(
        grads[0, 0].reshape(n_rep, n_spa * shard), REPLICA, split_axis=0, concat_axis=0, tiled=True
    )
    first = jnp.sum(received.astype(jnp.float32), axis=0)
    summed = sent_and_summed(first.reshape(n_spa, shard), "spatial", 0)
    grad = summed.reshape(shard) / (n_rep * n_spa)
    gsq_local = jnp.dot(onehot, grad * grad, precision=lax.Precision.HIGHEST)
    wsq_local = jnp.dot(onehot, master * master, precision=lax.Precision.HIGHEST)
    wsq, gsq = in_one(
        (wsq_local, gsq_local), (("replica_0", "replica_1"), ("replica_2", "spatial"))
    )
    wnorm = jnp.sqrt(wsq)
    gnorm = jnp.sqrt(gsq)
    skipped = lars_skip.astype(jnp.float32)
    ratio = 0.02 * wnorm / (gnorm + 0.001 * wnorm + 1e-06)
    trust = skipped + (1.0 - skipped) * ratio
    decay = (1.0 - skipped) * 0.001
    trust_pos = jnp.dot(trust, onehot, precision=lax.Precision.HIGHEST)
    decay_pos = jnp.dot(decay, onehot, precision=lax.Precision.HIGHEST)
    new_velocity = 0.9 * velocity + 8.0 * trust_pos * (grad + decay_pos * master)
    new_master = master - new_velocity
    new_weights = gathered_by_axis(
        new_master.astype(jnp.bfloat16), (("replica_0", "replica_1"), ("replica_2", "spatial")), 0
    )
    return (new_weights, new_master, new_velocity)


def solution(mesh):
    finer = Mesh(
        mesh.devices.reshape(8, 4, 2, mesh.shape["spatial"]),
        ("replica_0", "replica_1", "replica_2", "spatial"),
    )
    in_specs = (P(REPLICA, "spatial", None), P(REPLICA_SPATIAL), P(REPLICA_SPATIAL), P(), P(), P())
    out_specs = (P(), P(REPLICA_SPATIAL), P(REPLICA_SPATIAL))
    return jax.shard_map(
        shards, mesh=finer, in_specs=in_specs, out_specs=out_specs, check_vma=False
    )
```

profile of v0, /device:TPU:1, one launch (start us, length us, event | category | flops | bytes accessed | tf_op | source)
XLA Modules:
  0.0 241.4 jit_solution(13452952206500173183)
XLA Ops:
  0.6 37.8 %reduce.4 = bf16[852992]{0:T(1024)(128)(2,1)} reduce(bf16[1,1,852992]{2,1,0:T(2,128)(2,1)} %param.6, bf16[]{:T(256)} %constant.46), dimensions={0,1}, to_apply=%param.6.reduce_sub_computation | reduce | bytes 3411970 | tf_op args[0]
  38.4 3.1 %all_to_all.34 = bf16[64,1,13328]{2,1,0:T(2,128)(2,1)S(1)} reshape(bf16[852992]{0:T(1024)(128)(2,1)} %reduce.4) | data formatting | bytes 3411968 | tf_op jit(solution)/shard_map/all_to_all | solution.py:66
  41.5 0.5 broadcast.59
  42.1 12.9 %reduce.9 = bf16[64,13328]{1,0:T(8,128)(2,1)} reduce(bf16[64,1,13328]{2,1,0:T(2,128)(2,1)S(1)} %all_to_all.34, bf16[]{:T(256)} %broadcast.59), dimensions={1}, to_apply=%all_to_all.34.reduce_sub_computation | reduce | bytes 3411970 | tf_op jit(solution)/shard_map/all_to_all | solution.py:66
  54.9 5.0 %reshape.42 = bf16[64,2,6664]{2,1,0:T(2,128)(2,1)} reshape(bf16[64,13328]{1,0:T(8,128)(2,1)} %reduce.9) | data formatting | bytes 3411968
  59.9 0.0 copy-start
  59.9 0.0 copy-start.2
  59.9 0.0 copy-start.4
  60.0 15.1 %all-to-all-start = ((bf16[64,2,6664]{2,1,0:T(2,128)(2,1)}), bf16[64,2,6664]{2,1,0:T(2,128)(2,1)}, u32[]{:S(2)}, u32[]{:S(2)}) async-start(bf16[64,2,6664]{2,1,0:T(2,128)(2,1)} %reshape.42), calls=%async_computation | async-start | bytes 3473408 | tf_op jit(solution)/shard_map/all_to_all | solution.py:66
  75.1 0.0 copy-done
  75.1 0.0 copy-done.2
  75.2 0.0 copy-done.4
  75.2 42.2 %all-to-all-done = bf16[64,2,6664]{2,1,0:T(2,128)(2,1)} async-done(((bf16[64,2,6664]{2,1,0:T(2,128)(2,1)}), bf16[64,2,6664]{2,1,0:T(2,128)(2,1)}, u32[]{:S(2)}, u32[]{:S(2)}) %all-to-all-start) | async-done | bytes 1706016 | tf_op jit(solution)/shard_map/all_to_all | solution.py:66
  117.4 9.9 %reshape.43 = bf16[64,1,13328]{2,1,0:T(2,128)(2,1)S(1)} reshape(bf16[64,2,6664]{2,1,0:T(2,128)(2,1)} %all-to-all-done) | data formatting | bytes 3411968
  127.3 0.0 copy-start.3
  127.4 0.0 copy-start.1
  127.4 3.5 %convert_reduce_fusion = f32[13328]{0:T(1024)S(1)} fusion(bf16[64,1,13328]{2,1,0:T(2,128)(2,1)S(1)} %reshape.43), kind=kLoop, calls=%fused_computation | loop fusion | flops 1692656 | bytes 1759296 | tf_op jit(solution)/shard_map/reduce_sum | solution.py:69
  130.9 0.8 reshape_reshape.6
  131.7 6.8 %all-to-all-start.1 = ((f32[8,1,1666]{2,1,0:T(1,128)}), f32[8,1,1666]{2,1,0:T(1,128)S(1)}, u32[]{:S(2)}, u32[]{:S(2)}) async-start(f32[8,1,1666]{2,1,0:T(1,128)} %reshape_reshape.6), calls=%async_computation.1 | async-start | bytes 114688 | tf_op jit(solution)/shard_map/all_to_all | solution.py:18
  138.5 0.2 convolution_bitcast_fusion.1
  138.7 7.0 %all-to-all-done.1 = f32[8,1,1666]{2,1,0:T(1,128)S(1)} async-done(((f32[8,1,1666]{2,1,0:T(1,128)}), f32[8,1,1666]{2,1,0:T(1,128)S(1)}, u32[]{:S(2)}, u32[]{:S(2)}) %all-to-all-start.1) | async-done | bytes 53344 | tf_op jit(solution)/shard_map/all_to_all | solution.py:18
  145.7 0.2 convolution_bitcast_fusion
  145.9 0.1 pad_maximum_fusion
  146.0 12.5 %all_to_all.41 = f32[16,1,12]{2,1,0:T(1,128)S(1)} all-to-all(f32[16,1,12]{2,1,0:T(1,128)S(1)} %broadcast_in_dim.16), channel_id=1, replica_groups=mesh['replica_0'=8,'replica_1'=4,'replica_2'=2,'spatial'=8] {'replica_2'..., dimensions={0} | all-to-all | bytes 1536 | tf_op jit(solution)/shard_map/all_to_all | solution.py:24
  158.6 0.6 broadcast_in_dim.17
  159.2 4.4 %all-to-all-start.3 = ((f32[32,1,12]{2,1,0:T(1,128)}), f32[32,1,12]{2,1,0:T(1,128)S(1)}, u32[]{:S(2)}, u32[]{:S(2)}) async-start(f32[32,1,12]{2,1,0:T(1,128)} %broadcast_in_dim.17), calls=%async_computation.3 | async-start | bytes 32768 | tf_op jit(solution)/shard_map/all_to_all | solution.py:24
  163.6 0.0 copy-done.3
  163.6 0.2 convolution_reduce_fusion
  163.9 8.3 %all-to-all-done.3 = f32[32,1,12]{2,1,0:T(1,128)S(1)} async-done(((f32[32,1,12]{2,1,0:T(1,128)}), f32[32,1,12]{2,1,0:T(1,128)S(1)}, u32[]{:S(2)}, u32[]{:S(2)}) %all-to-all-start.3) | async-done | bytes 1568 | tf_op jit(solution)/shard_map/all_to_all | solution.py:24
  172.2 0.1 reduce_sum.39
  172.2 0.3 convolution_reduce_fusion.1
  172.5 0.0 copy-done.1
  172.5 0.6 fusion.23
  173.1 0.1 broadcast_in_dim.18
  173.2 1.2 reduce.10
  174.5 0.2 reshape.44
  174.6 12.2 %all_to_all.42 = bf16[32,2,833]{2,1,0:T(2,128)(2,1)S(1)} all-to-all(bf16[32,2,833]{2,1,0:T(2,128)(2,1)S(1)} %reshape.44), channel_id=1, replica_groups=mesh['replica_0'=8,'replica_1'=4,'replica_2'=2,'spatial'=8] {'replica_0'..., dimensions={0} | all-to-all | bytes 213248 | tf_op jit(solution)/shard_map/all_to_all | solution.py:24
  186.9 0.2 reshape.45
  187.1 0.2 broadcast_in_dim.19
  187.3 48.8 %all_to_all.43 = bf16[16,32,1666]{2,1,0:T(8,128)(2,1)S(1)} all-to-all(bf16[16,32,1666]{2,1,0:T(8,128)(2,1)S(1)} %broadcast_in_dim.19), channel_id=1, replica_groups=mesh['replica_0'=8,'replica_1'=4,'replica_2'=2,'spatial'=8] {'replica_2'..., dimensions={0} | all-to-all | bytes 3411968 | tf_op jit(solution)/shard_map/all_to_all | solution.py:24
  236.1 1.0 copy.23
  237.1 4.2 %reshape_reshape.7 = bf16[852992]{0:T(1024)(128)(2,1)} reshape(bf16[32,16,1666]{2,1,0:T(8,128)(2,1)S(1)} %copy.23) | data formatting | bytes 3411968 | tf_op jit(solution)/shard_map/reshape;reshape | solution.py:48
  (10 shorter events, 0.1 us)
Async XLA Ops:
  59.9 15.2 %copy-start = (f32[1666]{0:T(1024)S(1)}, f32[1666]{0:T(1024)}, u32[]{:S(2)}) copy-start(f32[1666]{0:T(1024)} %param.7) | copy-start | bytes 19996
  59.9 15.2 %copy-start.2 = (s32[6]{0:T(128)S(1)}, s32[6]{0:T(128)}, u32[]{:S(2)}) copy-start(s32[6]{0:T(128)} %param.10) | copy-start | bytes 76
  59.9 15.2 %copy-start.4 = (s32[6]{0:T(128)S(1)}, s32[6]{0:T(128)}, u32[]{:S(2)}) copy-start(s32[6]{0:T(128)} %param.9) | copy-start | bytes 76
  60.0 57.5 %all-to-all-start = ((bf16[64,2,6664]{2,1,0:T(2,128)(2,1)}), bf16[64,2,6664]{2,1,0:T(2,128)(2,1)}, u32[]{:S(2)}, u32[]{:S(2)}) async-start(bf16[64,2,6664]{2,1,0:T(2,128)(2,1)} %reshape.42), calls=%async_computation | async-start | bytes 3473408 | tf_op jit(solution)/shard_map/all_to_all | solution.py:66
  127.3 36.3 %copy-start.3 = (s32[6]{0:T(128)S(1)}, s32[6]{0:T(128)}, u32[]{:S(2)}) copy-start(s32[6]{0:T(128)} %param.11) | copy-start | bytes 76
  127.4 45.1 %copy-start.1 = (f32[1666]{0:T(1024)S(1)}, f32[1666]{0:T(1024)}, u32[]{:S(2)}) copy-start(f32[1666]{0:T(1024)} %param.8) | copy-start | bytes 19996
  131.7 14.0 %all-to-all-start.1 = ((f32[8,1,1666]{2,1,0:T(1,128)}), f32[8,1,1666]{2,1,0:T(1,128)S(1)}, u32[]{:S(2)}, u32[]{:S(2)}) async-start(f32[8,1,1666]{2,1,0:T(1,128)} %reshape_reshape.6), calls=%async_computation.1 | async-start | bytes 114688 | tf_op jit(solution)/shard_map/all_to_all | solution.py:18
  159.2 13.0 %all-to-all-start.3 = ((f32[32,1,12]{2,1,0:T(1,128)}), f32[32,1,12]{2,1,0:T(1,128)S(1)}, u32[]{:S(2)}, u32[]{:S(2)}) async-start(f32[32,1,12]{2,1,0:T(1,128)} %broadcast_in_dim.17), calls=%async_computation.3 | async-start | bytes 32768 | tf_op jit(solution)/shard_map/all_to_all | solution.py:24
where the time goes:
time: 243 us; the launch traced here: 241 us
  blocking collectives  73.6 us (30%)
  waiting for transfers between devices  57.5 us (24%)
  other arithmetic  56.3 us (23%)
  starting transfers between devices  26.4 us (11%)
  local copies, waits for them, and re-layouts  25.9 us (11%)
    all_to_all x3, blocking collectives, copy_for_each(): return lax.all_to_all(copies, axis, split_axis=0, concat_axis=0, tiled=True)  73.6 us
    all_to_all x1, waiting for transfers between devices, shards(): lax.all_to_all(grads[0, 0].reshape(n_rep, n_spa * shard), REPLICA, split_...  42.2 us
    unnamed x1, other arithmetic  37.8 us
    unnamed x15, local copies, waits for them, and re-layouts  15.3 us
    all_to_all x1, starting transfers between devices, shards(): lax.all_to_all(grads[0, 0].reshape(n_rep, n_spa * shard), REPLICA, split_...  15.1 us
    all_to_all x1, other arithmetic, shards(): lax.all_to_all(grads[0, 0].reshape(n_rep, n_spa * shard), REPLICA, split_...  12.9 us
    all_to_all x1, waiting for transfers between devices, copy_for_each(): return lax.all_to_all(copies, axis, split_axis=0, concat_axis=0, tiled=True)  8.28 us
    all_to_all x1, waiting for transfers between devices, sent_and_summed(): lax.all_to_all(in_blocks(shard, dim, count), axis, 0, 0, tiled=True)  6.95 us
  transfers between devices with their start and end apart: 3, of which 3 were waited for; matrix products, arithmetic and copies ran while one was open for 0% of the time, Pallas kernels for 0%

commit v1 on v0

v1 whole, which is shorter than its diff:
```python
import jax
import jax.numpy as jnp
from jax import lax
from jax.experimental import pallas as pl
from jax.experimental.pallas import tpu as pltpu
from jax.sharding import Mesh
from jax.sharding import PartitionSpec as P

AXES = ("z", "x", "c", "y")
NZ, NX, NC, NY = 8, 4, 2, 8
NQ = NX * NC
LANES = 128
SHARD = 1666
BLOCK = NY * SHARD
ROWS = 6664
Z_ROWS = ROWS // NZ
Q_ROWS = 104
Y_ROWS = 13
SLOT = 16
TALL = 112
LAYERS = 6
f32 = jnp.float32
bf16 = jnp.bfloat16
VMEM = pl.BlockSpec(memory_space=pltpu.VMEM)
SMEM = pl.BlockSpec(memory_space=pltpu.SMEM)
PARAMS = pltpu.CompilerParams(vmem_limit_bytes=40 * 1024 * 1024)


def call(kernel, out_shape, ins, scratch=()):
    many = isinstance(out_shape, tuple)
    return pl.pallas_call(
        kernel,
        out_shape=out_shape,
        in_specs=list(ins),
        out_specs=(VMEM,) * len(out_shape) if many else VMEM,
        scratch_shapes=list(scratch),
        compiler_params=PARAMS,
    )


def row_of(z, q):
    return z * Z_ROWS + q * Q_ROWS


def pack_kernel(x_ref, o_ref):
    for z in range(NZ):
        for q in range(NQ):
            base = row_of(z, q)
            o_ref[q, z, :Q_ROWS, :] = x_ref[base : base + Q_ROWS, :].astype(bf16)
            last = x_ref[base + Q_ROWS : base + Q_ROWS + 1, :]
            o_ref[q, z, Q_ROWS:, :] = jnp.broadcast_to(last, (TALL - Q_ROWS, LANES)).astype(bf16)


def positions():
    z = lax.axis_index("z")
    q = lax.axis_index("x") * NC + lax.axis_index("c")
    row = lax.broadcasted_iota(jnp.int32, (TALL, LANES), 0)
    lane = lax.broadcasted_iota(jnp.int32, (TALL, LANES), 1)
    local = row * LANES + lane - 2 * NY * q
    valid = (local >= 0) & (local < BLOCK)
    return local + (z * NQ + q) * BLOCK, valid


def in_layer(tab_ref, l, pos):
    start = tab_ref[l]
    return (pos >= start) & (pos < start + tab_ref[LAYERS + l])


def norms_kernel(tab_ref, r_ref, n_ref, g_ref, m_ref, v_ref):
    g = r_ref[0, :TALL, :]
    for y in range(1, NY):
        g = g + r_ref[y, :TALL, :]
    g = g * (1.0 / 512.0)
    g_ref[...] = g
    m_ref[...] = jnp.zeros_like(m_ref)
    v_ref[...] = jnp.zeros_like(v_ref)
    for y in range(NY):
        rows = slice(y * Y_ROWS, y * Y_ROWS + Y_ROWS + 1)
        m_ref[rows, :] += r_ref[y, TALL : TALL + Y_ROWS + 1, :]
        v_ref[rows, :] += r_ref[y, TALL + SLOT : TALL + SLOT + Y_ROWS + 1, :]
    m = m_ref[...]
    pos, valid = positions()
    gg = jnp.where(valid, g * g, 0.0)
    mm = jnp.where(valid, m * m, 0.0)
    lane = lax.broadcasted_iota(jnp.int32, (1, LANES), 1)
    total = jnp.zeros((1, LANES), f32)
    for l in range(LAYERS):
        mask = in_layer(tab_ref, l, pos)
        for at, square in ((l, mm), (8 + l, gg)):
            rows = jnp.sum(jnp.where(mask, square, 0.0), axis=0, keepdims=True)
            total = total + jnp.where(lane == at, jnp.sum(rows, axis=1, keepdims=True), 0.0)
    n_ref[...] = jnp.broadcast_to(total[None], n_ref.shape)


def update_kernel(tab_ref, n_ref, g_ref, m_ref, v_ref, w_ref, om_ref, ov_ref, nm, nv, turn):
    norms = jnp.sum(n_ref[...], axis=0)
    lane1 = lax.broadcasted_iota(jnp.int32, (1, LANES), 1)
    pos, valid = positions()
    trust_pos = jnp.zeros((TALL, LANES), f32)
    decay_pos = jnp.zeros((TALL, LANES), f32)
    for l in range(LAYERS):
        wsq = jnp.sum(jnp.where(lane1 == l, norms, 0.0), axis=1, keepdims=True)
        gsq = jnp.sum(jnp.where(lane1 == 8 + l, norms, 0.0), axis=1, keepdims=True)
        wnorm, gnorm = jnp.sqrt(wsq), jnp.sqrt(gsq)
        skipped = tab_ref[2 * LAYERS + l].astype(f32)
        ratio = 0.02 * wnorm / (gnorm + 0.001 * wnorm + 1e-06)
        trust = skipped + (1.0 - skipped) * ratio
        mask = in_layer(tab_ref, l, pos)
        trust_pos = jnp.where(mask, trust, trust_pos)
        decay_pos = jnp.where(mask, (1.0 - skipped) * 0.001, decay_pos)
    m = m_ref[...]
    new_v = 0.9 * v_ref[...] + 8.0 * trust_pos * (g_ref[...] + decay_pos * m)
    new_m = m - new_v
    nm[...] = new_m
    nv[...] = new_v
    w = jnp.where(valid, new_m, 0.0).astype(bf16)
    for z in range(NZ):
        w_ref[z] = w
    q = lax.axis_index("x") * NC + lax.axis_index("c")
    y = lax.axis_index("y")
    shift = 2 * (NY * q + y)
    lane = lax.broadcasted_iota(jnp.int32, (SLOT, LANES), 1)
    for src, out in ((nm, om_ref), (nv, ov_ref)):
        own = src[:SLOT, :]
        for k in range(1, NY):
            own = jnp.where(y == k, src[k * Y_ROWS : k * Y_ROWS + SLOT, :], own)
        turned = pltpu.roll(own, lax.rem(LANES - shift, LANES), 1)
        turn[:SLOT, :] = turned
        turn[SLOT:, :] = jnp.zeros((8, LANES), f32)
        out[...] = jnp.where(lane < LANES - shift, turned, turn[1 : SLOT + 1, :])


def lay_out_kernel(a_ref, b_ref, o_ref, rows):
    c = lax.axis_index("c")
    for z in range(NZ):
        carry = None
        for q in range(NQ):
            x, cc = q // NC, q % NC
            mine, other = a_ref[x, z], b_ref[x, z]
            block = jnp.where(c == cc, mine.astype(f32), other.astype(f32))
            base = row_of(z, q)
            rows[base : base + Q_ROWS, :] = block[:Q_ROWS, :]
            if carry is not None:
                rows[base : base + 1, :] += carry
            carry = block[Q_ROWS : Q_ROWS + 1, :]
        rows[row_of(z, NQ) : row_of(z, NQ) + 1, :] = carry

    def narrow(k, _):
        at = pl.ds(pl.multiple_of(k * 136, 8), 136)
        o_ref[at, :] = rows[at, :].astype(bf16)
        return _

    lax.fori_loop(0, ROWS // 136, narrow, 0)


def sent(x, axes):
    return lax.all_to_all(x, axes, 0, 0, tiled=True)


def shards(grads, master, velocity, layer_offsets, layer_sizes, lars_skip):
    q = lax.axis_index("x") * NC + lax.axis_index("c")
    y = lax.axis_index("y")
    shift = 2 * (NY * q + y)
    tab = jnp.concatenate([layer_offsets, layer_sizes, lars_skip])

    def placed(a):
        flat = lax.dynamic_update_slice(jnp.zeros((SLOT * LANES,), f32), a, (shift,))
        return flat.reshape(SLOT, LANES)

    wide = grads.astype(f32).reshape(ROWS, LANES)
    packed = call(pack_kernel, jax.ShapeDtypeStruct((NQ, NZ, TALL, LANES), bf16), [VMEM])(wide)
    received = sent(packed, ("x", "c"))
    over_q = jnp.sum(received.astype(f32), axis=0)
    over_z = jnp.sum(sent(over_q, "z"), axis=0)
    mine = jnp.concatenate([over_z, placed(master), placed(velocity)])
    shared = sent(jnp.broadcast_to(mine, (NY, *mine.shape)), "y")
    tall = jax.ShapeDtypeStruct((TALL, LANES), f32)
    norms, g, m, v = call(
        norms_kernel,
        (jax.ShapeDtypeStruct((NZ * NQ, 1, LANES), f32), tall, tall, tall),
        [SMEM, VMEM],
    )(tab, shared)
    norms = sent(norms, ("z", "x", "c"))
    slot = jax.ShapeDtypeStruct((SLOT, LANES), f32)
    w, new_master, new_velocity = call(
        update_kernel,
        (jax.ShapeDtypeStruct((NZ, TALL, LANES), bf16), slot, slot),
        [SMEM, VMEM, VMEM, VMEM, VMEM],
        [
            pltpu.VMEM((TALL, LANES), f32),
            pltpu.VMEM((TALL, LANES), f32),
            pltpu.VMEM((SLOT + 8, LANES), f32),
        ],
    )(tab, norms, g, m, v)
    w = sent(w, "z")
    w = lax.all_gather(w.reshape(NZ * TALL, LANES), "x").reshape(NX, NZ, TALL, LANES)
    other = lax.ppermute(w, "c", [(0, 1), (1, 0)])
    weights = call(
        lay_out_kernel,
        jax.ShapeDtypeStruct((ROWS, LANES), bf16),
        [VMEM, VMEM],
        [pltpu.VMEM((ROWS, LANES), f32)],
    )(w, other)
    return (
        weights.reshape(ROWS * LANES),
        new_master.reshape(SLOT * LANES)[:SHARD],
        new_velocity.reshape(SLOT * LANES)[:SHARD],
    )


def solution(mesh):
    finer = Mesh(mesh.devices.reshape(NZ, NX, NC, NY), AXES)
    owned = P(AXES)
    in_specs = (P(("z", "x", "c"), "y", None), owned, owned, P(), P(), P())
    return jax.shard_map(
        shards, mesh=finer, in_specs=in_specs, out_specs=(P(), owned, owned), check_vma=False
    )
```

time: 243 us -> 141 us (0.58)
  other arithmetic: 56.3 us -> 7.3 us
  local copies, waits for them, and re-layouts: 25.9 us -> 1.46 us
  waiting for transfers between devices: 57.5 us -> 33.8 us
  starting transfers between devices: 26.4 us -> 19.5 us
  Pallas kernels: 0 us -> 4.36 us
    unnamed x1 -> x0, other arithmetic: 37.8 us -> none
    all_to_all x3 -> x2, waiting for transfers between devices: 57.5 us -> 31.7 us  [sent(): return lax.all_to_all(x, axes, 0, 0, tiled=True)]
    unnamed x15 -> x10, local copies, waits for them, and re-layouts: 15.3 us -> 0.02 us
    all_to_all x3 -> x2, starting transfers between devices: 26.4 us -> 13.3 us  [sent(): return lax.all_to_all(x, axes, 0, 0, tiled=True)]
    all_to_all x1 -> x0, other arithmetic: 12.9 us -> none  [shards(): lax.all_to_all(grads[0, 0].reshape(n_rep, n_spa * shard), REPLICA, split_...]
    all_to_all x3, blocking collectives: 73.6 us -> 61.3 us  [sent(): return lax.all_to_all(x, axes, 0, 0, tiled=True)]
    all_gather x0 -> x1, blocking collectives: none -> 12.1 us  [shards(): lax.all_gather(w.reshape(NZ * TALL, LANES), 'x')]
    ppermute x0 -> x1, starting transfers between devices: none -> 6.24 us  [shards(): other = lax.ppermute(w, 'c', [(0, 1), (1, 0)])]
where the time goes in v1:
time: 141 us
  blocking collectives  73.4 us (52%)
  waiting for transfers between devices  33.8 us (24%)
  starting transfers between devices  19.5 us (14%)
  other arithmetic  7.3 us (5%)
  Pallas kernels  4.36 us (3%)
  local copies, waits for them, and re-layouts  1.46 us (1%)
    all_to_all x3, blocking collectives, sent(): return lax.all_to_all(x, axes, 0, 0, tiled=True)  61.3 us
    all_to_all x2, waiting for transfers between devices, sent(): return lax.all_to_all(x, axes, 0, 0, tiled=True)  31.7 us
    all_to_all x2, starting transfers between devices, sent(): return lax.all_to_all(x, axes, 0, 0, tiled=True)  13.3 us
    all_gather x1, blocking collectives, shards(): lax.all_gather(w.reshape(NZ * TALL, LANES), 'x')  12.1 us
    ppermute x1, starting transfers between devices, shards(): other = lax.ppermute(w, 'c', [(0, 1), (1, 0)])  6.24 us
    reshape x1, other arithmetic, shards(): wide = grads.astype(f32).reshape(ROWS, LANES)  6.18 us
  transfers between devices with their start and end apart: 3, of which 3 were waited for; matrix products, arithmetic and copies ran while one was open for 0% of the time, Pallas kernels for 0%

profile of v1, /device:TPU:1, one launch (start us, length us, event | category | flops | bytes accessed | tf_op | source)
XLA Modules:
  0.0 140.5 jit_solution(9144718523051514315)
XLA Ops:
  0.6 6.2 %reshape.37 = f32[1,1,852992]{2,1,0:T(1,128)S(1)} convert(bf16[1,1,852992]{2,1,0:T(2,128)(2,1)} %param.6) | non-fusion elementwise | flops 852992 | bytes 5117952 | tf_op jit(solution)/shard_map/reshape | solution.py:170
  6.8 0.2 shard_map.85
  7.0 32.6 %all_to_all.25 = bf16[8,8,112,128]{3,2,1,0:T(8,128)(2,1)S(1)} all-to-all(bf16[8,8,112,128]{3,2,1,0:T(8,128)(2,1)S(1)} %shard_map.85), channel_id=1, replica_groups=mesh['z'=8,'x'=4,'c'=2,'y'=8] {'x','c'}, dimensions={0} | all-to-all | bytes 3670016 | tf_op jit(solution)/shard_map/all_to_all | solution.py:157
  39.6 0.0 copy-start
  39.6 0.0 copy-start.1
  39.6 1.0 convert_reduce_fusion
  40.7 0.0 copy-start.2
  40.7 0.0 copy-start.3
  40.7 0.0 copy-start.4
  40.7 6.5 %all-to-all-start.1 = ((f32[8,112,128]{2,1,0:T(8,128)}), f32[8,112,128]{2,1,0:T(8,128)S(1)}, u32[]{:S(2)}, u32[]{:S(2)}) async-start(f32[8,112,128]{2,1,0:T(8,128)} %convert_reduce_fusion), calls=%async_computation.1 | async-start | bytes 917504 | tf_op jit(solution)/shard_map/all_to_all | solution.py:157
  47.2 0.0 copy-done
  47.2 0.3 dynamic_update_slice.6
  47.5 0.0 copy-done.1
  47.5 0.3 dynamic_update_slice.7
  47.8 14.6 %all-to-all-done.1 = f32[8,112,128]{2,1,0:T(8,128)S(1)} async-done(((f32[8,112,128]{2,1,0:T(8,128)}), f32[8,112,128]{2,1,0:T(8,128)S(1)}, u32[]{:S(2)}, u32[]{:S(2)}) %all-to-all-start.1) | async-done | bytes 458784 | tf_op jit(solution)/shard_map/all_to_all | solution.py:157
  62.4 0.9 broadcast_in_dim.3
  63.3 6.8 %all-to-all-start.2 = ((f32[8,144,128]{2,1,0:T(8,128)}), f32[8,144,128]{2,1,0:T(8,128)S(1)}, u32[]{:S(2)}, u32[]{:S(2)}) async-start(f32[8,144,128]{2,1,0:T(8,128)} %broadcast_in_dim.3), calls=%async_computation.2 | async-start | bytes 1179648 | tf_op jit(solution)/shard_map/all_to_all | solution.py:157
  70.1 0.0 copy-done.2
  70.1 0.0 copy-done.3
  70.1 0.0 copy-done.4
  70.1 0.1 pad_add_fusion.tab_ref
  70.2 17.1 %all-to-all-done.2.r_ref = f32[8,144,128]{2,1,0:T(8,128)S(1)} async-done(((f32[8,144,128]{2,1,0:T(8,128)}), f32[8,144,128]{2,1,0:T(8,128)S(1)}, u32[]{:S(2)}, u32[]{:S(2)}) %all-to-all-start.2) | async-done | bytes 589856 | tf_op jit(solution)/shard_map/all_to_all | solution.py:157
  87.2 0.8 shard_map.86
  88.1 16.1 %all_to_all.26.n_ref = f32[64,1,128]{2,1,0:T(1,128)S(1)} all-to-all(f32[64,1,128]{2,1,0:T(1,128)S(1)} %get-tuple-element.10), channel_id=1, replica_groups=mesh['z'=8,'x'=4,'c'=2,'y'=8] {'z','x','c'}, dimensions={0} | all-to-all | bytes 65536 | tf_op jit(solution)/shard_map/all_to_all | solution.py:157
  104.2 1.5 %shard_map.87 = (bf16[8,112,128]{2,1,0:T(8,128)(2,1)S(1)}, f32[16,128]{1,0:T(8,128)}, f32[16,128]{1,0:T(8,128)}) custom-call(s32[18]{0:T(128)S(1)} %pad_add_fusion.tab_ref, f32[64,1,128]{2,1,0:T(1,128)S(1)} %all_to_all.26.n_ref, f32[112,128]{1,0:T(8,128)S(1)} %get-tuple-element.11.g_ref, f32[112,128]{1,0:T(8,128)S(1)} %get-tuple-element.12.m_ref, ...), custom_call_target="tpu_custom_call" | custom-call | tf_op jit(solution)/shard_map/pallas_call | solution.py:185
  105.7 12.5 %all_to_all.27 = bf16[8,112,128]{2,1,0:T(8,128)(2,1)S(1)} all-to-all(bf16[8,112,128]{2,1,0:T(8,128)(2,1)S(1)} %get-tuple-element.14), channel_id=1, replica_groups=mesh['z'=8,'x'=4,'c'=2,'y'=8] {'z'}, dimensions={0} | all-to-all | bytes 458752 | tf_op jit(solution)/shard_map/all_to_all | solution.py:157
  118.2 12.1 %all_gather.3 = bf16[4,896,128]{2,1,0:T(8,128)(2,1)S(1)} all-gather(bf16[1,896,128]{2,1,0:T(8,128)(2,1)S(1)} %bitcast.14), channel_id=1, replica_groups=mesh['z'=8,'x'=4,'c'=2,'y'=8] {'x'}, dimensions={0}, use_global_device_ids=true | all-gather | bytes 1146880 | tf_op jit(solution)/shard_map/all_gather | solution.py:196
  130.3 6.2 %collective-permute-start = (bf16[4,8,112,128]{3,2,1,0:T(8,128)(2,1)S(1)}, bf16[4,8,112,128]{3,2,1,0:T(8,128)(2,1)S(1)}, u32[]{:S(2)}, u32[]{:S(2)}) collective-permute-start(bf16[4,8,112,128]{3,2,1,0:T(8,128)(2,1)S(1)} %bitcast.11), channel_id=1, source_target_pairs={{0,8},{8,0},{1,9},{9,1},{2,10},{10,2},{3,11},{11,3},{4,12},{12,4},... | collective-permute-start | bytes 2752520 | tf_op jit(solution)/shard_map/ppermute | solution.py:197
  136.5 2.1 %collective-permute-done.b_ref = bf16[4,8,112,128]{3,2,1,0:T(8,128)(2,1)S(1)} collective-permute-done((bf16[4,8,112,128]{3,2,1,0:T(8,128)(2,1)S(1)}, bf16[4,8,112,128]{3,2,1,0:T(8,128)(2,1)S(1)}, u32[]{:S(2)}, u32[]{:S(2)}) %collective-permute-start) | collective-permute-done | bytes 917536 | tf_op jit(solution)/shard_map/ppermute | solution.py:197
  138.6 1.9 %shard_map.88 = bf16[6664,128]{1,0:T(8,128)(2,1)} custom-call(bf16[4,8,112,128]{3,2,1,0:T(8,128)(2,1)S(1)} %bitcast.12, bf16[4,8,112,128]{3,2,1,0:T(8,128)(2,1)S(1)} %collective-permute-done.b_ref), custom_call_target="tpu_custom_call" | custom-call | tf_op jit(solution)/shard_map/pallas_call | solution.py:198
  (4 shorter events, 0.0 us)
Async XLA Ops:
  39.6 7.5 %copy-start = (f32[1666]{0:T(1024)S(1)}, f32[1666]{0:T(1024)}, u32[]{:S(2)}) copy-start(f32[1666]{0:T(1024)} %param.7) | copy-start | bytes 19996
  39.6 7.8 %copy-start.1 = (f32[1666]{0:T(1024)S(1)}, f32[1666]{0:T(1024)}, u32[]{:S(2)}) copy-start(f32[1666]{0:T(1024)} %param.8) | copy-start | bytes 19996
  40.7 29.4 %copy-start.2 = (s32[6]{0:T(128)S(1)}, s32[6]{0:T(128)}, u32[]{:S(2)}) copy-start(s32[6]{0:T(128)} %param.11) | copy-start | bytes 76
  40.7 29.4 %copy-start.3 = (s32[6]{0:T(128)S(1)}, s32[6]{0:T(128)}, u32[]{:S(2)}) copy-start(s32[6]{0:T(128)} %param.10) | copy-start | bytes 76
  40.7 29.4 %copy-start.4 = (s32[6]{0:T(128)S(1)}, s32[6]{0:T(128)}, u32[]{:S(2)}) copy-start(s32[6]{0:T(128)} %param.9) | copy-start | bytes 76
  40.7 21.7 %all-to-all-start.1 = ((f32[8,112,128]{2,1,0:T(8,128)}), f32[8,112,128]{2,1,0:T(8,128)S(1)}, u32[]{:S(2)}, u32[]{:S(2)}) async-start(f32[8,112,128]{2,1,0:T(8,128)} %convert_reduce_fusion), calls=%async_computation.1 | async-start | bytes 917504 | tf_op jit(solution)/shard_map/all_to_all | solution.py:157
  63.3 24.0 %all-to-all-start.2 = ((f32[8,144,128]{2,1,0:T(8,128)}), f32[8,144,128]{2,1,0:T(8,128)S(1)}, u32[]{:S(2)}, u32[]{:S(2)}) async-start(f32[8,144,128]{2,1,0:T(8,128)} %broadcast_in_dim.3), calls=%async_computation.2 | async-start | bytes 1179648 | tf_op jit(solution)/shard_map/all_to_all | solution.py:157
  130.3 8.3 %collective-permute-start = (bf16[4,8,112,128]{3,2,1,0:T(8,128)(2,1)S(1)}, bf16[4,8,112,128]{3,2,1,0:T(8,128)(2,1)S(1)}, u32[]{:S(2)}, u32[]{:S(2)}) collective-permute-start(bf16[4,8,112,128]{3,2,1,0:T(8,128)(2,1)S(1)} %bitcast.11), channel_id=1, source_target_pairs={{0,8},{8,0},{1,9},{9,1},{2,10},{10,2},{3,11},{11,3},{4,12},{12,4},... | collective-permute-start | bytes 2752520 | tf_op jit(solution)/shard_map/ppermute | solution.py:197

commit v2 on v1

v2 whole, which is shorter than its diff:
```python
import jax
import jax.numpy as jnp
from jax import lax
from jax.experimental import pallas as pl
from jax.experimental.pallas import tpu as pltpu
from jax.sharding import Mesh
from jax.sharding import PartitionSpec as P

AXES = ("z", "x", "c", "y")
NZ, NX, NC, NY = 8, 4, 2, 8
NQ = NX * NC
LANES = 128
SHARD = 1666
ROWS = 6664
Z_ROWS = ROWS // NZ
Q_ROWS = 104
Y_ROWS = 13
SLOT = 16
NORM_ROW = 14
TALL = 105
BLOCK_ROWS = NZ * TALL
LAYERS = 6
f32 = jnp.float32
bf16 = jnp.bfloat16
VMEM = pl.BlockSpec(memory_space=pltpu.VMEM)
SMEM = pl.BlockSpec(memory_space=pltpu.SMEM)
PARAMS = pltpu.CompilerParams(vmem_limit_bytes=40 * 1024 * 1024)


def shape(*dims, dtype=f32):
    return jax.ShapeDtypeStruct(dims, dtype)


def call(kernel, out_shape, ins, scratch=()):
    many = isinstance(out_shape, tuple)
    return pl.pallas_call(
        kernel,
        out_shape=out_shape,
        in_specs=list(ins),
        out_specs=(VMEM,) * len(out_shape) if many else VMEM,
        scratch_shapes=[pltpu.VMEM(s, f32) for s in scratch],
        compiler_params=PARAMS,
    )


def row_of(z, q):
    return z * Z_ROWS + q * Q_ROWS


def q_index():
    return lax.axis_index("x") * NC + lax.axis_index("c")


def pack_kernel(x_ref, o_ref, rows):
    for q in range(NQ):
        for z in range(NZ):
            base = row_of(z, q)
            rows[z * TALL : (z + 1) * TALL, :] = x_ref[base : base + TALL, :]
        o_ref[q] = rows[...].astype(bf16)


def spread_kernel(r_ref, o_ref, rows):
    total = r_ref[0].astype(f32)
    for q in range(1, NQ):
        total = total + r_ref[q].astype(f32)
    rows[...] = total
    for z in range(NZ):
        for y in range(NY):
            base = z * TALL + y * Y_ROWS
            o_ref[z * NY + y, :NORM_ROW, :] = rows[base : base + NORM_ROW, :]
            o_ref[z * NY + y, NORM_ROW:, :] = jnp.zeros((SLOT - NORM_ROW, LANES), f32)


def slot_positions():
    q, y = q_index(), lax.axis_index("y")
    owner = (lax.axis_index("z") * NQ + q) * NY + y
    row = lax.broadcasted_iota(jnp.int32, (SLOT, LANES), 0)
    lane = lax.broadcasted_iota(jnp.int32, (SLOT, LANES), 1)
    local = row * LANES + lane - 2 * (NY * q + y)
    return local + owner * SHARD, (local >= 0) & (local < SHARD)


def in_layer(tab_ref, l, pos):
    start = tab_ref[l]
    return (pos >= start) & (pos < start + tab_ref[LAYERS + l])


def skipped(tab_ref, l):
    return tab_ref[2 * LAYERS + l].astype(f32)


def owner_kernel(tab_ref, r_ref, m_ref, v_ref, o_ref, h_ref):
    g = r_ref[0]
    for k in range(1, NZ * NY):
        g = g + r_ref[k]
    pos, valid = slot_positions()
    g = jnp.where(valid, g * (1.0 / 512.0), 0.0)
    m = m_ref[...]
    lane = lax.broadcasted_iota(jnp.int32, (1, LANES), 1)
    total = jnp.zeros((1, LANES), f32)
    decay = jnp.zeros((SLOT, LANES), f32)
    for l in range(LAYERS):
        mask = in_layer(tab_ref, l, pos)
        decay = jnp.where(mask, (1.0 - skipped(tab_ref, l)) * 0.001, decay)
        for at, square in ((l, m * m), (8 + l, g * g)):
            rows = jnp.sum(jnp.where(mask, square, 0.0), axis=0, keepdims=True)
            total = total + jnp.where(lane == at, jnp.sum(rows, axis=1, keepdims=True), 0.0)
    h = g + decay * m
    h_ref[...] = h
    row = lax.broadcasted_iota(jnp.int32, (SLOT, LANES), 0)
    out = jnp.where(row == NORM_ROW, total, h)
    a = m - 0.9 * v_ref[...]
    for k in range(NZ * NY):
        o_ref[k, :SLOT, :] = out
        o_ref[k, SLOT:, :] = a


def group_kernel(s_ref, o_ref):
    total = s_ref[0, NORM_ROW : NORM_ROW + 1, :]
    for k in range(1, NZ * NY):
        total = total + s_ref[k, NORM_ROW : NORM_ROW + 1, :]
    o_ref[...] = jnp.broadcast_to(total[None], o_ref.shape)


def update_kernel(tab_ref, n_ref, s_ref, h_ref, m_ref, v_ref, w_ref, om_ref, ov_ref, hs, as_, turn):
    norms = jnp.sum(n_ref[...], axis=0)
    lane1 = lax.broadcasted_iota(jnp.int32, (1, LANES), 1)
    trusts = []
    for l in range(LAYERS):
        wsq = jnp.sum(jnp.where(lane1 == l, norms, 0.0), axis=1, keepdims=True)
        gsq = jnp.sum(jnp.where(lane1 == 8 + l, norms, 0.0), axis=1, keepdims=True)
        wnorm, gnorm = jnp.sqrt(wsq), jnp.sqrt(gsq)
        skip = skipped(tab_ref, l)
        ratio = 0.02 * wnorm / (gnorm + 0.001 * wnorm + 1e-06)
        trusts.append(skip + (1.0 - skip) * ratio)

    def trust_at(pos):
        trust = jnp.zeros(pos.shape, f32)
        for l in range(LAYERS):
            trust = jnp.where(in_layer(tab_ref, l, pos), trusts[l], trust)
        return trust

    for at, block in ((0, hs), (SLOT, as_)):
        for z in range(NZ):
            carry = None
            for y in range(NY):
                base = z * TALL + y * Y_ROWS
                block[base : base + Y_ROWS + 1, :] = s_ref[z * NY + y, at : at + Y_ROWS + 1, :]
                if carry is not None:
                    block[base : base + 1, :] += carry
                carry = s_ref[z * NY + y, at + Y_ROWS : at + Y_ROWS + 1, :]
    q = q_index()
    row = lax.broadcasted_iota(jnp.int32, (BLOCK_ROWS, LANES), 0)
    lane = lax.broadcasted_iota(jnp.int32, (BLOCK_ROWS, LANES), 1)
    extra = jnp.zeros((BLOCK_ROWS, LANES), jnp.int32)
    for z in range(1, NZ):
        extra = jnp.where(row >= z * TALL, z * (Z_ROWS - TALL), extra)
    pos = (row + extra + q * Q_ROWS) * LANES + lane
    w_ref[...] = (as_[...] - 8.0 * trust_at(pos) * hs[...]).astype(bf16)

    y = lax.axis_index("y")
    shift = 2 * (NY * q + y)
    pos, _ = slot_positions()
    new_v = 0.9 * v_ref[...] + 8.0 * trust_at(pos) * h_ref[...]
    new_m = m_ref[...] - new_v
    lane = lax.broadcasted_iota(jnp.int32, (SLOT, LANES), 1)
    for own, out in ((new_m, om_ref), (new_v, ov_ref)):
        turned = pltpu.roll(own, lax.rem(LANES - shift, LANES), 1)
        turn[:SLOT, :] = turned
        turn[SLOT:, :] = jnp.zeros((8, LANES), f32)
        out[...] = jnp.where(lane < LANES - shift, turned, turn[1 : SLOT + 1, :])


def lay_out_kernel(a_ref, b_ref, o_ref, block, rows):
    c = lax.axis_index("c")
    for q in range(NQ):
        x, cc = q // NC, q % NC
        block[...] = jnp.where(c == cc, a_ref[x].astype(f32), b_ref[x].astype(f32))
        for z in range(NZ):
            base = row_of(z, q)
            if q == 0:
                rows[base : base + TALL, :] = block[z * TALL : (z + 1) * TALL, :]
            else:
                rows[base : base + 1, :] += block[z * TALL : z * TALL + 1, :]
                rows[base + 1 : base + TALL, :] = block[z * TALL + 1 : (z + 1) * TALL, :]

    def narrow(k, _):
        at = pl.ds(pl.multiple_of(k * 136, 8), 136)
        o_ref[at, :] = rows[at, :].astype(bf16)
        return _

    lax.fori_loop(0, ROWS // 136, narrow, 0)


def sent(x, axes):
    return lax.all_to_all(x, axes, 0, 0, tiled=True)


def shards(grads, master, velocity, layer_offsets, layer_sizes, lars_skip):
    shift = 2 * (NY * q_index() + lax.axis_index("y"))
    tab = jnp.concatenate([layer_offsets, layer_sizes, lars_skip])

    def placed(a):
        flat = lax.dynamic_update_slice(jnp.zeros((SLOT * LANES,), f32), a, (shift,))
        return flat.reshape(SLOT, LANES)

    m, v, grads, tab = lax.optimization_barrier((placed(master), placed(velocity), grads, tab))
    wide = grads.astype(f32).reshape(ROWS, LANES)
    tall = (BLOCK_ROWS, LANES)
    packed = call(pack_kernel, shape(NQ, *tall, dtype=bf16), [VMEM], [tall])(wide)
    received = sent(packed, ("x", "c"))
    slots = shape(NZ * NY, SLOT, LANES)
    slot = shape(SLOT, LANES)
    spread = call(spread_kernel, slots, [VMEM], [tall])(received)
    reduced = sent(spread, ("z", "y"))
    pairs = shape(NZ * NY, 2 * SLOT, LANES)
    shared, h = call(owner_kernel, (pairs, slot), [SMEM] + [VMEM] * 3)(tab, reduced, m, v)
    shared = sent(shared, ("z", "y"))
    norms = call(group_kernel, shape(NQ, 1, LANES), [VMEM])(shared)
    norms = sent(norms, ("x", "c"))
    w, new_master, new_velocity = call(
        update_kernel,
        (shape(*tall, dtype=bf16), slot, slot),
        [SMEM] + [VMEM] * 5,
        [tall, tall, (SLOT + 8, LANES)],
    )(tab, norms, shared, h, m, v)
    w = lax.all_gather(w, "x")
    other = lax.ppermute(w, "c", [(0, 1), (1, 0)])
    weights = call(
        lay_out_kernel, shape(ROWS, LANES, dtype=bf16), [VMEM, VMEM], [tall, (ROWS, LANES)]
    )(w, other)
    return (
        weights.reshape(ROWS * LANES),
        new_master.reshape(SLOT * LANES)[:SHARD],
        new_velocity.reshape(SLOT * LANES)[:SHARD],
    )


def solution(mesh):
    finer = Mesh(mesh.devices.reshape(NZ, NX, NC, NY), AXES)
    owned = P(AXES)
    in_specs = (P(("z", "x", "c"), "y", None), owned, owned, P(), P(), P())

    return jax.shard_map(
        shards, mesh=finer, in_specs=in_specs, out_specs=(P(), owned, owned), check_vma=False
    )
```

time: 141 us -> 139 us (0.986)
  blocking collectives: 73.4 us -> 116 us
  waiting for transfers between devices: 33.8 us -> 2 us
  starting transfers between devices: 19.5 us -> 5.81 us
    all_to_all x3 -> x4, blocking collectives: 61.3 us -> 105 us  [sent(): return lax.all_to_all(x, axes, 0, 0, tiled=True)]
    all_to_all x2 -> x0, waiting for transfers between devices: 31.7 us -> none  [sent(): return lax.all_to_all(x, axes, 0, 0, tiled=True)]
    all_to_all x2 -> x0, starting transfers between devices: 13.3 us -> none  [sent(): return lax.all_to_all(x, axes, 0, 0, tiled=True)]
    pallas_call x4 -> x6, Pallas kernels: 4.36 us -> 5.69 us  [the longest x1 2.19 us: shards(): call(lay_out_kernel, shape(ROWS, LANES, dtype=bf16), [VMEM, VMEM], [tall,...]
  transfers between devices with their start and end apart: 3 -> 1, of which waited for: 3 -> 1; matrix products, arithmetic and copies ran while one was open for 0% -> 0% of each run, Pallas kernels for 0% -> 0%
where the time goes in v2:
time: 139 us
  blocking collectives  116 us (83%)
  other arithmetic  6.94 us (5%)
  starting transfers between devices  5.81 us (4%)
  Pallas kernels  5.69 us (4%)
  waiting for transfers between devices  2 us (1%)
  local copies, waits for them, and re-layouts  1.8 us (1%)
    all_to_all x4, blocking collectives, sent(): return lax.all_to_all(x, axes, 0, 0, tiled=True)  105 us
    all_gather x1, blocking collectives, shards(): w = lax.all_gather(w, 'x')  10.9 us
    reshape x1, other arithmetic, shards(): wide = grads.astype(f32).reshape(ROWS, LANES)  6.17 us
    ppermute x1, starting transfers between devices, shards(): other = lax.ppermute(w, 'c', [(0, 1), (1, 0)])  5.81 us
  transfers between devices with their start and end apart: 1, of which 1 were waited for; matrix products, arithmetic and copies ran while one was open for 0% of the time, Pallas kernels for 0%

profile of v2, /device:TPU:1, one launch (start us, length us, event | category | flops | bytes accessed | tf_op | source)
XLA Modules:
  0.0 139.0 jit_solution(5909091591632088535)
XLA Ops:
  0.6 0.9 dynamic_update_slice.6
  1.6 0.9 dynamic_update_slice.7
  2.4 0.8 pad_add_fusion.tab_ref
  3.2 6.2 %reshape.33 = f32[1,1,852992]{2,1,0:T(1,128)S(1)} convert(bf16[1,1,852992]{2,1,0:T(2,128)(2,1)} %param.6) | non-fusion elementwise | flops 852992 | bytes 5117952 | tf_op jit(solution)/shard_map/reshape | solution.py:208
  9.4 0.4 shard_map.85
  9.8 31.5 %all_to_all.20.r_ref = bf16[8,840,128]{2,1,0:T(8,128)(2,1)S(1)} all-to-all(bf16[8,840,128]{2,1,0:T(8,128)(2,1)S(1)} %shard_map.85), channel_id=1, replica_groups=mesh['z'=8,'x'=4,'c'=2,'y'=8] {'x','c'}, dimensions={0} | all-to-all | bytes 3440640 | tf_op jit(solution)/shard_map/all_to_all | solution.py:196
  41.3 0.4 shard_map.86
  41.7 29.6 %all_to_all.21.r_ref = f32[64,16,128]{2,1,0:T(8,128)S(1)} all-to-all(f32[64,16,128]{2,1,0:T(8,128)S(1)} %shard_map.86), channel_id=1, replica_groups=mesh['z'=8,'x'=4,'c'=2,'y'=8] {'z','y'}, dimensions={0} | all-to-all | bytes 1048576 | tf_op jit(solution)/shard_map/all_to_all | solution.py:196
  71.3 0.8 shard_map.87
  72.1 32.7 %all_to_all.22.s_ref = f32[64,32,128]{2,1,0:T(8,128)S(1)} all-to-all(f32[64,32,128]{2,1,0:T(8,128)S(1)} %get-tuple-element.16), channel_id=1, replica_groups=mesh['z'=8,'x'=4,'c'=2,'y'=8] {'z','y'}, dimensions={0} | all-to-all | bytes 2097152 | tf_op jit(solution)/shard_map/all_to_all | solution.py:196
  104.8 0.1 shard_map.88
  104.8 11.4 %all_to_all.23.n_ref = f32[8,1,128]{2,1,0:T(1,128)S(1)} all-to-all(f32[8,1,128]{2,1,0:T(1,128)S(1)} %shard_map.88), channel_id=1, replica_groups=mesh['z'=8,'x'=4,'c'=2,'y'=8] {'x','c'}, dimensions={0} | all-to-all | bytes 8192 | tf_op jit(solution)/shard_map/all_to_all | solution.py:196
  116.2 1.9 %shard_map.89 = (bf16[840,128]{1,0:T(8,128)(2,1)S(1)}, f32[16,128]{1,0:T(8,128)}, f32[16,128]{1,0:T(8,128)}) custom-call(s32[18]{0:T(128)S(1)} %pad_add_fusion.tab_ref, f32[8,1,128]{2,1,0:T(1,128)S(1)} %all_to_all.23.n_ref, f32[64,32,128]{2,1,0:T(8,128)S(1)} %all_to_all.22.s_ref, f32[16,128]{1,0:T(8,128)S(1)} %get-tuple-element.17.h_ref, ...), custom_call_target="tpu_custom_call" | custom-call | tf_op jit(solution)/shard_map/pallas_call | solution.py:221
  118.1 10.9 %all-gather = bf16[3360,128]{1,0:T(8,128)(2,1)S(1)} all-gather(bf16[840,128]{1,0:T(8,128)(2,1)S(1)} %get-tuple-element.18), channel_id=2, replica_groups=mesh['z'=8,'x'=4,'c'=2,'y'=8] {'x'}, dimensions={0}, use_global_device_ids=true | all-gather | bytes 1075200 | tf_op jit(solution)/shard_map/all_gather | solution.py:227
  129.0 5.8 %collective-permute-start = (bf16[4,840,128]{2,1,0:T(8,128)(2,1)S(1)}, bf16[4,840,128]{2,1,0:T(8,128)(2,1)S(1)}, u32[]{:S(2)}, u32[]{:S(2)}) collective-permute-start(bf16[4,840,128]{2,1,0:T(8,128)(2,1)S(1)} %bitcast.10), channel_id=1, source_target_pairs={{0,8},{8,0},{1,9},{9,1},{2,10},{10,2},{3,11},{11,3},{4,12},{12,4},... | collective-permute-start | bytes 2580488 | tf_op jit(solution)/shard_map/ppermute | solution.py:228
  134.8 2.0 %collective-permute-done.b_ref = bf16[4,840,128]{2,1,0:T(8,128)(2,1)S(1)} collective-permute-done((bf16[4,840,128]{2,1,0:T(8,128)(2,1)S(1)}, bf16[4,840,128]{2,1,0:T(8,128)(2,1)S(1)}, u32[]{:S(2)}, u32[]{:S(2)}) %collective-permute-start) | collective-permute-done | bytes 860192 | tf_op jit(solution)/shard_map/ppermute | solution.py:228
  136.8 2.2 %shard_map.90 = bf16[6664,128]{1,0:T(8,128)(2,1)} custom-call(bf16[4,840,128]{2,1,0:T(8,128)(2,1)S(1)} %bitcast.11, bf16[4,840,128]{2,1,0:T(8,128)(2,1)S(1)} %collective-permute-done.b_ref), custom_call_target="tpu_custom_call" | custom-call | tf_op jit(solution)/shard_map/pallas_call | solution.py:229
  (2 shorter events, 0.0 us)
Async XLA Ops:
  129.0 7.8 %collective-permute-start = (bf16[4,840,128]{2,1,0:T(8,128)(2,1)S(1)}, bf16[4,840,128]{2,1,0:T(8,128)(2,1)S(1)}, u32[]{:S(2)}, u32[]{:S(2)}) collective-permute-start(bf16[4,840,128]{2,1,0:T(8,128)(2,1)S(1)} %bitcast.10), channel_id=1, source_target_pairs={{0,8},{8,0},{1,9},{9,1},{2,10},{10,2},{3,11},{11,3},{4,12},{12,4},... | collective-permute-start | bytes 2580488 | tf_op jit(solution)/shard_map/ppermute | solution.py:228

commit v3 on v2

--- a/solution.py
+++ b/solution.py
@@ -17,8 +17,9 @@
 Y_ROWS = 13
 SLOT = 16
 NORM_ROW = 14
-TALL = 105
-BLOCK_ROWS = NZ * TALL
+TOUCHED = 105
+BLOCK_ROWS = NZ * TOUCHED
+TALL = 112
 LAYERS = 6
 f32 = jnp.float32
 bf16 = jnp.bfloat16
@@ -55,7 +56,7 @@
     for q in range(NQ):
         for z in range(NZ):
             base = row_of(z, q)
-            rows[z * TALL : (z + 1) * TALL, :] = x_ref[base : base + TALL, :]
+            rows[z * TOUCHED : (z + 1) * TOUCHED, :] = x_ref[base : base + TOUCHED, :]
         o_ref[q] = rows[...].astype(bf16)
 
 
@@ -66,7 +67,7 @@
     rows[...] = total
     for z in range(NZ):
         for y in range(NY):
-            base = z * TALL + y * Y_ROWS
+            base = z * TOUCHED + y * Y_ROWS
             o_ref[z * NY + y, :NORM_ROW, :] = rows[base : base + NORM_ROW, :]
             o_ref[z * NY + y, NORM_ROW:, :] = jnp.zeros((SLOT - NORM_ROW, LANES), f32)
 
@@ -110,19 +111,28 @@
     row = lax.broadcasted_iota(jnp.int32, (SLOT, LANES), 0)
     out = jnp.where(row == NORM_ROW, total, h)
     a = m - 0.9 * v_ref[...]
-    for k in range(NZ * NY):
+    for k in range(NY):
         o_ref[k, :SLOT, :] = out
         o_ref[k, SLOT:, :] = a
 
 
-def group_kernel(s_ref, o_ref):
+def group_kernel(s_ref, n_ref, hs_ref, as_ref):
     total = s_ref[0, NORM_ROW : NORM_ROW + 1, :]
-    for k in range(1, NZ * NY):
-        total = total + s_ref[k, NORM_ROW : NORM_ROW + 1, :]
-    o_ref[...] = jnp.broadcast_to(total[None], o_ref.shape)
-
-
-def update_kernel(tab_ref, n_ref, s_ref, h_ref, m_ref, v_ref, w_ref, om_ref, ov_ref, hs, as_, turn):
+    for y in range(1, NY):
+        total = total + s_ref[y, NORM_ROW : NORM_ROW + 1, :]
+    n_ref[...] = jnp.broadcast_to(total[None], n_ref.shape)
+    for at, block in ((0, hs_ref), (SLOT, as_ref)):
+        carry = None
+        block[NY * Y_ROWS :, :] = jnp.zeros((TALL - NY * Y_ROWS, LANES), f32)
+        for y in range(NY):
+            base = y * Y_ROWS
+            block[base : base + Y_ROWS + 1, :] = s_ref[y, at : at + Y_ROWS + 1, :]
+            if carry is not None:
+                block[base : base + 1, :] += carry
+            carry = s_ref[y, at + Y_ROWS : at + Y_ROWS + 1, :]
+
+
+def update_kernel(tab_ref, n_ref, hs_ref, as_ref, h_ref, m_ref, v_ref, w_ref, om_ref, ov_ref, turn):
     norms = jnp.sum(n_ref[...], axis=0)
     lane1 = lax.broadcasted_iota(jnp.int32, (1, LANES), 1)
     trusts = []
@@ -140,23 +150,13 @@
             trust = jnp.where(in_layer(tab_ref, l, pos), trusts[l], trust)
         return trust
 
-    for at, block in ((0, hs), (SLOT, as_)):
-        for z in range(NZ):
-            carry = None
-            for y in range(NY):
-                base = z * TALL + y * Y_ROWS
-                block[base : base + Y_ROWS + 1, :] = s_ref[z * NY + y, at : at + Y_ROWS + 1, :]
-                if carry is not None:
-                    block[base : base + 1, :] += carry
-                carry = s_ref[z * NY + y, at + Y_ROWS : at + Y_ROWS + 1, :]
     q = q_index()
-    row = lax.broadcasted_iota(jnp.int32, (BLOCK_ROWS, LANES), 0)
-    lane = lax.broadcasted_iota(jnp.int32, (BLOCK_ROWS, LANES), 1)
-    extra = jnp.zeros((BLOCK_ROWS, LANES), jnp.int32)
-    for z in range(1, NZ):
-        extra = jnp.where(row >= z * TALL, z * (Z_ROWS - TALL), extra)
-    pos = (row + extra + q * Q_ROWS) * LANES + lane
-    w_ref[...] = (as_[...] - 8.0 * trust_at(pos) * hs[...]).astype(bf16)
+    row = lax.broadcasted_iota(jnp.int32, (TALL, LANES), 0)
+    lane = lax.broadcasted_iota(jnp.int32, (TALL, LANES), 1)
+    pos = (row + lax.axis_index("z") * Z_ROWS + q * Q_ROWS) * LANES + lane
+    w = (as_ref[...] - 8.0 * trust_at(pos) * hs_ref[...]).astype(bf16)
+    for z in range(NZ):
+        w_ref[z] = w
 
     y = lax.axis_index("y")
     shift = 2 * (NY * q + y)
@@ -171,18 +171,19 @@
         out[...] = jnp.where(lane < LANES - shift, turned, turn[1 : SLOT + 1, :])
 
 
-def lay_out_kernel(a_ref, b_ref, o_ref, block, rows):
+def lay_out_kernel(a_ref, b_ref, o_ref, rows):
     c = lax.axis_index("c")
-    for q in range(NQ):
-        x, cc = q // NC, q % NC
-        block[...] = jnp.where(c == cc, a_ref[x].astype(f32), b_ref[x].astype(f32))
-        for z in range(NZ):
+    for z in range(NZ):
+        carry = None
+        for q in range(NQ):
+            x, cc = q // NC, q % NC
+            block = jnp.where(c == cc, a_ref[x, z].astype(f32), b_ref[x, z].astype(f32))
             base = row_of(z, q)
-            if q == 0:
-                rows[base : base + TALL, :] = block[z * TALL : (z + 1) * TALL, :]
-            else:
-                rows[base : base + 1, :] += block[z * TALL : z * TALL + 1, :]
-                rows[base + 1 : base + TALL, :] = block[z * TALL + 1 : (z + 1) * TALL, :]
+            rows[base : base + Q_ROWS, :] = block[:Q_ROWS, :]
+            if carry is not None:
+                rows[base : base + 1, :] += carry
+            carry = block[Q_ROWS : Q_ROWS + 1, :]
+        rows[row_of(z, NQ) : row_of(z, NQ) + 1, :] = carry
 
     def narrow(k, _):
         at = pl.ds(pl.multiple_of(k * 136, 8), 136)
@@ -204,30 +205,32 @@
         flat = lax.dynamic_update_slice(jnp.zeros((SLOT * LANES,), f32), a, (shift,))
         return flat.reshape(SLOT, LANES)
 
-    m, v, grads, tab = lax.optimization_barrier((placed(master), placed(velocity), grads, tab))
+    m, v = placed(master), placed(velocity)
     wide = grads.astype(f32).reshape(ROWS, LANES)
-    tall = (BLOCK_ROWS, LANES)
-    packed = call(pack_kernel, shape(NQ, *tall, dtype=bf16), [VMEM], [tall])(wide)
+    strip = (BLOCK_ROWS, LANES)
+    packed = call(pack_kernel, shape(NQ, *strip, dtype=bf16), [VMEM], [strip])(wide)
     received = sent(packed, ("x", "c"))
     slots = shape(NZ * NY, SLOT, LANES)
     slot = shape(SLOT, LANES)
-    spread = call(spread_kernel, slots, [VMEM], [tall])(received)
+    spread = call(spread_kernel, slots, [VMEM], [strip])(received)
     reduced = sent(spread, ("z", "y"))
-    pairs = shape(NZ * NY, 2 * SLOT, LANES)
+    pairs = shape(NY, 2 * SLOT, LANES)
     shared, h = call(owner_kernel, (pairs, slot), [SMEM] + [VMEM] * 3)(tab, reduced, m, v)
-    shared = sent(shared, ("z", "y"))
-    norms = call(group_kernel, shape(NQ, 1, LANES), [VMEM])(shared)
-    norms = sent(norms, ("x", "c"))
+    tall = shape(TALL, LANES)
+    norms, hs, as_ = call(group_kernel, (shape(NZ * NQ, 1, LANES), tall, tall), [VMEM])(
+        sent(shared, "y")
+    )
     w, new_master, new_velocity = call(
         update_kernel,
-        (shape(*tall, dtype=bf16), slot, slot),
-        [SMEM] + [VMEM] * 5,
-        [tall, tall, (SLOT + 8, LANES)],
-    )(tab, norms, shared, h, m, v)
-    w = lax.all_gather(w, "x")
+        (shape(NZ, TALL, LANES, dtype=bf16), slot, slot),
+        [SMEM] + [VMEM] * 6,
+        [(SLOT + 8, LANES)],
+    )(tab, sent(norms, ("z", "x", "c")), hs, as_, h, m, v)
+    w = sent(w, "z").reshape(NZ * TALL, LANES)
+    w = lax.all_gather(w, "x").reshape(NX, NZ, TALL, LANES)
     other = lax.ppermute(w, "c", [(0, 1), (1, 0)])
     weights = call(
-        lay_out_kernel, shape(ROWS, LANES, dtype=bf16), [VMEM, VMEM], [tall, (ROWS, LANES)]
+        lay_out_kernel, shape(ROWS, LANES, dtype=bf16), [VMEM, VMEM], [(ROWS, LANES)]
     )(w, other)
     return (
         weights.reshape(ROWS * LANES),

time: 139 us -> 136 us (0.978)
  blocking collectives: 116 us -> 85 us
  waiting for transfers between devices: 2 us -> 18.5 us
  starting transfers between devices: 5.81 us -> 18.9 us
    all_to_all x4, blocking collectives: 105 us -> 72.9 us  [sent(): return lax.all_to_all(x, axes, 0, 0, tiled=True)]
    all_to_all x0 -> x1, waiting for transfers between devices: none -> 16.4 us  [sent(): return lax.all_to_all(x, axes, 0, 0, tiled=True)]
    all_to_all x0 -> x1, starting transfers between devices: none -> 12.6 us  [sent(): return lax.all_to_all(x, axes, 0, 0, tiled=True)]
  transfers between devices with their start and end apart: 1 -> 2, of which waited for: 1 -> 2; matrix products, arithmetic and copies ran while one was open for 0% -> 0% of each run, Pallas kernels for 0% -> 0%
where the time goes in v3:
time: 136 us
  blocking collectives  85 us (62%)
  starting transfers between devices  18.9 us (14%)
  waiting for transfers between devices  18.5 us (14%)
  other arithmetic  6.25 us (5%)
  Pallas kernels  5.66 us (4%)
    all_to_all x4, blocking collectives, sent(): return lax.all_to_all(x, axes, 0, 0, tiled=True)  72.9 us
    all_to_all x1, waiting for transfers between devices, sent(): return lax.all_to_all(x, axes, 0, 0, tiled=True)  16.4 us
    all_to_all x1, starting transfers between devices, sent(): return lax.all_to_all(x, axes, 0, 0, tiled=True)  12.6 us
    all_gather x1, blocking collectives, shards(): w = lax.all_gather(w, 'x').reshape(NX, NZ, TALL, LANES)  12.1 us
    ppermute x1, starting transfers between devices, shards(): other = lax.ppermute(w, 'c', [(0, 1), (1, 0)])  6.24 us
    reshape x1, other arithmetic, shards(): wide = grads.astype(f32).reshape(ROWS, LANES)  6.18 us
  transfers between devices with their start and end apart: 2, of which 2 were waited for; matrix products, arithmetic and copies ran while one was open for 0% of the time, Pallas kernels for 0%

profile of v3, /device:TPU:1, one launch (start us, length us, event | category | flops | bytes accessed | tf_op | source)
XLA Modules:
  0.0 135.6 jit_solution(8804710420623668523)
XLA Ops:
  0.6 6.2 %reshape.37 = f32[1,1,852992]{2,1,0:T(1,128)S(1)} convert(bf16[1,1,852992]{2,1,0:T(2,128)(2,1)} %param.6) | non-fusion elementwise | flops 852992 | bytes 5117952 | tf_op jit(solution)/shard_map/reshape | solution.py:209
  6.8 0.4 shard_map.85
  7.2 31.5 %all_to_all.25.r_ref = bf16[8,840,128]{2,1,0:T(8,128)(2,1)S(1)} all-to-all(bf16[8,840,128]{2,1,0:T(8,128)(2,1)S(1)} %shard_map.85), channel_id=1, replica_groups=mesh['z'=8,'x'=4,'c'=2,'y'=8] {'x','c'}, dimensions={0} | all-to-all | bytes 3440640 | tf_op jit(solution)/shard_map/all_to_all | solution.py:197
  38.7 0.0 copy-start
  38.7 0.0 copy-start.1
  38.7 0.0 copy-start.2
  38.7 0.0 copy-start.3
  38.8 0.0 copy-start.4
  38.8 1.2 shard_map.86
  39.9 12.6 %all-to-all-start.1 = ((f32[64,16,128]{2,1,0:T(8,128)}), f32[64,16,128]{2,1,0:T(8,128)S(1)}, u32[]{:S(2)}, u32[]{:S(2)}) async-start(f32[64,16,128]{2,1,0:T(8,128)} %shard_map.86), calls=%async_computation.1 | async-start | bytes 1048576 | tf_op jit(solution)/shard_map/all_to_all | solution.py:197
  52.6 0.0 copy-done
  52.6 0.3 dynamic_update_slice.6
  52.9 0.0 copy-done.1
  52.9 0.3 dynamic_update_slice.7
  53.2 0.0 copy-done.2
  53.2 0.0 copy-done.3
  53.2 0.0 copy-done.4
  53.2 0.1 pad_add_fusion.tab_ref
  53.3 16.4 %all-to-all-done.1.r_ref = f32[64,16,128]{2,1,0:T(8,128)S(1)} async-done(((f32[64,16,128]{2,1,0:T(8,128)}), f32[64,16,128]{2,1,0:T(8,128)S(1)}, u32[]{:S(2)}, u32[]{:S(2)}) %all-to-all-start.1) | async-done | bytes 524320 | tf_op jit(solution)/shard_map/all_to_all | solution.py:197
  69.7 0.7 shard_map.87
  70.4 12.0 %all_to_all.26.s_ref = f32[8,32,128]{2,1,0:T(8,128)S(1)} all-to-all(f32[8,32,128]{2,1,0:T(8,128)S(1)} %get-tuple-element.11), channel_id=1, replica_groups=mesh['z'=8,'x'=4,'c'=2,'y'=8] {'y'}, dimensions={0} | all-to-all | bytes 262144 | tf_op jit(solution)/shard_map/all_to_all | solution.py:197
  82.5 16.8 %all_to_all.27.n_ref = f32[64,1,128]{2,1,0:T(1,128)S(1)} all-to-all(f32[64,1,128]{2,1,0:T(1,128)S(1)} %get-tuple-element.12), channel_id=1, replica_groups=mesh['z'=8,'x'=4,'c'=2,'y'=8] {'z','x','c'}, dimensions={0} | all-to-all | bytes 65536 | tf_op jit(solution)/shard_map/all_to_all | solution.py:197
  99.3 1.5 %shard_map.89 = (bf16[8,112,128]{2,1,0:T(8,128)(2,1)S(1)}, f32[16,128]{1,0:T(8,128)}, f32[16,128]{1,0:T(8,128)}) custom-call(s32[18]{0:T(128)S(1)} %pad_add_fusion.tab_ref, f32[64,1,128]{2,1,0:T(1,128)S(1)} %all_to_all.27.n_ref, f32[112,128]{1,0:T(8,128)S(1)} %get-tuple-element.13.hs_ref, f32[112,128]{1,0:T(8,128)S(1)} %get-tuple-element.14.as_ref, ...), custom_call_target="tpu_custom_call" | custom-call | tf_op jit(solution)/shard_map/pallas_call | solution.py:223
  100.8 12.5 %all_to_all.28 = bf16[8,112,128]{2,1,0:T(8,128)(2,1)S(1)} all-to-all(bf16[8,112,128]{2,1,0:T(8,128)(2,1)S(1)} %get-tuple-element.16), channel_id=1, replica_groups=mesh['z'=8,'x'=4,'c'=2,'y'=8] {'z'}, dimensions={0} | all-to-all | bytes 458752 | tf_op jit(solution)/shard_map/all_to_all | solution.py:197
  113.3 12.1 %all_gather.3 = bf16[4,896,128]{2,1,0:T(8,128)(2,1)S(1)} all-gather(bf16[1,896,128]{2,1,0:T(8,128)(2,1)S(1)} %bitcast.18), channel_id=1, replica_groups=mesh['z'=8,'x'=4,'c'=2,'y'=8] {'x'}, dimensions={0}, use_global_device_ids=true | all-gather | bytes 1146880 | tf_op jit(solution)/shard_map/all_gather | solution.py:230
  125.4 6.2 %collective-permute-start = (bf16[4,8,112,128]{3,2,1,0:T(8,128)(2,1)S(1)}, bf16[4,8,112,128]{3,2,1,0:T(8,128)(2,1)S(1)}, u32[]{:S(2)}, u32[]{:S(2)}) collective-permute-start(bf16[4,8,112,128]{3,2,1,0:T(8,128)(2,1)S(1)} %bitcast.11), channel_id=1, source_target_pairs={{0,8},{8,0},{1,9},{9,1},{2,10},{10,2},{3,11},{11,3},{4,12},{12,4},... | collective-permute-start | bytes 2752520 | tf_op jit(solution)/shard_map/ppermute | solution.py:231
  131.7 2.1 %collective-permute-done.b_ref = bf16[4,8,112,128]{3,2,1,0:T(8,128)(2,1)S(1)} collective-permute-done((bf16[4,8,112,128]{3,2,1,0:T(8,128)(2,1)S(1)}, bf16[4,8,112,128]{3,2,1,0:T(8,128)(2,1)S(1)}, u32[]{:S(2)}, u32[]{:S(2)}) %collective-permute-start) | collective-permute-done | bytes 917536 | tf_op jit(solution)/shard_map/ppermute | solution.py:231
  133.7 1.9 %shard_map.90 = bf16[6664,128]{1,0:T(8,128)(2,1)} custom-call(bf16[4,8,112,128]{3,2,1,0:T(8,128)(2,1)S(1)} %bitcast.12, bf16[4,8,112,128]{3,2,1,0:T(8,128)(2,1)S(1)} %collective-permute-done.b_ref), custom_call_target="tpu_custom_call" | custom-call | tf_op jit(solution)/shard_map/pallas_call | solution.py:232
  (3 shorter events, 0.0 us)
Async XLA Ops:
  38.7 13.9 %copy-start = (f32[1666]{0:T(1024)S(1)}, f32[1666]{0:T(1024)}, u32[]{:S(2)}) copy-start(f32[1666]{0:T(1024)} %param.7) | copy-start | bytes 19996
  38.7 14.2 %copy-start.1 = (f32[1666]{0:T(1024)S(1)}, f32[1666]{0:T(1024)}, u32[]{:S(2)}) copy-start(f32[1666]{0:T(1024)} %param.8) | copy-start | bytes 19996
  38.7 14.5 %copy-start.2 = (s32[6]{0:T(128)S(1)}, s32[6]{0:T(128)}, u32[]{:S(2)}) copy-start(s32[6]{0:T(128)} %param.11) | copy-start | bytes 76
  38.7 14.5 %copy-start.3 = (s32[6]{0:T(128)S(1)}, s32[6]{0:T(128)}, u32[]{:S(2)}) copy-start(s32[6]{0:T(128)} %param.10) | copy-start | bytes 76
  38.8 14.5 %copy-start.4 = (s32[6]{0:T(128)S(1)}, s32[6]{0:T(128)}, u32[]{:S(2)}) copy-start(s32[6]{0:T(128)} %param.9) | copy-start | bytes 76
  39.9 29.8 %all-to-all-start.1 = ((f32[64,16,128]{2,1,0:T(8,128)}), f32[64,16,128]{2,1,0:T(8,128)S(1)}, u32[]{:S(2)}, u32[]{:S(2)}) async-start(f32[64,16,128]{2,1,0:T(8,128)} %shard_map.86), calls=%async_computation.1 | async-start | bytes 1048576 | tf_op jit(solution)/shard_map/all_to_all | solution.py:197
  125.4 8.3 %collective-permute-start = (bf16[4,8,112,128]{3,2,1,0:T(8,128)(2,1)S(1)}, bf16[4,8,112,128]{3,2,1,0:T(8,128)(2,1)S(1)}, u32[]{:S(2)}, u32[]{:S(2)}) collective-permute-start(bf16[4,8,112,128]{3,2,1,0:T(8,128)(2,1)S(1)} %bitcast.11), channel_id=1, source_target_pairs={{0,8},{8,0},{1,9},{9,1},{2,10},{10,2},{3,11},{11,3},{4,12},{12,4},... | collective-permute-start | bytes 2752520 | tf_op jit(solution)/shard_map/ppermute | solution.py:231

commit v4 on v2

v4 whole, which is shorter than its diff:
```python
import jax
import jax.numpy as jnp
from jax import lax
from jax.experimental import pallas as pl
from jax.experimental.pallas import tpu as pltpu
from jax.sharding import Mesh
from jax.sharding import PartitionSpec as P

AXES = ("zh", "zl", "x", "c", "yh", "yl")
NEAR = ("zl", "x", "c", "yl")
FAR = ("zh", "yh")
NX, NC, NL, NH = 4, 2, 2, 4
NY, NZ = NH * NL, NH * NL
NQ = NX * NC
N_NEAR, N_FAR = NL * NQ * NL, NH * NH
LANES = 128
SHARD = 1666
ROWS = 6664
Z_ROWS = ROWS // NZ
Q_ROWS = 104
Y_ROWS = 13
TOUCHED = 14
SLOT = 16
NEAR_ROWS = N_FAR * TOUCHED
LAYERS = 6
f32 = jnp.float32
bf16 = jnp.bfloat16
VMEM = pl.BlockSpec(memory_space=pltpu.VMEM)
SMEM = pl.BlockSpec(memory_space=pltpu.SMEM)
PARAMS = pltpu.CompilerParams(vmem_limit_bytes=40 * 1024 * 1024)


def shape(*dims, dtype=f32):
    return jax.ShapeDtypeStruct(dims, dtype)


def call(kernel, out_shape, ins, scratch=()):
    many = isinstance(out_shape, tuple)
    return pl.pallas_call(
        kernel,
        out_shape=out_shape,
        in_specs=list(ins),
        out_specs=(VMEM,) * len(out_shape) if many else VMEM,
        scratch_shapes=[pltpu.VMEM(s, f32) for s in scratch],
        compiler_params=PARAMS,
    )


def row_of(z, q, y):
    return z * Z_ROWS + q * Q_ROWS + y * Y_ROWS


def z_index():
    return lax.axis_index("zh") * NL + lax.axis_index("zl")


def q_index():
    return lax.axis_index("x") * NC + lax.axis_index("c")


def y_index():
    return lax.axis_index("yh") * NL + lax.axis_index("yl")


def far_slots():
    return [(k, k // NH, k % NH) for k in range(N_FAR)]


def pack_kernel(x_ref, o_ref, rows):
    for near in range(N_NEAR):
        zl, q, yl = near // (NQ * NL), near // NL % NQ, near % NL
        for k, zh, yh in far_slots():
            base = row_of(zh * NL + zl, q, yh * NL + yl)
            rows[k * TOUCHED : (k + 1) * TOUCHED, :] = x_ref[base : base + TOUCHED, :]
        o_ref[near] = rows[...].astype(bf16)


def spread_kernel(r_ref, o_ref, rows):
    total = r_ref[0].astype(f32)
    for k in range(1, N_NEAR):
        total = total + r_ref[k].astype(f32)
    rows[...] = total
    for k in range(N_FAR):
        o_ref[k, :TOUCHED, :] = rows[k * TOUCHED : (k + 1) * TOUCHED, :]
        o_ref[k, TOUCHED:, :] = jnp.zeros((SLOT - TOUCHED, LANES), f32)


def slot_positions():
    q, y = q_index(), y_index()
    owner = (z_index() * NQ + q) * NY + y
    row = lax.broadcasted_iota(jnp.int32, (SLOT, LANES), 0)
    lane = lax.broadcasted_iota(jnp.int32, (SLOT, LANES), 1)
    local = row * LANES + lane - 2 * (NY * q + y)
    return local + owner * SHARD, (local >= 0) & (local < SHARD)


def in_layer(tab_ref, l, pos):
    start = tab_ref[l]
    return (pos >= start) & (pos < start + tab_ref[LAYERS + l])


def skipped(tab_ref, l):
    return tab_ref[2 * LAYERS + l].astype(f32)


def owner_kernel(tab_ref, r_ref, m_ref, v_ref, o_ref, h_ref):
    g = r_ref[0]
    for k in range(1, N_FAR):
        g = g + r_ref[k]
    pos, valid = slot_positions()
    g = jnp.where(valid, g * (1.0 / 512.0), 0.0)
    m = m_ref[...]
    lane = lax.broadcasted_iota(jnp.int32, (1, LANES), 1)
    total = jnp.zeros((1, LANES), f32)
    decay = jnp.zeros((SLOT, LANES), f32)
    for l in range(LAYERS):
        mask = in_layer(tab_ref, l, pos)
        decay = jnp.where(mask, (1.0 - skipped(tab_ref, l)) * 0.001, decay)
        for at, square in ((l, m * m), (8 + l, g * g)):
            rows = jnp.sum(jnp.where(mask, square, 0.0), axis=0, keepdims=True)
            total = total + jnp.where(lane == at, jnp.sum(rows, axis=1, keepdims=True), 0.0)
    h = g + decay * m
    h_ref[...] = h
    row = lax.broadcasted_iota(jnp.int32, (SLOT, LANES), 0)
    out = jnp.where(row == TOUCHED, total, h)
    a = m - 0.9 * v_ref[...]
    for k in range(N_FAR):
        o_ref[k, :SLOT, :] = out
        o_ref[k, SLOT:, :] = a


def group_kernel(s_ref, n_ref):
    total = s_ref[0, TOUCHED : TOUCHED + 1, :]
    for k in range(1, N_FAR):
        total = total + s_ref[k, TOUCHED : TOUCHED + 1, :]
    n_ref[...] = jnp.broadcast_to(total[None], n_ref.shape)


def update_kernel(tab_ref, n_ref, s_ref, h_ref, m_ref, v_ref, w_ref, om_ref, ov_ref, rows, turn):
    norms = jnp.sum(n_ref[...], axis=0)
    lane1 = lax.broadcasted_iota(jnp.int32, (1, LANES), 1)
    trusts = []
    for l in range(LAYERS):
        wsq = jnp.sum(jnp.where(lane1 == l, norms, 0.0), axis=1, keepdims=True)
        gsq = jnp.sum(jnp.where(lane1 == 8 + l, norms, 0.0), axis=1, keepdims=True)
        wnorm, gnorm = jnp.sqrt(wsq), jnp.sqrt(gsq)
        skip = skipped(tab_ref, l)
        ratio = 0.02 * wnorm / (gnorm + 0.001 * wnorm + 1e-06)
        trusts.append(skip + (1.0 - skip) * ratio)

    def trust_at(pos):
        trust = jnp.zeros(pos.shape, f32)
        for l in range(LAYERS):
            trust = jnp.where(in_layer(tab_ref, l, pos), trusts[l], trust)
        return trust

    q = q_index()
    at = lax.broadcasted_iota(jnp.int32, (SLOT, LANES), 0) * LANES
    at = at + lax.broadcasted_iota(jnp.int32, (SLOT, LANES), 1)
    for k, zh, yh in far_slots():
        z, y = zh * NL + lax.axis_index("zl"), yh * NL + lax.axis_index("yl")
        pos = at + row_of(z, q, y) * LANES
        w = s_ref[k, SLOT:, :] - 8.0 * trust_at(pos) * s_ref[k, :SLOT, :]
        rows[k * TOUCHED : (k + 1) * TOUCHED, :] = w[:TOUCHED, :]
    w = rows[...].astype(bf16)
    for k in range(NL * NX * NL):
        w_ref[k] = w

    shift = 2 * (NY * q + y_index())
    pos, _ = slot_positions()
    new_v = 0.9 * v_ref[...] + 8.0 * trust_at(pos) * h_ref[...]
    new_m = m_ref[...] - new_v
    lane = lax.broadcasted_iota(jnp.int32, (SLOT, LANES), 1)
    for own, out in ((new_m, om_ref), (new_v, ov_ref)):
        turned = pltpu.roll(own, lax.rem(LANES - shift, LANES), 1)
        turn[:SLOT, :] = turned
        turn[SLOT:, :] = jnp.zeros((8, LANES), f32)
        out[...] = jnp.where(lane < LANES - shift, turned, turn[1 : SLOT + 1, :])


def lay_out_kernel(a_ref, b_ref, o_ref, block, tail, rows):
    c = lax.axis_index("c")
    for near in range(N_NEAR):
        zl, q, yl = near // (NQ * NL), near // NL % NQ, near % NL
        cc, peer = q % NC, (zl * NX + q // NC) * NL + yl
        block[...] = jnp.where(c == cc, a_ref[peer].astype(f32), b_ref[peer].astype(f32))
        for k, zh, yh in far_slots():
            z, y = zh * NL + zl, yh * NL + yl
            base, at = row_of(z, q, y), k * TOUCHED
            rows[base : base + Y_ROWS, :] = block[at : at + Y_ROWS, :]
            owner = (z * NQ + q) * NY + y
            tail[owner : owner + 1, :] = block[at + Y_ROWS : at + TOUCHED, :]
    for z in range(NZ):
        for k in range(NQ * NY):
            q, y = k // NY, k % NY
            base, owner = row_of(z, q, y), z * NQ * NY + k
            if k + 1 < NQ * NY:
                rows[base + Y_ROWS : base + TOUCHED, :] += tail[owner : owner + 1, :]
            else:
                rows[base + Y_ROWS : base + TOUCHED, :] = tail[owner : owner + 1, :]

    def narrow(k, _):
        at = pl.ds(pl.multiple_of(k * 136, 8), 136)
        o_ref[at, :] = rows[at, :].astype(bf16)
        return _

    lax.fori_loop(0, ROWS // 136, narrow, 0)


def sent(x, axes):
    return lax.all_to_all(x, axes, 0, 0, tiled=True)


def shards(grads, master, velocity, layer_offsets, layer_sizes, lars_skip):
    shift = 2 * (NY * q_index() + y_index())
    tab = jnp.concatenate([layer_offsets, layer_sizes, lars_skip])

    def placed(a):
        flat = lax.dynamic_update_slice(jnp.zeros((SLOT * LANES,), f32), a, (shift,))
        return flat.reshape(SLOT, LANES)

    m, v = placed(master), placed(velocity)
    wide = grads.astype(f32).reshape(ROWS, LANES)
    wide, m, v, tab = lax.optimization_barrier((wide, m, v, tab))
    near, far, slot = (NEAR_ROWS, LANES), (SLOT, LANES), shape(SLOT, LANES)
    packed = call(pack_kernel, shape(N_NEAR, *near, dtype=bf16), [VMEM], [near])(wide)
    spread = call(spread_kernel, shape(N_FAR, *far), [VMEM], [near])(sent(packed, NEAR))
    shared, h = call(
        owner_kernel, (shape(N_FAR, 2 * SLOT, LANES), slot), [SMEM] + [VMEM] * 3
    )(tab, sent(spread, FAR), m, v)
    shared = sent(shared, FAR)
    norms = call(group_kernel, shape(N_NEAR, 1, LANES), [VMEM])(shared)
    w, new_master, new_velocity = call(
        update_kernel,
        (shape(NL * NX * NL, *near, dtype=bf16), slot, slot),
        [SMEM] + [VMEM] * 5,
        [near, (SLOT + 8, LANES)],
    )(tab, sent(norms, NEAR), shared, h, m, v)
    w = sent(w, ("zl", "x", "yl"))
    other = lax.ppermute(w, "c", [(0, 1), (1, 0)])
    weights = call(
        lay_out_kernel,
        shape(ROWS, LANES, dtype=bf16),
        [VMEM, VMEM],
        [near, (N_NEAR * N_FAR, LANES), (ROWS, LANES)],
    )(w, other)
    return (
        weights.reshape(ROWS * LANES),
        new_master.reshape(SLOT * LANES)[:SHARD],
        new_velocity.reshape(SLOT * LANES)[:SHARD],
    )


def solution(mesh):
    finer = Mesh(mesh.devices.reshape(NH, NL, NX, NC, NH, NL), AXES)
    owned = P(AXES)
    in_specs = (P(("zh", "zl", "x", "c"), ("yh", "yl"), None), owned, owned, P(), P(), P())
    return jax.shard_map(
        shards, mesh=finer, in_specs=in_specs, out_specs=(P(), owned, owned), check_vma=False
    )
```

time: 139 us -> 122 us (0.88)
  blocking collectives: 116 us -> 102 us
  starting transfers between devices: 5.81 us -> 4.27 us
    all_gather x1 -> x0, blocking collectives: 10.9 us -> none  [shards(): w = lax.all_gather(w, 'x')]
    all_to_all x4 -> x5, blocking collectives: 105 us -> 102 us  [sent(): return lax.all_to_all(x, axes, 0, 0, tiled=True)]
    ppermute x1, starting transfers between devices: 5.81 us -> 4.27 us  [shards(): other = lax.ppermute(w, 'c', [(0, 1), (1, 0)])]
where the time goes in v4:
time: 122 us; the launch traced here: 121 us
  blocking collectives  102 us (84%)
  other arithmetic  6.28 us (5%)
  Pallas kernels  5.46 us (4%)
  starting transfers between devices  4.27 us (3%)
  waiting for transfers between devices  2.08 us (2%)
    all_to_all x5, blocking collectives, sent(): return lax.all_to_all(x, axes, 0, 0, tiled=True)  102 us
    reshape x1, other arithmetic, shards(): wide = grads.astype(f32).reshape(ROWS, LANES)  6.2 us
    ppermute x1, starting transfers between devices, shards(): other = lax.ppermute(w, 'c', [(0, 1), (1, 0)])  4.27 us
    pallas_call x1, Pallas kernels, shards(): call(lay_out_kernel, shape(ROWS, LANES, dtype=bf16), [VMEM, VMEM], [near,...  2.51 us
  transfers between devices with their start and end apart: 1, of which 1 were waited for; matrix products, arithmetic and copies ran while one was open for 0% of the time, Pallas kernels for 0%

profile of v4, /device:TPU:1, one launch (start us, length us, event | category | flops | bytes accessed | tf_op | source)
XLA Modules:
  0.0 121.3 jit_solution(12920826800365320765)
XLA Ops:
  0.6 0.0 copy-start
  0.7 0.0 copy-start.1
  0.7 0.0 copy-start.2
  0.7 0.0 copy-start.3
  0.7 0.0 copy-start.4
  0.7 6.2 %reshape.34 = f32[1,1,852992]{2,1,0:T(1,128)S(1)} convert(bf16[1,1,852992]{2,1,0:T(2,128)(2,1)} %param.6) | non-fusion elementwise | flops 852992 | bytes 5117952 | tf_op jit(solution)/shard_map/reshape | solution.py:223
  6.9 0.0 copy-done
  6.9 0.3 dynamic_update_slice.6
  7.2 0.0 copy-done.1
  7.2 0.3 dynamic_update_slice.7
  7.5 0.0 copy-done.2
  7.5 0.0 copy-done.3
  7.5 0.0 copy-done.4
  7.5 0.1 pad_add_fusion.tab_ref
  7.6 0.5 shard_map.85
  8.1 34.2 %all_to_all.25.r_ref = bf16[32,224,128]{2,1,0:T(8,128)(2,1)S(1)} all-to-all(bf16[32,224,128]{2,1,0:T(8,128)(2,1)S(1)} %shard_map.85), channel_id=1, replica_groups=mesh['zh'=4,'zl'=2,'x'=4,'c'=2,'yh'=4,'yl'=2] {'zl','x','c','yl'}, dimensions={0} | all-to-all | bytes 3670016 | tf_op jit(solution)/shard_map/all_to_all | solution.py:211
  42.3 0.3 shard_map.86
  42.6 23.8 %all_to_all.26.r_ref = f32[16,16,128]{2,1,0:T(8,128)S(1)} all-to-all(f32[16,16,128]{2,1,0:T(8,128)S(1)} %shard_map.86), channel_id=1, replica_groups=mesh['zh'=4,'zl'=2,'x'=4,'c'=2,'yh'=4,'yl'=2] {'zh','yh'}, dimensions={0} | all-to-all | bytes 262144 | tf_op jit(solution)/shard_map/all_to_all | solution.py:211
  66.4 0.7 shard_map.87
  67.1 14.7 %all_to_all.27.s_ref = f32[16,32,128]{2,1,0:T(8,128)S(1)} all-to-all(f32[16,32,128]{2,1,0:T(8,128)S(1)} %get-tuple-element.16), channel_id=1, replica_groups=mesh['zh'=4,'zl'=2,'x'=4,'c'=2,'yh'=4,'yl'=2] {'zh','yh'}, dimensions={0} | all-to-all | bytes 524288 | tf_op jit(solution)/shard_map/all_to_all | solution.py:211
  81.8 13.7 %all_to_all.28.n_ref = f32[32,1,128]{2,1,0:T(1,128)S(1)} all-to-all(f32[32,1,128]{2,1,0:T(1,128)S(1)} %shard_map.88), channel_id=1, replica_groups=mesh['zh'=4,'zl'=2,'x'=4,'c'=2,'yh'=4,'yl'=2] {'zl','x','c','yl'}, dimensions={0} | all-to-all | bytes 32768 | tf_op jit(solution)/shard_map/all_to_all | solution.py:211
  95.6 1.5 %shard_map.89 = (bf16[16,224,128]{2,1,0:T(8,128)(2,1)S(1)}, f32[16,128]{1,0:T(8,128)}, f32[16,128]{1,0:T(8,128)}) custom-call(s32[18]{0:T(128)S(1)} %pad_add_fusion.tab_ref, f32[32,1,128]{2,1,0:T(1,128)S(1)} %all_to_all.28.n_ref, f32[16,32,128]{2,1,0:T(8,128)S(1)} %all_to_all.27.s_ref, f32[16,128]{1,0:T(8,128)S(1)} %get-tuple-element.17.h_ref, ...), custom_call_target="tpu_custom_call" | custom-call | tf_op jit(solution)/shard_map/pallas_call | solution.py:233
  97.0 15.4 %all_to_all.29.a_ref = bf16[16,224,128]{2,1,0:T(8,128)(2,1)S(1)} all-to-all(bf16[16,224,128]{2,1,0:T(8,128)(2,1)S(1)} %get-tuple-element.18), channel_id=1, replica_groups=mesh['zh'=4,'zl'=2,'x'=4,'c'=2,'yh'=4,'yl'=2] {'zl','x','yl'}, dimensions={0} | all-to-all | bytes 1835008 | tf_op jit(solution)/shard_map/all_to_all | solution.py:211
  112.4 4.3 %collective-permute-start = (bf16[16,224,128]{2,1,0:T(8,128)(2,1)S(1)}, bf16[16,224,128]{2,1,0:T(8,128)(2,1)S(1)}, u32[]{:S(2)}, u32[]{:S(2)}) collective-permute-start(bf16[16,224,128]{2,1,0:T(8,128)(2,1)S(1)} %all_to_all.29.a_ref), channel_id=1, source_target_pairs={{0,8},{8,0},{1,9},{9,1},{2,10},{10,2},{3,11},{11,3},{4,12},{12,4},... | collective-permute-start | bytes 2752520 | tf_op jit(solution)/shard_map/ppermute | solution.py:240
  116.7 2.1 %collective-permute-done.b_ref = bf16[16,224,128]{2,1,0:T(8,128)(2,1)S(1)} collective-permute-done((bf16[16,224,128]{2,1,0:T(8,128)(2,1)S(1)}, bf16[16,224,128]{2,1,0:T(8,128)(2,1)S(1)}, u32[]{:S(2)}, u32[]{:S(2)}) %collective-permute-start) | collective-permute-done | bytes 917536 | tf_op jit(solution)/shard_map/ppermute | solution.py:240
  118.8 2.5 %shard_map.90 = bf16[6664,128]{1,0:T(8,128)(2,1)} custom-call(bf16[16,224,128]{2,1,0:T(8,128)(2,1)S(1)} %all_to_all.29.a_ref, bf16[16,224,128]{2,1,0:T(8,128)(2,1)S(1)} %collective-permute-done.b_ref), custom_call_target="tpu_custom_call" | custom-call | tf_op jit(solution)/shard_map/pallas_call | solution.py:241
  (3 shorter events, 0.0 us)
Async XLA Ops:
  0.6 6.3 %copy-start = (f32[1666]{0:T(1024)S(1)}, f32[1666]{0:T(1024)}, u32[]{:S(2)}) copy-start(f32[1666]{0:T(1024)} %param.7) | copy-start | bytes 19996
  0.7 6.6 %copy-start.1 = (f32[1666]{0:T(1024)S(1)}, f32[1666]{0:T(1024)}, u32[]{:S(2)}) copy-start(f32[1666]{0:T(1024)} %param.8) | copy-start | bytes 19996
  0.7 6.9 %copy-start.2 = (s32[6]{0:T(128)S(1)}, s32[6]{0:T(128)}, u32[]{:S(2)}) copy-start(s32[6]{0:T(128)} %param.11) | copy-start | bytes 76
  0.7 6.8 %copy-start.3 = (s32[6]{0:T(128)S(1)}, s32[6]{0:T(128)}, u32[]{:S(2)}) copy-start(s32[6]{0:T(128)} %param.10) | copy-start | bytes 76
  0.7 6.8 %copy-start.4 = (s32[6]{0:T(128)S(1)}, s32[6]{0:T(128)}, u32[]{:S(2)}) copy-start(s32[6]{0:T(128)} %param.9) | copy-start | bytes 76
  112.4 6.4 %collective-permute-start = (bf16[16,224,128]{2,1,0:T(8,128)(2,1)S(1)}, bf16[16,224,128]{2,1,0:T(8,128)(2,1)S(1)}, u32[]{:S(2)}, u32[]{:S(2)}) collective-permute-start(bf16[16,224,128]{2,1,0:T(8,128)(2,1)S(1)} %all_to_all.29.a_ref), channel_id=1, source_target_pairs={{0,8},{8,0},{1,9},{9,1},{2,10},{10,2},{3,11},{11,3},{4,12},{12,4},... | collective-permute-start | bytes 2752520 | tf_op jit(solution)/shard_map/ppermute | solution.py:240

commit v5 on v4

--- a/solution.py
+++ b/solution.py
@@ -23,6 +23,9 @@
 SLOT = 16
 NEAR_ROWS = N_FAR * TOUCHED
 LAYERS = 6
+STEPS = 7
+STEP_ROWS = ROWS // STEPS
+CHUNK = 136
 f32 = jnp.float32
 bf16 = jnp.bfloat16
 VMEM = pl.BlockSpec(memory_space=pltpu.VMEM)
@@ -66,13 +69,44 @@
     return [(k, k // NH, k % NH) for k in range(N_FAR)]
 
 
-def pack_kernel(x_ref, o_ref, rows):
+def pack_kernel(x_ref, o_ref, held, sems, wide, rows):
+    copies = []
+    for i in range(STEPS):
+        at = pl.ds(i * STEP_ROWS, STEP_ROWS)
+        copies.append(pltpu.make_async_copy(x_ref.at[at], held.at[at], sems.at[i]))
+        copies[-1].start()
+    for i in range(STEPS):
+        copies[i].wait()
+
+        def widen(k, _):
+            at = i * STEP_ROWS + k * CHUNK
+            for r in range(CHUNK):
+                wide[pl.ds(at + r, 1), :] = held[at + r].astype(f32)
+            return _
+
+        lax.fori_loop(0, STEP_ROWS // CHUNK, widen, 0)
     for near in range(N_NEAR):
         zl, q, yl = near // (NQ * NL), near // NL % NQ, near % NL
         for k, zh, yh in far_slots():
             base = row_of(zh * NL + zl, q, yh * NL + yl)
-            rows[k * TOUCHED : (k + 1) * TOUCHED, :] = x_ref[base : base + TOUCHED, :]
+            rows[k * TOUCHED : (k + 1) * TOUCHED, :] = wide[base : base + TOUCHED, :]
         o_ref[near] = rows[...].astype(bf16)
+
+
+def packed(grads):
+    return pl.pallas_call(
+        pack_kernel,
+        out_shape=shape(N_NEAR, NEAR_ROWS, LANES, dtype=bf16),
+        in_specs=[pl.BlockSpec(memory_space=pl.ANY)],
+        out_specs=VMEM,
+        scratch_shapes=[
+            pltpu.VMEM((ROWS, 1, LANES), bf16),
+            pltpu.SemaphoreType.DMA((STEPS,)),
+            pltpu.VMEM((ROWS, LANES), f32),
+            pltpu.VMEM((NEAR_ROWS, LANES), f32),
+        ],
+        compiler_params=pltpu.CompilerParams(vmem_limit_bytes=51 * 1024 * 1024),
+    )(grads.reshape(ROWS, 1, LANES))
 
 
 def spread_kernel(r_ref, o_ref, rows):
@@ -136,39 +170,46 @@
     n_ref[...] = jnp.broadcast_to(total[None], n_ref.shape)
 
 
-def update_kernel(tab_ref, n_ref, s_ref, h_ref, m_ref, v_ref, w_ref, om_ref, ov_ref, rows, turn):
+def trust_at(tab_ref, trust, pos):
+    lane = lax.broadcasted_iota(jnp.int32, (1, LANES), 1)
+    out = jnp.zeros(pos[0].shape, f32)
+    outs = [out] * len(pos)
+    for l in range(LAYERS):
+        one = jnp.sum(jnp.where(lane == l, trust, 0.0), axis=1, keepdims=True)
+        outs = [jnp.where(in_layer(tab_ref, l, p), one, o) for p, o in zip(pos, outs)]
+    return outs
+
+
+def update_kernel(tab_ref, n_ref, s_ref, w_ref, t_ref, rows):
     norms = jnp.sum(n_ref[...], axis=0)
-    lane1 = lax.broadcasted_iota(jnp.int32, (1, LANES), 1)
-    trusts = []
+    lane = lax.broadcasted_iota(jnp.int32, (1, LANES), 1)
+    skip = jnp.zeros((1, LANES), f32)
     for l in range(LAYERS):
-        wsq = jnp.sum(jnp.where(lane1 == l, norms, 0.0), axis=1, keepdims=True)
-        gsq = jnp.sum(jnp.where(lane1 == 8 + l, norms, 0.0), axis=1, keepdims=True)
-        wnorm, gnorm = jnp.sqrt(wsq), jnp.sqrt(gsq)
-        skip = skipped(tab_ref, l)
-        ratio = 0.02 * wnorm / (gnorm + 0.001 * wnorm + 1e-06)
-        trusts.append(skip + (1.0 - skip) * ratio)
-
-    def trust_at(pos):
-        trust = jnp.zeros(pos.shape, f32)
-        for l in range(LAYERS):
-            trust = jnp.where(in_layer(tab_ref, l, pos), trusts[l], trust)
-        return trust
-
-    q = q_index()
+        skip = jnp.where(lane == l, skipped(tab_ref, l), skip)
+    wnorm = jnp.sqrt(norms)
+    gnorm = pltpu.roll(wnorm, LANES - 8, 1)
+    ratio = 0.02 * wnorm / (gnorm + 0.001 * wnorm + 1e-06)
+    trust = skip + (1.0 - skip) * ratio
+    t_ref[...] = trust
     at = lax.broadcasted_iota(jnp.int32, (SLOT, LANES), 0) * LANES
     at = at + lax.broadcasted_iota(jnp.int32, (SLOT, LANES), 1)
-    for k, zh, yh in far_slots():
-        z, y = zh * NL + lax.axis_index("zl"), yh * NL + lax.axis_index("yl")
-        pos = at + row_of(z, q, y) * LANES
-        w = s_ref[k, SLOT:, :] - 8.0 * trust_at(pos) * s_ref[k, :SLOT, :]
+    pos = [
+        at + row_of(zh * NL + lax.axis_index("zl"), q_index(), yh * NL + lax.axis_index("yl")) * LANES
+        for _, zh, yh in far_slots()
+    ]
+    for k, t in enumerate(trust_at(tab_ref, trust, pos)):
+        w = s_ref[k, SLOT:, :] - 8.0 * t * s_ref[k, :SLOT, :]
         rows[k * TOUCHED : (k + 1) * TOUCHED, :] = w[:TOUCHED, :]
     w = rows[...].astype(bf16)
     for k in range(NL * NX * NL):
         w_ref[k] = w
 
-    shift = 2 * (NY * q + y_index())
+
+def own_kernel(tab_ref, t_ref, h_ref, m_ref, v_ref, om_ref, ov_ref, turn):
+    shift = 2 * (NY * q_index() + y_index())
     pos, _ = slot_positions()
-    new_v = 0.9 * v_ref[...] + 8.0 * trust_at(pos) * h_ref[...]
+    (trust,) = trust_at(tab_ref, t_ref[...], [pos])
+    new_v = 0.9 * v_ref[...] + 8.0 * trust * h_ref[...]
     new_m = m_ref[...] - new_v
     lane = lax.broadcasted_iota(jnp.int32, (SLOT, LANES), 1)
     for own, out in ((new_m, om_ref), (new_v, ov_ref)):
@@ -178,22 +219,28 @@
         out[...] = jnp.where(lane < LANES - shift, turned, turn[1 : SLOT + 1, :])
 
 
-def lay_out_kernel(a_ref, b_ref, o_ref, block, tail, rows):
-    c = lax.axis_index("c")
-    for near in range(N_NEAR):
-        zl, q, yl = near // (NQ * NL), near // NL % NQ, near % NL
-        cc, peer = q % NC, (zl * NX + q // NC) * NL + yl
-        block[...] = jnp.where(c == cc, a_ref[peer].astype(f32), b_ref[peer].astype(f32))
+def put_core(w_ref, c, block, rows, tail):
+    for peer in range(NL * NX * NL):
+        zl, x, yl = peer // (NX * NL), peer // NL % NX, peer % NL
+        block[...] = w_ref[peer].astype(f32)
         for k, zh, yh in far_slots():
             z, y = zh * NL + zl, yh * NL + yl
-            base, at = row_of(z, q, y), k * TOUCHED
-            rows[base : base + Y_ROWS, :] = block[at : at + Y_ROWS, :]
+            at, q = k * TOUCHED, x * NC
             owner = (z * NQ + q) * NY + y
-            tail[owner : owner + 1, :] = block[at + Y_ROWS : at + TOUCHED, :]
+            base = row_of(z, q, y) + c * Q_ROWS
+            rows[pl.ds(base, Y_ROWS), :] = block[at : at + Y_ROWS, :]
+            tail[pl.ds(owner + c * NY, 1), :] = block[at + Y_ROWS : at + TOUCHED, :]
+
+
+def own_half_kernel(w_ref, rows, tail, block):
+    put_core(w_ref, lax.axis_index("c"), block, rows, tail)
+
+
+def lay_out_kernel(w_ref, rows, tail, o_ref, block):
+    put_core(w_ref, 1 - lax.axis_index("c"), block, rows, tail)
     for z in range(NZ):
         for k in range(NQ * NY):
-            q, y = k // NY, k % NY
-            base, owner = row_of(z, q, y), z * NQ * NY + k
+            base, owner = row_of(z, k // NY, k % NY), z * NQ * NY + k
             if k + 1 < NQ * NY:
                 rows[base + Y_ROWS : base + TOUCHED, :] += tail[owner : owner + 1, :]
             else:
@@ -220,30 +267,43 @@
         return flat.reshape(SLOT, LANES)
 
     m, v = placed(master), placed(velocity)
-    wide = grads.astype(f32).reshape(ROWS, LANES)
-    wide, m, v, tab = lax.optimization_barrier((wide, m, v, tab))
     near, far, slot = (NEAR_ROWS, LANES), (SLOT, LANES), shape(SLOT, LANES)
-    packed = call(pack_kernel, shape(N_NEAR, *near, dtype=bf16), [VMEM], [near])(wide)
-    spread = call(spread_kernel, shape(N_FAR, *far), [VMEM], [near])(sent(packed, NEAR))
+    sending, m, v, tab = lax.optimization_barrier((packed(grads), m, v, tab))
+    spread = call(spread_kernel, shape(N_FAR, *far), [VMEM], [near])(sent(sending, NEAR))
     shared, h = call(
         owner_kernel, (shape(N_FAR, 2 * SLOT, LANES), slot), [SMEM] + [VMEM] * 3
     )(tab, sent(spread, FAR), m, v)
     shared = sent(shared, FAR)
     norms = call(group_kernel, shape(N_NEAR, 1, LANES), [VMEM])(shared)
-    w, new_master, new_velocity = call(
+    w, trust = call(
         update_kernel,
-        (shape(NL * NX * NL, *near, dtype=bf16), slot, slot),
-        [SMEM] + [VMEM] * 5,
-        [near, (SLOT + 8, LANES)],
-    )(tab, sent(norms, NEAR), shared, h, m, v)
+        (shape(NL * NX * NL, *near, dtype=bf16), shape(1, LANES)),
+        [SMEM, VMEM, VMEM],
+        [near],
+    )(tab, sent(norms, NEAR), shared)
     w = sent(w, ("zl", "x", "yl"))
     other = lax.ppermute(w, "c", [(0, 1), (1, 0)])
-    weights = call(
-        lay_out_kernel,
-        shape(ROWS, LANES, dtype=bf16),
-        [VMEM, VMEM],
-        [near, (N_NEAR * N_FAR, LANES), (ROWS, LANES)],
-    )(w, other)
+    rows, tail = call(
+        own_half_kernel, (shape(ROWS, LANES), shape(N_NEAR * N_FAR, LANES)), [VMEM], [near]
+    )(w)
+    new_master, new_velocity = call(
+        own_kernel, (slot, slot), [SMEM] + [VMEM] * 4, [(SLOT + 8, LANES)]
+    )(tab, trust, h, m, v)
+    _, _, weights = pl.pallas_call(
+        lambda w_ref, r_in, t_in, rows, tail, o_ref, block: lay_out_kernel(
+            w_ref, rows, tail, o_ref, block
+        ),
+        out_shape=(
+            shape(ROWS, LANES),
+            shape(N_NEAR * N_FAR, LANES),
+            shape(ROWS, LANES, dtype=bf16),
+        ),
+        in_specs=[VMEM] * 3,
+        out_specs=(VMEM,) * 3,
+        input_output_aliases={1: 0, 2: 1},
+        scratch_shapes=[pltpu.VMEM(near, f32)],
+        compiler_params=PARAMS,
+    )(other, rows, tail)
     return (
         weights.reshape(ROWS * LANES),
         new_master.reshape(SLOT * LANES)[:SHARD],

time: 122 us -> 118 us (0.967)
  other arithmetic: 6.28 us -> 0.08 us
  Pallas kernels: 5.46 us -> 9.94 us
  waiting for transfers between devices: 2.08 us -> 0.38 us
    reshape x1 -> x0, other arithmetic: 6.2 us -> none  [shards(): wide = grads.astype(f32).reshape(ROWS, LANES)]
    pallas_call x4 -> x6, Pallas kernels: 4.76 us -> 9.24 us  [the longest x1 4.11 us: packed(): pl.pallas_call(pack_kernel, out_shape=shape(N_NEAR, NEAR_ROWS, LANES, dty...]
    ppermute x1, waiting for transfers between devices: 2.08 us -> 0.38 us  [shards(): other = lax.ppermute(w, 'c', [(0, 1), (1, 0)])]
  transfers between devices with their start and end apart: 1 -> 1, of which waited for: 1 -> 1; matrix products, arithmetic and copies ran while one was open for 0% -> 0% of each run, Pallas kernels for 0% -> 1%
where the time goes in v5:
time: 118 us
  blocking collectives  102 us (86%)
  Pallas kernels  9.94 us (8%)
  starting transfers between devices  4.27 us (4%)
    all_to_all x5, blocking collectives, sent(): return lax.all_to_all(x, axes, 0, 0, tiled=True)  102 us
    ppermute x1, starting transfers between devices, shards(): other = lax.ppermute(w, 'c', [(0, 1), (1, 0)])  4.27 us
    pallas_call x1, Pallas kernels, packed(): pl.pallas_call(pack_kernel, out_shape=shape(N_NEAR, NEAR_ROWS, LANES, dty...  4.11 us
  transfers between devices with their start and end apart: 1, of which 1 were waited for; matrix products, arithmetic and copies ran while one was open for 0% of the time, Pallas kernels for 1%

profile of v5, /device:TPU:1, one launch (start us, length us, event | category | flops | bytes accessed | tf_op | source)
XLA Modules:
  0.0 117.9 jit_solution(4663316666199182550)
XLA Ops:
  0.6 0.0 copy-start
  0.6 0.0 copy-start.1
  0.7 0.0 copy-start.2
  0.7 0.0 copy-start.3
  0.7 0.0 copy-start.4
  0.7 4.1 %shard_map.85 = bf16[32,224,128]{2,1,0:T(8,128)(2,1)S(1)} custom-call(bf16[6664,1,128]{2,1,0:T(2,128)(2,1)} %bitcast.12), custom_call_target="tpu_custom_call" | custom-call | tf_op jit(solution)/shard_map/pallas_call | solution.py:97
  4.8 0.0 copy-done
  4.8 0.3 dynamic_update_slice.6
  5.1 0.0 copy-done.1
  5.1 0.3 dynamic_update_slice.7
  5.4 0.0 copy-done.2
  5.4 0.0 copy-done.3
  5.4 0.0 copy-done.4
  5.4 0.1 pad_add_fusion.tab_ref
  5.5 34.2 %all_to_all.25.r_ref = bf16[32,224,128]{2,1,0:T(8,128)(2,1)S(1)} all-to-all(bf16[32,224,128]{2,1,0:T(8,128)(2,1)S(1)} %shard_map.85), channel_id=1, replica_groups=mesh['zh'=4,'zl'=2,'x'=4,'c'=2,'yh'=4,'yl'=2] {'zl','x','c','yl'}, dimensions={0} | all-to-all | bytes 3670016 | tf_op jit(solution)/shard_map/all_to_all | solution.py:258
  39.7 0.3 shard_map.86
  40.0 23.8 %all_to_all.26.r_ref = f32[16,16,128]{2,1,0:T(8,128)S(1)} all-to-all(f32[16,16,128]{2,1,0:T(8,128)S(1)} %shard_map.86), channel_id=1, replica_groups=mesh['zh'=4,'zl'=2,'x'=4,'c'=2,'yh'=4,'yl'=2] {'zh','yh'}, dimensions={0} | all-to-all | bytes 262144 | tf_op jit(solution)/shard_map/all_to_all | solution.py:258
  63.8 0.7 shard_map.87
  64.5 14.7 %all_to_all.27.s_ref = f32[16,32,128]{2,1,0:T(8,128)S(1)} all-to-all(f32[16,32,128]{2,1,0:T(8,128)S(1)} %get-tuple-element.20), channel_id=1, replica_groups=mesh['zh'=4,'zl'=2,'x'=4,'c'=2,'yh'=4,'yl'=2] {'zh','yh'}, dimensions={0} | all-to-all | bytes 524288 | tf_op jit(solution)/shard_map/all_to_all | solution.py:258
  79.2 13.7 %all_to_all.28.n_ref = f32[32,1,128]{2,1,0:T(1,128)S(1)} all-to-all(f32[32,1,128]{2,1,0:T(1,128)S(1)} %shard_map.88), channel_id=1, replica_groups=mesh['zh'=4,'zl'=2,'x'=4,'c'=2,'yh'=4,'yl'=2] {'zl','x','c','yl'}, dimensions={0} | all-to-all | bytes 32768 | tf_op jit(solution)/shard_map/all_to_all | solution.py:258
  93.0 0.9 shard_map.89
  93.9 15.4 %all_to_all.29.w_ref = bf16[16,224,128]{2,1,0:T(8,128)(2,1)S(1)} all-to-all(bf16[16,224,128]{2,1,0:T(8,128)(2,1)S(1)} %get-tuple-element.21), channel_id=1, replica_groups=mesh['zh'=4,'zl'=2,'x'=4,'c'=2,'yh'=4,'yl'=2] {'zl','x','yl'}, dimensions={0} | all-to-all | bytes 1835008 | tf_op jit(solution)/shard_map/all_to_all | solution.py:258
  109.3 4.3 %collective-permute-start = (bf16[16,224,128]{2,1,0:T(8,128)(2,1)S(1)}, bf16[16,224,128]{2,1,0:T(8,128)(2,1)S(1)}, u32[]{:S(2)}, u32[]{:S(2)}) collective-permute-start(bf16[16,224,128]{2,1,0:T(8,128)(2,1)S(1)} %all_to_all.29.w_ref), channel_id=1, source_target_pairs={{0,8},{8,0},{1,9},{9,1},{2,10},{10,2},{3,11},{11,3},{4,12},{12,4},... | collective-permute-start | bytes 2752520 | tf_op jit(solution)/shard_map/ppermute | solution.py:285
  113.6 1.3 %shard_map.92 = (f32[16,128]{1,0:T(8,128)}, f32[16,128]{1,0:T(8,128)}) custom-call(s32[18]{0:T(128)S(1)} %pad_add_fusion.tab_ref, f32[1,128]{1,0:T(1,128)S(1)} %get-tuple-element.25.t_ref, f32[16,128]{1,0:T(8,128)S(1)} %get-tuple-element.26.h_ref, f32[16,128]{1,0:T(8,128)S(1)} %bitcast.11, f32[16,128]{1,0:T(8,128)S(1)} %bitcast.9), custom_call_target="tpu_custom_call" | custom-call | tf_op jit(solution)/shard_map/pallas_call | solution.py:289
  114.9 0.4 shard_map.90
  115.3 0.4 collective-permute-done.w_ref
  115.6 2.2 %shard_map.91 = (f32[6664,128]{1,0:T(8,128)S(1)}, f32[512,128]{1,0:T(8,128)S(1)}, bf16[6664,128]{1,0:T(8,128)(2,1)}) custom-call(bf16[16,224,128]{2,1,0:T(8,128)(2,1)S(1)} %collective-permute-done.w_ref, f32[6664,128]{1,0:T(8,128)S(1)} %get-tuple-element.22.r_in, f32[512,128]{1,0:T(8,128)S(1)} %get-tuple-element.23.t_in), custom_call_target="tpu_custom_call", output_to_operand_aliasing={{0}: (1, {}), {1}: (2, {})} | custom-call | tf_op jit(solution)/shard_map/pallas_call | solution.py:292
  (3 shorter events, 0.0 us)
Async XLA Ops:
  0.6 4.2 %copy-start = (f32[1666]{0:T(1024)S(1)}, f32[1666]{0:T(1024)}, u32[]{:S(2)}) copy-start(f32[1666]{0:T(1024)} %param.7) | copy-start | bytes 19996
  0.6 4.5 %copy-start.1 = (f32[1666]{0:T(1024)S(1)}, f32[1666]{0:T(1024)}, u32[]{:S(2)}) copy-start(f32[1666]{0:T(1024)} %param.8) | copy-start | bytes 19996
  0.7 4.8 %copy-start.2 = (s32[6]{0:T(128)S(1)}, s32[6]{0:T(128)}, u32[]{:S(2)}) copy-start(s32[6]{0:T(128)} %param.11) | copy-start | bytes 76
  0.7 4.8 %copy-start.3 = (s32[6]{0:T(128)S(1)}, s32[6]{0:T(128)}, u32[]{:S(2)}) copy-start(s32[6]{0:T(128)} %param.10) | copy-start | bytes 76
  0.7 4.8 %copy-start.4 = (s32[6]{0:T(128)S(1)}, s32[6]{0:T(128)}, u32[]{:S(2)}) copy-start(s32[6]{0:T(128)} %param.9) | copy-start | bytes 76
  109.3 6.4 %collective-permute-start = (bf16[16,224,128]{2,1,0:T(8,128)(2,1)S(1)}, bf16[16,224,128]{2,1,0:T(8,128)(2,1)S(1)}, u32[]{:S(2)}, u32[]{:S(2)}) collective-permute-start(bf16[16,224,128]{2,1,0:T(8,128)(2,1)S(1)} %all_to_all.29.w_ref), channel_id=1, source_target_pairs={{0,8},{8,0},{1,9},{9,1},{2,10},{10,2},{3,11},{11,3},{4,12},{12,4},... | collective-permute-start | bytes 2752520 | tf_op jit(solution)/shard_map/ppermute | solution.py:285

commit v6 on v5

--- a/solution.py
+++ b/solution.py
@@ -137,7 +137,22 @@
     return tab_ref[2 * LAYERS + l].astype(f32)
 
 
-def owner_kernel(tab_ref, r_ref, m_ref, v_ref, o_ref, h_ref):
+def placed(flat_ref, rows):
+    whole = SHARD // LANES
+    rows[...] = jnp.zeros((SLOT + 8, LANES), f32)
+    for k in range(whole):
+        rows[8 + k, :] = flat_ref[pl.ds(k * LANES, LANES)]
+    rows[8 + whole, pl.ds(0, SHARD - whole * LANES)] = flat_ref[pl.ds(whole * LANES, SHARD - whole * LANES)]
+    shift = 2 * (NY * q_index() + y_index())
+    lane = lax.broadcasted_iota(jnp.int32, (SLOT, LANES), 1)
+    here = pltpu.roll(rows[8:, :], shift, 1)
+    above = pltpu.roll(rows[7 : SLOT + 7, :], shift, 1)
+    return jnp.where(lane >= shift, here, above)
+
+
+def owner_kernel(tab_ref, r_ref, mf_ref, vf_ref, o_ref, h_ref, m_ref, v_ref, rows):
+    m_ref[...] = placed(mf_ref, rows)
+    v_ref[...] = placed(vf_ref, rows)
     g = r_ref[0]
     for k in range(1, N_FAR):
         g = g + r_ref[k]
@@ -219,39 +234,49 @@
         out[...] = jnp.where(lane < LANES - shift, turned, turn[1 : SLOT + 1, :])
 
 
-def put_core(w_ref, c, block, rows, tail):
-    for peer in range(NL * NX * NL):
-        zl, x, yl = peer // (NX * NL), peer // NL % NX, peer % NL
-        block[...] = w_ref[peer].astype(f32)
-        for k, zh, yh in far_slots():
-            z, y = zh * NL + zl, yh * NL + yl
-            at, q = k * TOUCHED, x * NC
-            owner = (z * NQ + q) * NY + y
-            base = row_of(z, q, y) + c * Q_ROWS
-            rows[pl.ds(base, Y_ROWS), :] = block[at : at + Y_ROWS, :]
-            tail[pl.ds(owner + c * NY, 1), :] = block[at + Y_ROWS : at + TOUCHED, :]
+def put_core(w_ref, c, z, block, rows, tail):
+    zh, zl = z // NL, z % NL
+    part = NH * TOUCHED
+    for x in range(NX):
+        for yl in range(NL):
+            peer = (zl * NX + x) * NL + yl
+            block[yl * part : (yl + 1) * part, :] = w_ref[peer, zh * part : (zh + 1) * part, :].astype(f32)
+        before = None
+        for y in range(NY):
+            at = (y % NL) * part + y // NL * TOUCHED
+            base = row_of(z, x * NC, y) + c * Q_ROWS
+            if before is None:
+                rows[pl.ds(base, Y_ROWS), :] = block[at : at + Y_ROWS, :]
+            else:
+                rows[pl.ds(base, 1), :] = block[at : at + 1, :] + block[before : before + 1, :]
+                rows[pl.ds(base + 1, Y_ROWS - 1), :] = block[at + 1 : at + Y_ROWS, :]
+            before = at + Y_ROWS
+        tail[pl.ds(z * NQ + x * NC + c, 1), :] = block[before : before + 1, :]
 
 
 def own_half_kernel(w_ref, rows, tail, block):
-    put_core(w_ref, lax.axis_index("c"), block, rows, tail)
-
-
-def lay_out_kernel(w_ref, rows, tail, o_ref, block):
-    put_core(w_ref, 1 - lax.axis_index("c"), block, rows, tail)
     for z in range(NZ):
-        for k in range(NQ * NY):
-            base, owner = row_of(z, k // NY, k % NY), z * NQ * NY + k
-            if k + 1 < NQ * NY:
-                rows[base + Y_ROWS : base + TOUCHED, :] += tail[owner : owner + 1, :]
+        put_core(w_ref, lax.axis_index("c"), z, block, rows, tail)
+
+
+def lay_out_kernel(w_ref, rows_in, tail_in, rows, tail, o_ref, block, narrow, sems):
+    copies = []
+    for z in range(NZ):
+        put_core(w_ref, 1 - lax.axis_index("c"), z, block, rows, tail)
+        for q in range(NQ):
+            last = row_of(z, q + 1, 0)
+            one = tail[z * NQ + q : z * NQ + q + 1, :]
+            if q + 1 < NQ:
+                rows[last : last + 1, :] += one
             else:
-                rows[base + Y_ROWS : base + TOUCHED, :] = tail[owner : owner + 1, :]
-
-    def narrow(k, _):
-        at = pl.ds(pl.multiple_of(k * 136, 8), 136)
-        o_ref[at, :] = rows[at, :].astype(bf16)
-        return _
-
-    lax.fori_loop(0, ROWS // 136, narrow, 0)
+                rows[last : last + 1, :] = one
+        start, stop = z * Z_ROWS // 8 * 8, (z + 1) * Z_ROWS // 8 * 8
+        narrow[start:stop, :] = rows[start:stop, :].astype(bf16)
+        at = pl.ds(start, stop - start)
+        copies.append(pltpu.make_async_copy(narrow.at[at], o_ref.at[at], sems.at[z]))
+        copies[-1].start()
+    for copy in copies:
+        copy.wait()
 
 
 def sent(x, axes):
@@ -259,20 +284,16 @@
 
 
 def shards(grads, master, velocity, layer_offsets, layer_sizes, lars_skip):
-    shift = 2 * (NY * q_index() + y_index())
     tab = jnp.concatenate([layer_offsets, layer_sizes, lars_skip])
-
-    def placed(a):
-        flat = lax.dynamic_update_slice(jnp.zeros((SLOT * LANES,), f32), a, (shift,))
-        return flat.reshape(SLOT, LANES)
-
-    m, v = placed(master), placed(velocity)
     near, far, slot = (NEAR_ROWS, LANES), (SLOT, LANES), shape(SLOT, LANES)
-    sending, m, v, tab = lax.optimization_barrier((packed(grads), m, v, tab))
+    sending, tab = lax.optimization_barrier((packed(grads), tab))
     spread = call(spread_kernel, shape(N_FAR, *far), [VMEM], [near])(sent(sending, NEAR))
-    shared, h = call(
-        owner_kernel, (shape(N_FAR, 2 * SLOT, LANES), slot), [SMEM] + [VMEM] * 3
-    )(tab, sent(spread, FAR), m, v)
+    shared, h, m, v = call(
+        owner_kernel,
+        (shape(N_FAR, 2 * SLOT, LANES), slot, slot, slot),
+        [SMEM] + [VMEM] * 3,
+        [(SLOT + 8, LANES)],
+    )(tab, sent(spread, FAR), master, velocity)
     shared = sent(shared, FAR)
     norms = call(group_kernel, shape(N_NEAR, 1, LANES), [VMEM])(shared)
     w, trust = call(
@@ -283,25 +304,23 @@
     )(tab, sent(norms, NEAR), shared)
     w = sent(w, ("zl", "x", "yl"))
     other = lax.ppermute(w, "c", [(0, 1), (1, 0)])
-    rows, tail = call(
-        own_half_kernel, (shape(ROWS, LANES), shape(N_NEAR * N_FAR, LANES)), [VMEM], [near]
-    )(w)
+    halves = (shape(ROWS, LANES), shape(NZ * NQ, LANES))
+    block = (NL * NH * TOUCHED, LANES)
+    rows, tail = call(own_half_kernel, halves, [VMEM], [block])(w)
     new_master, new_velocity = call(
         own_kernel, (slot, slot), [SMEM] + [VMEM] * 4, [(SLOT + 8, LANES)]
     )(tab, trust, h, m, v)
     _, _, weights = pl.pallas_call(
-        lambda w_ref, r_in, t_in, rows, tail, o_ref, block: lay_out_kernel(
-            w_ref, rows, tail, o_ref, block
-        ),
-        out_shape=(
-            shape(ROWS, LANES),
-            shape(N_NEAR * N_FAR, LANES),
-            shape(ROWS, LANES, dtype=bf16),
-        ),
+        lay_out_kernel,
+        out_shape=(*halves, shape(ROWS, LANES, dtype=bf16)),
         in_specs=[VMEM] * 3,
-        out_specs=(VMEM,) * 3,
+        out_specs=(VMEM, VMEM, pl.BlockSpec(memory_space=pl.ANY)),
         input_output_aliases={1: 0, 2: 1},
-        scratch_shapes=[pltpu.VMEM(near, f32)],
+        scratch_shapes=[
+            pltpu.VMEM(block, f32),
+            pltpu.VMEM((ROWS, LANES), bf16),
+            pltpu.SemaphoreType.DMA((NZ,)),
+        ],
         compiler_params=PARAMS,
     )(other, rows, tail)
     return (

time: 118 us -> 117 us (level)
  no operation moved by 1% of the time
where the time goes in v6:
time: 117 us
  blocking collectives  102 us (87%)
  Pallas kernels  9.24 us (8%)
  starting transfers between devices  4.27 us (4%)
    all_to_all x5, blocking collectives, sent(): return lax.all_to_all(x, axes, 0, 0, tiled=True)  102 us
    ppermute x1, starting transfers between devices, shards(): other = lax.ppermute(w, 'c', [(0, 1), (1, 0)])  4.27 us
    pallas_call x1, Pallas kernels, packed(): pl.pallas_call(pack_kernel, out_shape=shape(N_NEAR, NEAR_ROWS, LANES, dty...  4.11 us
  transfers between devices with their start and end apart: 1, of which 1 were waited for; matrix products, arithmetic and copies ran while one was open for 0% of the time, Pallas kernels for 1%

profile of v6, /device:TPU:1, one launch (start us, length us, event | category | flops | bytes accessed | tf_op | source)
XLA Modules:
  0.0 116.5 jit_solution(11454132533878242694)
XLA Ops:
  0.6 0.0 copy-start.2
  0.6 0.0 copy-start.3
  0.7 0.0 copy-start.4
  0.7 4.1 %shard_map.85 = bf16[32,224,128]{2,1,0:T(8,128)(2,1)S(1)} custom-call(bf16[6664,1,128]{2,1,0:T(2,128)(2,1)} %bitcast.6), custom_call_target="tpu_custom_call" | custom-call | tf_op jit(solution)/shard_map/pallas_call | solution.py:97
  4.8 0.0 copy-done.2
  4.8 0.0 copy-done.3
  4.8 0.0 copy-done.4
  4.8 0.0 copy-start
  4.8 0.0 copy-start.1
  4.8 0.1 pad_add_fusion.tab_ref
  4.9 34.2 %all_to_all.25.r_ref = bf16[32,224,128]{2,1,0:T(8,128)(2,1)S(1)} all-to-all(bf16[32,224,128]{2,1,0:T(8,128)(2,1)S(1)} %shard_map.85), channel_id=1, replica_groups=mesh['zh'=4,'zl'=2,'x'=4,'c'=2,'yh'=4,'yl'=2] {'zl','x','c','yl'}, dimensions={0} | all-to-all | bytes 3670016 | tf_op jit(solution)/shard_map/all_to_all | solution.py:283
  39.1 0.3 shard_map.86
  39.4 23.8 %all_to_all.26.r_ref = f32[16,16,128]{2,1,0:T(8,128)S(1)} all-to-all(f32[16,16,128]{2,1,0:T(8,128)S(1)} %shard_map.86), channel_id=1, replica_groups=mesh['zh'=4,'zl'=2,'x'=4,'c'=2,'yh'=4,'yl'=2] {'zh','yh'}, dimensions={0} | all-to-all | bytes 262144 | tf_op jit(solution)/shard_map/all_to_all | solution.py:283
  63.2 0.0 copy-done
  63.2 0.0 copy-done.1
  63.2 0.7 shard_map.87
  64.0 14.7 %all_to_all.27.s_ref = f32[16,32,128]{2,1,0:T(8,128)S(1)} all-to-all(f32[16,32,128]{2,1,0:T(8,128)S(1)} %get-tuple-element.18), channel_id=1, replica_groups=mesh['zh'=4,'zl'=2,'x'=4,'c'=2,'yh'=4,'yl'=2] {'zh','yh'}, dimensions={0} | all-to-all | bytes 524288 | tf_op jit(solution)/shard_map/all_to_all | solution.py:283
  78.7 13.7 %all_to_all.28.n_ref = f32[32,1,128]{2,1,0:T(1,128)S(1)} all-to-all(f32[32,1,128]{2,1,0:T(1,128)S(1)} %shard_map.88), channel_id=1, replica_groups=mesh['zh'=4,'zl'=2,'x'=4,'c'=2,'yh'=4,'yl'=2] {'zl','x','c','yl'}, dimensions={0} | all-to-all | bytes 32768 | tf_op jit(solution)/shard_map/all_to_all | solution.py:283
  92.4 0.9 shard_map.89
  93.4 15.4 %all_to_all.29.w_ref = bf16[16,224,128]{2,1,0:T(8,128)(2,1)S(1)} all-to-all(bf16[16,224,128]{2,1,0:T(8,128)(2,1)S(1)} %get-tuple-element.19), channel_id=1, replica_groups=mesh['zh'=4,'zl'=2,'x'=4,'c'=2,'yh'=4,'yl'=2] {'zl','x','yl'}, dimensions={0} | all-to-all | bytes 1835008 | tf_op jit(solution)/shard_map/all_to_all | solution.py:283
  108.7 4.3 %collective-permute-start = (bf16[16,224,128]{2,1,0:T(8,128)(2,1)S(1)}, bf16[16,224,128]{2,1,0:T(8,128)(2,1)S(1)}, u32[]{:S(2)}, u32[]{:S(2)}) collective-permute-start(bf16[16,224,128]{2,1,0:T(8,128)(2,1)S(1)} %all_to_all.29.w_ref), channel_id=1, source_target_pairs={{0,8},{8,0},{1,9},{9,1},{2,10},{10,2},{3,11},{11,3},{4,12},{12,4},... | collective-permute-start | bytes 2752520 | tf_op jit(solution)/shard_map/ppermute | solution.py:306
  113.0 1.3 %shard_map.92 = (f32[16,128]{1,0:T(8,128)}, f32[16,128]{1,0:T(8,128)}) custom-call(s32[18]{0:T(128)S(1)} %pad_add_fusion.tab_ref, f32[1,128]{1,0:T(1,128)S(1)} %get-tuple-element.23.t_ref, f32[16,128]{1,0:T(8,128)S(1)} %get-tuple-element.24.h_ref, f32[16,128]{1,0:T(8,128)S(1)} %get-tuple-element.25.m_ref, f32[16,128]{1,0:T(8,128)S(1)} %get-tuple-element.26.v_ref), custom_call_target="tpu_custom_call" | custom-call | tf_op jit(solution)/shard_map/pallas_call | solution.py:310
  114.3 0.4 shard_map.90
  114.8 0.3 collective-permute-done.w_ref
  115.1 1.4 %shard_map.91 = (f32[6664,128]{1,0:T(8,128)S(1)}, f32[64,128]{1,0:T(8,128)S(1)}, bf16[6664,128]{1,0:T(8,128)(2,1)}) custom-call(bf16[16,224,128]{2,1,0:T(8,128)(2,1)S(1)} %collective-permute-done.w_ref, f32[6664,128]{1,0:T(8,128)S(1)} %get-tuple-element.20.rows_in, f32[64,128]{1,0:T(8,128)S(1)} %get-tuple-element.21.tail_in), custom_call_target="tpu_custom_call", output_to_operand_aliasing={{0}: (1, {}), {1}: (2, {})} | custom-call | tf_op jit(solution)/shard_map/pallas_call | solution.py:313
  (1 shorter events, 0.0 us)
Async XLA Ops:
  0.6 4.2 %copy-start.2 = (s32[6]{0:T(128)S(1)}, s32[6]{0:T(128)}, u32[]{:S(2)}) copy-start(s32[6]{0:T(128)} %param.11) | copy-start | bytes 76
  0.6 4.2 %copy-start.3 = (s32[6]{0:T(128)S(1)}, s32[6]{0:T(128)}, u32[]{:S(2)}) copy-start(s32[6]{0:T(128)} %param.10) | copy-start | bytes 76
  0.7 4.2 %copy-start.4 = (s32[6]{0:T(128)S(1)}, s32[6]{0:T(128)}, u32[]{:S(2)}) copy-start(s32[6]{0:T(128)} %param.9) | copy-start | bytes 76
  4.8 58.4 %copy-start = (f32[1666]{0:T(1024)S(1)}, f32[1666]{0:T(1024)}, u32[]{:S(2)}) copy-start(f32[1666]{0:T(1024)} %mf_ref.1) | copy-start | bytes 19996
  4.8 58.4 %copy-start.1 = (f32[1666]{0:T(1024)S(1)}, f32[1666]{0:T(1024)}, u32[]{:S(2)}) copy-start(f32[1666]{0:T(1024)} %vf_ref.1) | copy-start | bytes 19996
  108.7 6.4 %collective-permute-start = (bf16[16,224,128]{2,1,0:T(8,128)(2,1)S(1)}, bf16[16,224,128]{2,1,0:T(8,128)(2,1)S(1)}, u32[]{:S(2)}, u32[]{:S(2)}) collective-permute-start(bf16[16,224,128]{2,1,0:T(8,128)(2,1)S(1)} %all_to_all.29.w_ref), channel_id=1, source_target_pairs={{0,8},{8,0},{1,9},{9,1},{2,10},{10,2},{3,11},{11,3},{4,12},{12,4},... | collective-permute-start | bytes 2752520 | tf_op jit(solution)/shard_map/ppermute | solution.py:306

commit v7 on v6

--- a/solution.py
+++ b/solution.py
@@ -6,9 +6,10 @@
 from jax.sharding import Mesh
 from jax.sharding import PartitionSpec as P
 
-AXES = ("zh", "zl", "x", "c", "yh", "yl")
-NEAR = ("zl", "x", "c", "yl")
+AXES = ("zh", "zl", "xh", "xl", "c", "yh", "yl")
+NEAR = ("zl", "xh", "xl", "c", "yl")
 FAR = ("zh", "yh")
+WIDE = ("zh", "xh", "yh")
 NX, NC, NL, NH = 4, 2, 2, 4
 NY, NZ = NH * NL, NH * NL
 NQ = NX * NC
@@ -22,6 +23,9 @@
 TOUCHED = 14
 SLOT = 16
 NEAR_ROWS = N_FAR * TOUCHED
+NXH = NX // 2
+N_CUBE, N_WIDE = 8, NH * NXH * NH
+HALF_ROWS = N_WIDE * TOUCHED
 LAYERS = 6
 STEPS = 7
 STEP_ROWS = ROWS // STEPS
@@ -58,7 +62,7 @@
 
 
 def q_index():
-    return lax.axis_index("x") * NC + lax.axis_index("c")
+    return (lax.axis_index("xh") * 2 + lax.axis_index("xl")) * NC + lax.axis_index("c")
 
 
 def y_index():
@@ -85,36 +89,63 @@
             return _
 
         lax.fori_loop(0, STEP_ROWS // CHUNK, widen, 0)
-    for near in range(N_NEAR):
-        zl, q, yl = near // (NQ * NL), near // NL % NQ, near % NL
-        for k, zh, yh in far_slots():
-            base = row_of(zh * NL + zl, q, yh * NL + yl)
+    for label in range(N_CUBE):
+        zl, xl, yl = label // 4, label // 2 % 2, label % 2
+        for k in range(NC * N_WIDE):
+            c, zh, xh, yh = k // N_WIDE, k // (NXH * NH) % NH, k // NH % NXH, k % NH
+            base = row_of(zh * NL + zl, (xh * 2 + xl) * NC + c, yh * NL + yl)
             rows[k * TOUCHED : (k + 1) * TOUCHED, :] = wide[base : base + TOUCHED, :]
-        o_ref[near] = rows[...].astype(bf16)
+        o_ref[label] = rows[...].astype(bf16)
 
 
 def packed(grads):
     return pl.pallas_call(
         pack_kernel,
-        out_shape=shape(N_NEAR, NEAR_ROWS, LANES, dtype=bf16),
+        out_shape=shape(N_CUBE, NC * HALF_ROWS, LANES, dtype=bf16),
         in_specs=[pl.BlockSpec(memory_space=pl.ANY)],
         out_specs=VMEM,
         scratch_shapes=[
             pltpu.VMEM((ROWS, 1, LANES), bf16),
             pltpu.SemaphoreType.DMA((STEPS,)),
             pltpu.VMEM((ROWS, LANES), f32),
-            pltpu.VMEM((NEAR_ROWS, LANES), f32),
+            pltpu.VMEM((NC * HALF_ROWS, LANES), f32),
         ],
         compiler_params=pltpu.CompilerParams(vmem_limit_bytes=51 * 1024 * 1024),
     )(grads.reshape(ROWS, 1, LANES))
 
 
-def spread_kernel(r_ref, o_ref, rows):
+def cubes():
+    def pair(k, parity, count, c):
+        return (2 * k + 2 * c * (1 - parity) + parity) % count
+
+    groups = []
+    for c in range(NC):
+        for kz in range(NZ // 2):
+            for kx in range(NX // 2):
+                for ky in range(NY // 2):
+                    group = []
+                    for label in range(N_CUBE):
+                        z = pair(kz, label // 4, NZ, c)
+                        x = pair(kx, label // 2 % 2, NX, c)
+                        y = pair(ky, label % 2, NY, c)
+                        group.append(((z * NX + x) * NC + c) * NY + y)
+                    groups.append(group)
+    return groups
+
+
+def halve_kernel(r_ref, keep_ref, give_ref, rows):
     total = r_ref[0].astype(f32)
-    for k in range(1, N_NEAR):
+    for k in range(1, N_CUBE):
         total = total + r_ref[k].astype(f32)
     rows[...] = total
-    for k in range(N_FAR):
+    c = lax.axis_index("c")
+    keep_ref[...] = rows[pl.ds(pl.multiple_of(c * HALF_ROWS, 8), HALF_ROWS), :]
+    give_ref[...] = rows[pl.ds(pl.multiple_of((1 - c) * HALF_ROWS, 8), HALF_ROWS), :]
+
+
+def spread_kernel(a_ref, b_ref, o_ref, rows):
+    rows[...] = a_ref[...] + b_ref[...]
+    for k in range(N_WIDE):
         o_ref[k, :TOUCHED, :] = rows[k * TOUCHED : (k + 1) * TOUCHED, :]
         o_ref[k, TOUCHED:, :] = jnp.zeros((SLOT - TOUCHED, LANES), f32)
 
@@ -154,7 +185,7 @@
     m_ref[...] = placed(mf_ref, rows)
     v_ref[...] = placed(vf_ref, rows)
     g = r_ref[0]
-    for k in range(1, N_FAR):
+    for k in range(1, N_WIDE):
         g = g + r_ref[k]
     pos, valid = slot_positions()
     g = jnp.where(valid, g * (1.0 / 512.0), 0.0)
@@ -283,17 +314,26 @@
     return lax.all_to_all(x, axes, 0, 0, tiled=True)
 
 
+def swapped(x):
+    return lax.ppermute(x, "c", [(0, 1), (1, 0)])
+
+
 def shards(grads, master, velocity, layer_offsets, layer_sizes, lars_skip):
     tab = jnp.concatenate([layer_offsets, layer_sizes, lars_skip])
     near, far, slot = (NEAR_ROWS, LANES), (SLOT, LANES), shape(SLOT, LANES)
     sending, tab = lax.optimization_barrier((packed(grads), tab))
-    spread = call(spread_kernel, shape(N_FAR, *far), [VMEM], [near])(sent(sending, NEAR))
+    received = lax.all_to_all(sending, AXES, 0, 0, axis_index_groups=cubes(), tiled=True)
+    half = (HALF_ROWS, LANES)
+    keep, give = call(
+        halve_kernel, (shape(*half), shape(*half)), [VMEM], [(NC * HALF_ROWS, LANES)]
+    )(received)
+    spread = call(spread_kernel, shape(N_WIDE, *far), [VMEM, VMEM], [half])(keep, swapped(give))
     shared, h, m, v = call(
         owner_kernel,
         (shape(N_FAR, 2 * SLOT, LANES), slot, slot, slot),
         [SMEM] + [VMEM] * 3,
         [(SLOT + 8, LANES)],
-    )(tab, sent(spread, FAR), master, velocity)
+    )(tab, sent(spread, WIDE), master, velocity)
     shared = sent(shared, FAR)
     norms = call(group_kernel, shape(N_NEAR, 1, LANES), [VMEM])(shared)
     w, trust = call(
@@ -302,8 +342,8 @@
         [SMEM, VMEM, VMEM],
         [near],
     )(tab, sent(norms, NEAR), shared)
-    w = sent(w, ("zl", "x", "yl"))
-    other = lax.ppermute(w, "c", [(0, 1), (1, 0)])
+    w = sent(w, ("zl", "xh", "xl", "yl"))
+    other = swapped(w)
     halves = (shape(ROWS, LANES), shape(NZ * NQ, LANES))
     block = (NL * NH * TOUCHED, LANES)
     rows, tail = call(own_half_kernel, halves, [VMEM], [block])(w)
@@ -331,9 +371,9 @@
 
 
 def solution(mesh):
-    finer = Mesh(mesh.devices.reshape(NH, NL, NX, NC, NH, NL), AXES)
+    finer = Mesh(mesh.devices.reshape(NH, NL, NXH, 2, NC, NH, NL), AXES)
     owned = P(AXES)
-    in_specs = (P(("zh", "zl", "x", "c"), ("yh", "yl"), None), owned, owned, P(), P(), P())
+    in_specs = (P(("zh", "zl", "xh", "xl", "c"), ("yh", "yl"), None), owned, owned, P(), P(), P())
     return jax.shard_map(
         shards, mesh=finer, in_specs=in_specs, out_specs=(P(), owned, owned), check_vma=False
     )

time: 117 us -> 116 us (level)
  blocking collectives: 102 us -> 97.4 us
  starting transfers between devices: 4.27 us -> 6.19 us
  waiting for transfers between devices: 0.34 us -> 1.8 us
    all_to_all x5 -> x4, blocking collectives: 102 us -> 63.8 us  [sent(): return lax.all_to_all(x, axes, 0, 0, tiled=True)]
    all_to_all x0 -> x1, blocking collectives: none -> 33.6 us  [shards(): lax.all_to_all(sending, AXES, 0, 0, axis_index_groups=cubes(), tiled=True)]
    ppermute x1 -> x2, starting transfers between devices: 4.27 us -> 6.19 us  [swapped(): return lax.ppermute(x, 'c', [(0, 1), (1, 0)])]
    ppermute x1 -> x2, waiting for transfers between devices: 0.34 us -> 1.8 us  [swapped(): return lax.ppermute(x, 'c', [(0, 1), (1, 0)])]
    pallas_call x2 -> x3, Pallas kernels: 4.41 us -> 4.49 us  [the longest x1 4.05 us: packed(): pl.pallas_call(pack_kernel, out_shape=shape(N_CUBE, NC * HALF_ROWS, LANES...]
  transfers between devices with their start and end apart: 1 -> 2, of which waited for: 1 -> 2; matrix products, arithmetic and copies ran while one was open for 0% -> 0% of each run, Pallas kernels for 1% -> 1%
where the time goes in v7:
time: 116 us
  blocking collectives  97.4 us (84%)
  Pallas kernels  9.32 us (8%)
  starting transfers between devices  6.19 us (5%)
  waiting for transfers between devices  1.8 us (2%)
    all_to_all x4, blocking collectives, sent(): return lax.all_to_all(x, axes, 0, 0, tiled=True)  63.8 us
    all_to_all x1, blocking collectives, shards(): lax.all_to_all(sending, AXES, 0, 0, axis_index_groups=cubes(), tiled=True)  33.6 us
    ppermute x2, starting transfers between devices, swapped(): return lax.ppermute(x, 'c', [(0, 1), (1, 0)])  6.19 us
    pallas_call x1, Pallas kernels, packed(): pl.pallas_call(pack_kernel, out_shape=shape(N_CUBE, NC * HALF_ROWS, LANES...  4.05 us
  transfers between devices with their start and end apart: 2, of which 2 were waited for; matrix products, arithmetic and copies ran while one was open for 0% of the time, Pallas kernels for 1%

profile of v7, /device:TPU:1, one launch (start us, length us, event | category | flops | bytes accessed | tf_op | source)
XLA Modules:
  0.0 115.6 jit_solution(7747537353561922894)
XLA Ops:
  0.6 0.0 copy-start.2
  0.6 0.0 copy-start.3
  0.7 0.0 copy-start.4
  0.7 4.1 %shard_map.85 = bf16[8,896,128]{2,1,0:T(8,128)(2,1)S(1)} custom-call(bf16[6664,1,128]{2,1,0:T(2,128)(2,1)} %bitcast.6), custom_call_target="tpu_custom_call" | custom-call | tf_op jit(solution)/shard_map/pallas_call | solution.py:102
  4.7 0.0 copy-done.2
  4.7 0.0 copy-done.3
  4.7 0.0 copy-done.4
  4.8 0.0 copy-start
  4.8 0.0 copy-start.1
  4.8 0.1 pad_add_fusion.tab_ref
  4.9 33.6 %all_to_all.25.r_ref = bf16[8,896,128]{2,1,0:T(8,128)(2,1)S(1)} all-to-all(bf16[8,896,128]{2,1,0:T(8,128)(2,1)S(1)} %shard_map.85), channel_id=1, replica_groups={{0,1,16,17,64,65,80,81},{2,3,18,19,66,67,82,83},{4,5,20,21,68,69,84,85}..., dimensions={0} | all-to-all | bytes 3670016 | tf_op jit(solution)/shard_map/all_to_all | solution.py:325
  38.5 0.4 shard_map.86
  38.9 1.9 %collective-permute-start = (f32[448,128]{1,0:T(8,128)S(1)}, f32[448,128]{1,0:T(8,128)S(1)}, u32[]{:S(2)}, u32[]{:S(2)}) collective-permute-start(f32[448,128]{1,0:T(8,128)S(1)} %get-tuple-element.21), channel_id=1, source_target_pairs={{0,8},{8,0},{1,9},{9,1},{2,10},{10,2},{3,11},{11,3},{4,12},{12,4},... | collective-permute-start | bytes 688136 | tf_op jit(solution)/shard_map/ppermute | solution.py:318
  40.8 1.5 %collective-permute-done.b_ref = f32[448,128]{1,0:T(8,128)S(1)} collective-permute-done((f32[448,128]{1,0:T(8,128)S(1)}, f32[448,128]{1,0:T(8,128)S(1)}, u32[]{:S(2)}, u32[]{:S(2)}) %collective-permute-start) | collective-permute-done | bytes 229408 | tf_op jit(solution)/shard_map/ppermute | solution.py:318
  42.3 19.6 %all_to_all.26.r_ref = f32[32,16,128]{2,1,0:T(8,128)S(1)} all-to-all(f32[32,16,128]{2,1,0:T(8,128)S(1)} %shard_map.87), channel_id=1, replica_groups=mesh['zh'=4,'zl'=2,'xh'=2,'xl'=2,'c'=2,'yh'=4,'yl'=2] {'zh','xh','yh'}, dimensions={0} | all-to-all | bytes 524288 | tf_op jit(solution)/shard_map/all_to_all | solution.py:314
  61.9 0.0 copy-done
  61.9 0.0 copy-done.1
  61.9 0.8 shard_map.88
  62.7 18.4 %all_to_all.27.s_ref = f32[16,32,128]{2,1,0:T(8,128)S(1)} all-to-all(f32[16,32,128]{2,1,0:T(8,128)S(1)} %get-tuple-element.22), channel_id=1, replica_groups=mesh['zh'=4,'zl'=2,'xh'=2,'xl'=2,'c'=2,'yh'=4,'yl'=2] {'zh','yh'}, dimensions={0} | all-to-all | bytes 524288 | tf_op jit(solution)/shard_map/all_to_all | solution.py:314
  81.2 10.4 %all_to_all.28.n_ref = f32[32,1,128]{2,1,0:T(1,128)S(1)} all-to-all(f32[32,1,128]{2,1,0:T(1,128)S(1)} %shard_map.89), channel_id=1, replica_groups=mesh['zh'=4,'zl'=2,'xh'=2,'xl'=2,'c'=2,'yh'=4,'yl'=2] {'zl','xh','xl','c..., dimensions={0} | all-to-all | bytes 32768 | tf_op jit(solution)/shard_map/all_to_all | solution.py:314
  91.5 0.9 shard_map.90
  92.4 15.4 %all_to_all.29.w_ref = bf16[16,224,128]{2,1,0:T(8,128)(2,1)S(1)} all-to-all(bf16[16,224,128]{2,1,0:T(8,128)(2,1)S(1)} %get-tuple-element.23), channel_id=1, replica_groups=mesh['zh'=4,'zl'=2,'xh'=2,'xl'=2,'c'=2,'yh'=4,'yl'=2] {'zl','xh','xl','yl'}, dimensions={0} | all-to-all | bytes 1835008 | tf_op jit(solution)/shard_map/all_to_all | solution.py:314
  107.8 4.3 %collective-permute-start.1 = (bf16[16,224,128]{2,1,0:T(8,128)(2,1)S(1)}, bf16[16,224,128]{2,1,0:T(8,128)(2,1)S(1)}, u32[]{:S(2)}, u32[]{:S(2)}) collective-permute-start(bf16[16,224,128]{2,1,0:T(8,128)(2,1)S(1)} %all_to_all.29.w_ref), channel_id=1, source_target_pairs={{0,8},{8,0},{1,9},{9,1},{2,10},{10,2},{3,11},{11,3},{4,12},{12,4},... | collective-permute-start | bytes 2752520 | tf_op jit(solution)/shard_map/ppermute | solution.py:318
  112.1 1.3 %shard_map.93 = (f32[16,128]{1,0:T(8,128)}, f32[16,128]{1,0:T(8,128)}) custom-call(s32[18]{0:T(128)S(1)} %pad_add_fusion.tab_ref, f32[1,128]{1,0:T(1,128)S(1)} %get-tuple-element.27.t_ref, f32[16,128]{1,0:T(8,128)S(1)} %get-tuple-element.28.h_ref, f32[16,128]{1,0:T(8,128)S(1)} %get-tuple-element.29.m_ref, f32[16,128]{1,0:T(8,128)S(1)} %get-tuple-element.30.v_ref), custom_call_target="tpu_custom_call" | custom-call | tf_op jit(solution)/shard_map/pallas_call | solution.py:350
  113.4 0.4 shard_map.91
  113.8 0.3 collective-permute-done.1.w_ref
  114.2 1.4 %shard_map.92 = (f32[6664,128]{1,0:T(8,128)S(1)}, f32[64,128]{1,0:T(8,128)S(1)}, bf16[6664,128]{1,0:T(8,128)(2,1)}) custom-call(bf16[16,224,128]{2,1,0:T(8,128)(2,1)S(1)} %collective-permute-done.1.w_ref, f32[6664,128]{1,0:T(8,128)S(1)} %get-tuple-element.24.rows_in, ...), custom_call_target="tpu_custom_call", output_to_operand_aliasing={{0}: (1, {}), {1}: (2, {})} | custom-call | tf_op jit(solution)/shard_map/pallas_call | solution.py:353
  (2 shorter events, 0.1 us)
Async XLA Ops:
  0.6 4.1 %copy-start.2 = (s32[6]{0:T(128)S(1)}, s32[6]{0:T(128)}, u32[]{:S(2)}) copy-start(s32[6]{0:T(128)} %param.11) | copy-start | bytes 76
  0.6 4.1 %copy-start.3 = (s32[6]{0:T(128)S(1)}, s32[6]{0:T(128)}, u32[]{:S(2)}) copy-start(s32[6]{0:T(128)} %param.10) | copy-start | bytes 76
  0.7 4.1 %copy-start.4 = (s32[6]{0:T(128)S(1)}, s32[6]{0:T(128)}, u32[]{:S(2)}) copy-start(s32[6]{0:T(128)} %param.9) | copy-start | bytes 76
  4.8 57.2 %copy-start = (f32[1666]{0:T(1024)S(1)}, f32[1666]{0:T(1024)}, u32[]{:S(2)}) copy-start(f32[1666]{0:T(1024)} %mf_ref.1) | copy-start | bytes 19996
  4.8 57.2 %copy-start.1 = (f32[1666]{0:T(1024)S(1)}, f32[1666]{0:T(1024)}, u32[]{:S(2)}) copy-start(f32[1666]{0:T(1024)} %vf_ref.1) | copy-start | bytes 19996
  38.9 3.4 %collective-permute-start = (f32[448,128]{1,0:T(8,128)S(1)}, f32[448,128]{1,0:T(8,128)S(1)}, u32[]{:S(2)}, u32[]{:S(2)}) collective-permute-start(f32[448,128]{1,0:T(8,128)S(1)} %get-tuple-element.21), channel_id=1, source_target_pairs={{0,8},{8,0},{1,9},{9,1},{2,10},{10,2},{3,11},{11,3},{4,12},{12,4},... | collective-permute-start | bytes 688136 | tf_op jit(solution)/shard_map/ppermute | solution.py:318
  107.8 6.4 %collective-permute-start.1 = (bf16[16,224,128]{2,1,0:T(8,128)(2,1)S(1)}, bf16[16,224,128]{2,1,0:T(8,128)(2,1)S(1)}, u32[]{:S(2)}, u32[]{:S(2)}) collective-permute-start(bf16[16,224,128]{2,1,0:T(8,128)(2,1)S(1)} %all_to_all.29.w_ref), channel_id=1, source_target_pairs={{0,8},{8,0},{1,9},{9,1},{2,10},{10,2},{3,11},{11,3},{4,12},{12,4},... | collective-permute-start | bytes 2752520 | tf_op jit(solution)/shard_map/ppermute | solution.py:318

commit v8 on v7

--- a/solution.py
+++ b/solution.py
@@ -1,3 +1,5 @@
+import functools
+
 import jax
 import jax.numpy as jnp
 from jax import lax
@@ -115,8 +117,8 @@
 
 
 def cubes():
-    def pair(k, parity, count, c):
-        return (2 * k + 2 * c * (1 - parity) + parity) % count
+    def pair(k, parity, count, shifted):
+        return (2 * k + 2 * shifted * (1 - parity) + parity) % count
 
     groups = []
     for c in range(NC):
@@ -127,20 +129,20 @@
                     for label in range(N_CUBE):
                         z = pair(kz, label // 4, NZ, c)
                         x = pair(kx, label // 2 % 2, NX, c)
-                        y = pair(ky, label % 2, NY, c)
+                        y = pair(ky, label % 2, NY, 1 - c)
                         group.append(((z * NX + x) * NC + c) * NY + y)
                     groups.append(group)
     return groups
 
 
-def halve_kernel(r_ref, keep_ref, give_ref, rows):
-    total = r_ref[0].astype(f32)
+def half_kernel(mine, r_ref, o_ref):
+    c = lax.axis_index("c")
+    c = c if mine else 1 - c
+    at = pl.ds(pl.multiple_of(c * HALF_ROWS, 16), HALF_ROWS)
+    total = r_ref[0, at, :].astype(f32)
     for k in range(1, N_CUBE):
-        total = total + r_ref[k].astype(f32)
-    rows[...] = total
-    c = lax.axis_index("c")
-    keep_ref[...] = rows[pl.ds(pl.multiple_of(c * HALF_ROWS, 8), HALF_ROWS), :]
-    give_ref[...] = rows[pl.ds(pl.multiple_of((1 - c) * HALF_ROWS, 8), HALF_ROWS), :]
+        total = total + r_ref[k, at, :].astype(f32)
+    o_ref[...] = total
 
 
 def spread_kernel(a_ref, b_ref, o_ref, rows):
@@ -181,27 +183,30 @@
     return jnp.where(lane >= shift, here, above)
 
 
-def owner_kernel(tab_ref, r_ref, mf_ref, vf_ref, o_ref, h_ref, m_ref, v_ref, rows):
-    m_ref[...] = placed(mf_ref, rows)
-    v_ref[...] = placed(vf_ref, rows)
+def owner_kernel(tab_ref, r_ref, mf_ref, vf_ref, o_ref, h_ref, m_ref, v_ref, turn):
+    m_ref[...] = placed(mf_ref, turn)
+    v_ref[...] = placed(vf_ref, turn)
     g = r_ref[0]
     for k in range(1, N_WIDE):
         g = g + r_ref[k]
     pos, valid = slot_positions()
     g = jnp.where(valid, g * (1.0 / 512.0), 0.0)
     m = m_ref[...]
-    lane = lax.broadcasted_iota(jnp.int32, (1, LANES), 1)
-    total = jnp.zeros((1, LANES), f32)
+    row = lax.broadcasted_iota(jnp.int32, (SLOT, LANES), 0)
+    lane = lax.broadcasted_iota(jnp.int32, (SLOT, LANES), 1)
+    stack = jnp.zeros((SLOT, LANES), f32)
     decay = jnp.zeros((SLOT, LANES), f32)
+    mm, gg = m * m, g * g
     for l in range(LAYERS):
         mask = in_layer(tab_ref, l, pos)
         decay = jnp.where(mask, (1.0 - skipped(tab_ref, l)) * 0.001, decay)
-        for at, square in ((l, m * m), (8 + l, g * g)):
+        for at, square in ((l, mm), (8 + l, gg)):
             rows = jnp.sum(jnp.where(mask, square, 0.0), axis=0, keepdims=True)
-            total = total + jnp.where(lane == at, jnp.sum(rows, axis=1, keepdims=True), 0.0)
+            stack = jnp.where(row == at, rows, stack)
+    sums = jnp.sum(stack, axis=1, keepdims=True)
+    total = jnp.sum(jnp.where(lane == row, sums, 0.0), axis=0, keepdims=True)
     h = g + decay * m
     h_ref[...] = h
-    row = lax.broadcasted_iota(jnp.int32, (SLOT, LANES), 0)
     out = jnp.where(row == TOUCHED, total, h)
     a = m - 0.9 * v_ref[...]
     for k in range(N_FAR):
@@ -324,10 +329,9 @@
     sending, tab = lax.optimization_barrier((packed(grads), tab))
     received = lax.all_to_all(sending, AXES, 0, 0, axis_index_groups=cubes(), tiled=True)
     half = (HALF_ROWS, LANES)
-    keep, give = call(
-        halve_kernel, (shape(*half), shape(*half)), [VMEM], [(NC * HALF_ROWS, LANES)]
-    )(received)
-    spread = call(spread_kernel, shape(N_WIDE, *far), [VMEM, VMEM], [half])(keep, swapped(give))
+    give = swapped(call(functools.partial(half_kernel, False), shape(*half), [VMEM])(received))
+    keep = call(functools.partial(half_kernel, True), shape(*half), [VMEM])(received)
+    spread = call(spread_kernel, shape(N_WIDE, *far), [VMEM, VMEM], [half])(keep, give)
     shared, h, m, v = call(
         owner_kernel,
         (shape(N_FAR, 2 * SLOT, LANES), slot, slot, slot),

time: 116 us -> 116 us (level)
    all_to_all x4, blocking collectives: 63.8 us -> 67 us  [sent(): return lax.all_to_all(x, axes, 0, 0, tiled=True)]
    all_to_all x1, blocking collectives: 33.6 us -> 30.5 us  [shards(): lax.all_to_all(sending, AXES, 0, 0, axis_index_groups=cubes(), tiled=True)]
  transfers between devices with their start and end apart: 2 -> 2, of which waited for: 2 -> 2; matrix products, arithmetic and copies ran while one was open for 0% -> 0% of each run, Pallas kernels for 1% -> 2%
where the time goes in v8:
time: 116 us; the launch traced here: 115 us
  blocking collectives  97.5 us (84%)
  Pallas kernels  9.16 us (8%)
  starting transfers between devices  6.19 us (5%)
  waiting for transfers between devices  1.66 us (1%)
    all_to_all x4, blocking collectives, sent(): return lax.all_to_all(x, axes, 0, 0, tiled=True)  67 us
    all_to_all x1, blocking collectives, shards(): lax.all_to_all(sending, AXES, 0, 0, axis_index_groups=cubes(), tiled=True)  30.5 us
    ppermute x2, starting transfers between devices, swapped(): return lax.ppermute(x, 'c', [(0, 1), (1, 0)])  6.19 us
    pallas_call x1, Pallas kernels, packed(): pl.pallas_call(pack_kernel, out_shape=shape(N_CUBE, NC * HALF_ROWS, LANES...  4.05 us
  transfers between devices with their start and end apart: 2, of which 2 were waited for; matrix products, arithmetic and copies ran while one was open for 0% of the time, Pallas kernels for 2%

profile of v8, /device:TPU:1, one launch (start us, length us, event | category | flops | bytes accessed | tf_op | source)
XLA Modules:
  0.0 115.4 jit_solution(8173630455065780976)
XLA Ops:
  0.6 0.0 copy-start.2
  0.6 0.0 copy-start.3
  0.7 0.0 copy-start.4
  0.7 4.1 %shard_map.85 = bf16[8,896,128]{2,1,0:T(8,128)(2,1)S(1)} custom-call(bf16[6664,1,128]{2,1,0:T(2,128)(2,1)} %bitcast.6), custom_call_target="tpu_custom_call" | custom-call | tf_op jit(solution)/shard_map/pallas_call | solution.py:104
  4.7 0.0 copy-done.2
  4.7 0.0 copy-done.3
  4.7 0.0 copy-done.4
  4.8 0.1 pad_add_fusion.tab_ref
  4.8 30.5 %all_to_all.25.r_ref = bf16[8,896,128]{2,1,0:T(8,128)(2,1)S(1)} all-to-all(bf16[8,896,128]{2,1,0:T(8,128)(2,1)S(1)} %shard_map.85), channel_id=1, replica_groups={{2,1,18,17,66,65,82,81},{4,3,20,19,68,67,84,83},{6,5,22,21,70,69,86,85}..., dimensions={0} | all-to-all | bytes 3670016 | tf_op jit(solution)/shard_map/all_to_all | solution.py:330
  35.3 0.0 copy-start
  35.3 0.0 copy-start.1
  35.4 0.1 shard_map.87
  35.5 1.9 %collective-permute-start = (f32[448,128]{1,0:T(8,128)S(1)}, f32[448,128]{1,0:T(8,128)S(1)}, u32[]{:S(2)}, u32[]{:S(2)}) collective-permute-start(f32[448,128]{1,0:T(8,128)S(1)} %shard_map.87), channel_id=1, source_target_pairs={{0,8},{8,0},{1,9},{9,1},{2,10},{10,2},{3,11},{11,3},{4,12},{12,4},... | collective-permute-start | bytes 688136 | tf_op jit(solution)/shard_map/ppermute | solution.py:323
  37.4 0.1 shard_map.86.a_ref
  37.5 1.3 %collective-permute-done.b_ref = f32[448,128]{1,0:T(8,128)S(1)} collective-permute-done((f32[448,128]{1,0:T(8,128)S(1)}, f32[448,128]{1,0:T(8,128)S(1)}, u32[]{:S(2)}, u32[]{:S(2)}) %collective-permute-start) | collective-permute-done | bytes 229408 | tf_op jit(solution)/shard_map/ppermute | solution.py:323
  38.9 23.8 %all_to_all.26.r_ref = f32[32,16,128]{2,1,0:T(8,128)S(1)} all-to-all(f32[32,16,128]{2,1,0:T(8,128)S(1)} %shard_map.88), channel_id=1, replica_groups=mesh['zh'=4,'zl'=2,'xh'=2,'xl'=2,'c'=2,'yh'=4,'yl'=2] {'zh','xh','yh'}, dimensions={0} | all-to-all | bytes 524288 | tf_op jit(solution)/shard_map/all_to_all | solution.py:319
  62.7 0.0 copy-done
  62.7 0.0 copy-done.1
  62.7 0.7 shard_map.89
  63.4 17.2 %all_to_all.27.s_ref = f32[16,32,128]{2,1,0:T(8,128)S(1)} all-to-all(f32[16,32,128]{2,1,0:T(8,128)S(1)} %get-tuple-element.18), channel_id=1, replica_groups=mesh['zh'=4,'zl'=2,'xh'=2,'xl'=2,'c'=2,'yh'=4,'yl'=2] {'zh','yh'}, dimensions={0} | all-to-all | bytes 524288 | tf_op jit(solution)/shard_map/all_to_all | solution.py:319
  80.7 10.6 %all_to_all.28.n_ref = f32[32,1,128]{2,1,0:T(1,128)S(1)} all-to-all(f32[32,1,128]{2,1,0:T(1,128)S(1)} %shard_map.90), channel_id=1, replica_groups=mesh['zh'=4,'zl'=2,'xh'=2,'xl'=2,'c'=2,'yh'=4,'yl'=2] {'zl','xh','xl','c..., dimensions={0} | all-to-all | bytes 32768 | tf_op jit(solution)/shard_map/all_to_all | solution.py:319
  91.3 0.9 shard_map.91
  92.2 15.4 %all_to_all.29.w_ref = bf16[16,224,128]{2,1,0:T(8,128)(2,1)S(1)} all-to-all(bf16[16,224,128]{2,1,0:T(8,128)(2,1)S(1)} %get-tuple-element.19), channel_id=1, replica_groups=mesh['zh'=4,'zl'=2,'xh'=2,'xl'=2,'c'=2,'yh'=4,'yl'=2] {'zl','xh','xl','yl'}, dimensions={0} | all-to-all | bytes 1835008 | tf_op jit(solution)/shard_map/all_to_all | solution.py:319
  107.6 4.3 %collective-permute-start.1 = (bf16[16,224,128]{2,1,0:T(8,128)(2,1)S(1)}, bf16[16,224,128]{2,1,0:T(8,128)(2,1)S(1)}, u32[]{:S(2)}, u32[]{:S(2)}) collective-permute-start(bf16[16,224,128]{2,1,0:T(8,128)(2,1)S(1)} %all_to_all.29.w_ref), channel_id=1, source_target_pairs={{0,8},{8,0},{1,9},{9,1},{2,10},{10,2},{3,11},{11,3},{4,12},{12,4},... | collective-permute-start | bytes 2752520 | tf_op jit(solution)/shard_map/ppermute | solution.py:323
  111.9 1.3 %shard_map.94 = (f32[16,128]{1,0:T(8,128)}, f32[16,128]{1,0:T(8,128)}) custom-call(s32[18]{0:T(128)S(1)} %pad_add_fusion.tab_ref, f32[1,128]{1,0:T(1,128)S(1)} %get-tuple-element.23.t_ref, f32[16,128]{1,0:T(8,128)S(1)} %get-tuple-element.24.h_ref, f32[16,128]{1,0:T(8,128)S(1)} %get-tuple-element.25.m_ref, f32[16,128]{1,0:T(8,128)S(1)} %get-tuple-element.26.v_ref), custom_call_target="tpu_custom_call" | custom-call | tf_op jit(solution)/shard_map/pallas_call | solution.py:354
  113.2 0.4 shard_map.92
  113.6 0.3 collective-permute-done.1.w_ref
  114.0 1.4 %shard_map.93 = (f32[6664,128]{1,0:T(8,128)S(1)}, f32[64,128]{1,0:T(8,128)S(1)}, bf16[6664,128]{1,0:T(8,128)(2,1)}) custom-call(bf16[16,224,128]{2,1,0:T(8,128)(2,1)S(1)} %collective-permute-done.1.w_ref, f32[6664,128]{1,0:T(8,128)S(1)} %get-tuple-element.20.rows_in, ...), custom_call_target="tpu_custom_call", output_to_operand_aliasing={{0}: (1, {}), {1}: (2, {})} | custom-call | tf_op jit(solution)/shard_map/pallas_call | solution.py:357
  (2 shorter events, 0.1 us)
Async XLA Ops:
  0.6 4.1 %copy-start.2 = (s32[6]{0:T(128)S(1)}, s32[6]{0:T(128)}, u32[]{:S(2)}) copy-start(s32[6]{0:T(128)} %param.11) | copy-start | bytes 76
  0.6 4.1 %copy-start.3 = (s32[6]{0:T(128)S(1)}, s32[6]{0:T(128)}, u32[]{:S(2)}) copy-start(s32[6]{0:T(128)} %param.10) | copy-start | bytes 76
  0.7 4.1 %copy-start.4 = (s32[6]{0:T(128)S(1)}, s32[6]{0:T(128)}, u32[]{:S(2)}) copy-start(s32[6]{0:T(128)} %param.9) | copy-start | bytes 76
  35.3 27.4 %copy-start = (f32[1666]{0:T(1024)S(1)}, f32[1666]{0:T(1024)}, u32[]{:S(2)}) copy-start(f32[1666]{0:T(1024)} %mf_ref.1) | copy-start | bytes 19996
  35.3 27.4 %copy-start.1 = (f32[1666]{0:T(1024)S(1)}, f32[1666]{0:T(1024)}, u32[]{:S(2)}) copy-start(f32[1666]{0:T(1024)} %vf_ref.1) | copy-start | bytes 19996
  35.5 3.4 %collective-permute-start = (f32[448,128]{1,0:T(8,128)S(1)}, f32[448,128]{1,0:T(8,128)S(1)}, u32[]{:S(2)}, u32[]{:S(2)}) collective-permute-start(f32[448,128]{1,0:T(8,128)S(1)} %shard_map.87), channel_id=1, source_target_pairs={{0,8},{8,0},{1,9},{9,1},{2,10},{10,2},{3,11},{11,3},{4,12},{12,4},... | collective-permute-start | bytes 688136 | tf_op jit(solution)/shard_map/ppermute | solution.py:323
  107.6 6.4 %collective-permute-start.1 = (bf16[16,224,128]{2,1,0:T(8,128)(2,1)S(1)}, bf16[16,224,128]{2,1,0:T(8,128)(2,1)S(1)}, u32[]{:S(2)}, u32[]{:S(2)}) collective-permute-start(bf16[16,224,128]{2,1,0:T(8,128)(2,1)S(1)} %all_to_all.29.w_ref), channel_id=1, source_target_pairs={{0,8},{8,0},{1,9},{9,1},{2,10},{10,2},{3,11},{11,3},{4,12},{12,4},... | collective-permute-start | bytes 2752520 | tf_op jit(solution)/shard_map/ppermute | solution.py:323

commit v9 on v8

--- a/solution.py
+++ b/solution.py
@@ -29,9 +29,9 @@
 N_CUBE, N_WIDE = 8, NH * NXH * NH
 HALF_ROWS = N_WIDE * TOUCHED
 LAYERS = 6
-STEPS = 7
-STEP_ROWS = ROWS // STEPS
 CHUNK = 136
+STEPS = (2, 5, 7, 7, 7, 7, 7, 7)
+SPARE = 8
 f32 = jnp.float32
 bf16 = jnp.bfloat16
 VMEM = pl.BlockSpec(memory_space=pltpu.VMEM)
@@ -76,28 +76,28 @@
 
 
 def pack_kernel(x_ref, o_ref, held, sems, wide, rows):
-    copies = []
-    for i in range(STEPS):
-        at = pl.ds(i * STEP_ROWS, STEP_ROWS)
+    copies, starts = [], [CHUNK * sum(STEPS[:i]) for i in range(len(STEPS))]
+    for i, count in enumerate(STEPS):
+        at = pl.ds(starts[i], count * CHUNK)
         copies.append(pltpu.make_async_copy(x_ref.at[at], held.at[at], sems.at[i]))
         copies[-1].start()
-    for i in range(STEPS):
+    for i, count in enumerate(STEPS):
         copies[i].wait()
 
         def widen(k, _):
-            at = i * STEP_ROWS + k * CHUNK
+            at = starts[i] + k * CHUNK
             for r in range(CHUNK):
                 wide[pl.ds(at + r, 1), :] = held[at + r].astype(f32)
             return _
 
-        lax.fori_loop(0, STEP_ROWS // CHUNK, widen, 0)
+        lax.fori_loop(0, count, widen, 0)
     for label in range(N_CUBE):
         zl, xl, yl = label // 4, label // 2 % 2, label % 2
         for k in range(NC * N_WIDE):
             c, zh, xh, yh = k // N_WIDE, k // (NXH * NH) % NH, k // NH % NXH, k % NH
             base = row_of(zh * NL + zl, (xh * 2 + xl) * NC + c, yh * NL + yl)
             rows[k * TOUCHED : (k + 1) * TOUCHED, :] = wide[base : base + TOUCHED, :]
-        o_ref[label] = rows[...].astype(bf16)
+        o_ref[label] = rows[: NC * HALF_ROWS, :].astype(bf16)
 
 
 def packed(grads):
@@ -107,10 +107,10 @@
         in_specs=[pl.BlockSpec(memory_space=pl.ANY)],
         out_specs=VMEM,
         scratch_shapes=[
-            pltpu.VMEM((ROWS, 1, LANES), bf16),
-            pltpu.SemaphoreType.DMA((STEPS,)),
-            pltpu.VMEM((ROWS, LANES), f32),
-            pltpu.VMEM((NC * HALF_ROWS, LANES), f32),
+            pltpu.VMEM((ROWS + SPARE, 1, LANES), bf16),
+            pltpu.SemaphoreType.DMA((len(STEPS),)),
+            pltpu.VMEM((ROWS + SPARE, LANES), f32),
+            pltpu.VMEM((NC * HALF_ROWS + SPARE, LANES), f32),
         ],
         compiler_params=pltpu.CompilerParams(vmem_limit_bytes=51 * 1024 * 1024),
     )(grads.reshape(ROWS, 1, LANES))
@@ -146,7 +146,7 @@
 
 
 def spread_kernel(a_ref, b_ref, o_ref, rows):
-    rows[...] = a_ref[...] + b_ref[...]
+    rows[:HALF_ROWS, :] = a_ref[...] + b_ref[...]
     for k in range(N_WIDE):
         o_ref[k, :TOUCHED, :] = rows[k * TOUCHED : (k + 1) * TOUCHED, :]
         o_ref[k, TOUCHED:, :] = jnp.zeros((SLOT - TOUCHED, LANES), f32)
@@ -172,13 +172,13 @@
 
 def placed(flat_ref, rows):
     whole = SHARD // LANES
-    rows[...] = jnp.zeros((SLOT + 8, LANES), f32)
+    rows[...] = jnp.zeros((SLOT + 8 + SPARE, LANES), f32)
     for k in range(whole):
         rows[8 + k, :] = flat_ref[pl.ds(k * LANES, LANES)]
     rows[8 + whole, pl.ds(0, SHARD - whole * LANES)] = flat_ref[pl.ds(whole * LANES, SHARD - whole * LANES)]
     shift = 2 * (NY * q_index() + y_index())
     lane = lax.broadcasted_iota(jnp.int32, (SLOT, LANES), 1)
-    here = pltpu.roll(rows[8:, :], shift, 1)
+    here = pltpu.roll(rows[8 : SLOT + 8, :], shift, 1)
     above = pltpu.roll(rows[7 : SLOT + 7, :], shift, 1)
     return jnp.where(lane >= shift, here, above)
 
@@ -251,7 +251,7 @@
     for k, t in enumerate(trust_at(tab_ref, trust, pos)):
         w = s_ref[k, SLOT:, :] - 8.0 * t * s_ref[k, :SLOT, :]
         rows[k * TOUCHED : (k + 1) * TOUCHED, :] = w[:TOUCHED, :]
-    w = rows[...].astype(bf16)
+    w = rows[:NEAR_ROWS, :].astype(bf16)
     for k in range(NL * NX * NL):
         w_ref[k] = w
 
@@ -331,12 +331,12 @@
     half = (HALF_ROWS, LANES)
     give = swapped(call(functools.partial(half_kernel, False), shape(*half), [VMEM])(received))
     keep = call(functools.partial(half_kernel, True), shape(*half), [VMEM])(received)
-    spread = call(spread_kernel, shape(N_WIDE, *far), [VMEM, VMEM], [half])(keep, give)
+    spread = call(spread_kernel, shape(N_WIDE, *far), [VMEM, VMEM], [(HALF_ROWS + SPARE, LANES)])(keep, give)
     shared, h, m, v = call(
         owner_kernel,
         (shape(N_FAR, 2 * SLOT, LANES), slot, slot, slot),
         [SMEM] + [VMEM] * 3,
-        [(SLOT + 8, LANES)],
+        [(SLOT + 8 + SPARE, LANES)],
     )(tab, sent(spread, WIDE), master, velocity)
     shared = sent(shared, FAR)
     norms = call(group_kernel, shape(N_NEAR, 1, LANES), [VMEM])(shared)
@@ -344,12 +344,12 @@
         update_kernel,
         (shape(NL * NX * NL, *near, dtype=bf16), shape(1, LANES)),
         [SMEM, VMEM, VMEM],
-        [near],
+        [(NEAR_ROWS + SPARE, LANES)],
     )(tab, sent(norms, NEAR), shared)
     w = sent(w, ("zl", "xh", "xl", "yl"))
     other = swapped(w)
-    halves = (shape(ROWS, LANES), shape(NZ * NQ, LANES))
-    block = (NL * NH * TOUCHED, LANES)
+    halves = (shape(ROWS + SPARE, LANES), shape(NZ * NQ + SPARE, LANES))
+    block = (NL * NH * TOUCHED + SPARE, LANES)
     rows, tail = call(own_half_kernel, halves, [VMEM], [block])(w)
     new_master, new_velocity = call(
         own_kernel, (slot, slot), [SMEM] + [VMEM] * 4, [(SLOT + 8, LANES)]

time: 116 us -> 116 us (level)
  no operation moved by 1% of the time
where the time goes in v9:
time: 116 us; the launch traced here: 115 us
  blocking collectives  97.5 us (84%)
  Pallas kernels  9.08 us (8%)
  starting transfers between devices  6.19 us (5%)
  waiting for transfers between devices  1.67 us (1%)
    all_to_all x4, blocking collectives, sent(): return lax.all_to_all(x, axes, 0, 0, tiled=True)  67 us
    all_to_all x1, blocking collectives, shards(): lax.all_to_all(sending, AXES, 0, 0, axis_index_groups=cubes(), tiled=True)  30.5 us
    ppermute x2, starting transfers between devices, swapped(): return lax.ppermute(x, 'c', [(0, 1), (1, 0)])  6.19 us
    pallas_call x1, Pallas kernels, packed(): pl.pallas_call(pack_kernel, out_shape=shape(N_CUBE, NC * HALF_ROWS, LANES...  3.98 us
  transfers between devices with their start and end apart: 2, of which 2 were waited for; matrix products, arithmetic and copies ran while one was open for 0% of the time, Pallas kernels for 2%

profile of v9, /device:TPU:1, one launch (start us, length us, event | category | flops | bytes accessed | tf_op | source)
XLA Modules:
  0.0 115.3 jit_solution(15250128768047164277)
XLA Ops:
  0.6 0.0 copy-start.2
  0.6 0.0 copy-start.3
  0.7 0.0 copy-start.4
  0.7 4.0 %shard_map.85 = bf16[8,896,128]{2,1,0:T(8,128)(2,1)S(1)} custom-call(bf16[6664,1,128]{2,1,0:T(2,128)(2,1)} %bitcast.6), custom_call_target="tpu_custom_call" | custom-call | tf_op jit(solution)/shard_map/pallas_call | solution.py:104
  4.6 0.0 copy-done.2
  4.7 0.0 copy-done.3
  4.7 0.0 copy-done.4
  4.7 0.1 pad_add_fusion.tab_ref
  4.8 30.5 %all_to_all.25.r_ref = bf16[8,896,128]{2,1,0:T(8,128)(2,1)S(1)} all-to-all(bf16[8,896,128]{2,1,0:T(8,128)(2,1)S(1)} %shard_map.85), channel_id=1, replica_groups={{2,1,18,17,66,65,82,81},{4,3,20,19,68,67,84,83},{6,5,22,21,70,69,86,85}..., dimensions={0} | all-to-all | bytes 3670016 | tf_op jit(solution)/shard_map/all_to_all | solution.py:330
  35.3 0.0 copy-start
  35.3 0.0 copy-start.1
  35.3 0.1 shard_map.87
  35.4 1.9 %collective-permute-start = (f32[448,128]{1,0:T(8,128)S(1)}, f32[448,128]{1,0:T(8,128)S(1)}, u32[]{:S(2)}, u32[]{:S(2)}) collective-permute-start(f32[448,128]{1,0:T(8,128)S(1)} %shard_map.87), channel_id=1, source_target_pairs={{0,8},{8,0},{1,9},{9,1},{2,10},{10,2},{3,11},{11,3},{4,12},{12,4},... | collective-permute-start | bytes 688136 | tf_op jit(solution)/shard_map/ppermute | solution.py:323
  37.3 0.1 shard_map.86.a_ref
  37.5 1.3 %collective-permute-done.b_ref = f32[448,128]{1,0:T(8,128)S(1)} collective-permute-done((f32[448,128]{1,0:T(8,128)S(1)}, f32[448,128]{1,0:T(8,128)S(1)}, u32[]{:S(2)}, u32[]{:S(2)}) %collective-permute-start) | collective-permute-done | bytes 229408 | tf_op jit(solution)/shard_map/ppermute | solution.py:323
  38.8 23.8 %all_to_all.26.r_ref = f32[32,16,128]{2,1,0:T(8,128)S(1)} all-to-all(f32[32,16,128]{2,1,0:T(8,128)S(1)} %shard_map.88), channel_id=1, replica_groups=mesh['zh'=4,'zl'=2,'xh'=2,'xl'=2,'c'=2,'yh'=4,'yl'=2] {'zh','xh','yh'}, dimensions={0} | all-to-all | bytes 524288 | tf_op jit(solution)/shard_map/all_to_all | solution.py:319
  62.6 0.0 copy-done
  62.6 0.0 copy-done.1
  62.6 0.7 shard_map.89
  63.4 17.2 %all_to_all.27.s_ref = f32[16,32,128]{2,1,0:T(8,128)S(1)} all-to-all(f32[16,32,128]{2,1,0:T(8,128)S(1)} %get-tuple-element.18), channel_id=1, replica_groups=mesh['zh'=4,'zl'=2,'xh'=2,'xl'=2,'c'=2,'yh'=4,'yl'=2] {'zh','yh'}, dimensions={0} | all-to-all | bytes 524288 | tf_op jit(solution)/shard_map/all_to_all | solution.py:319
  80.6 10.6 %all_to_all.28.n_ref = f32[32,1,128]{2,1,0:T(1,128)S(1)} all-to-all(f32[32,1,128]{2,1,0:T(1,128)S(1)} %shard_map.90), channel_id=1, replica_groups=mesh['zh'=4,'zl'=2,'xh'=2,'xl'=2,'c'=2,'yh'=4,'yl'=2] {'zl','xh','xl','c..., dimensions={0} | all-to-all | bytes 32768 | tf_op jit(solution)/shard_map/all_to_all | solution.py:319
  91.2 0.9 shard_map.91
  92.2 15.4 %all_to_all.29.w_ref = bf16[16,224,128]{2,1,0:T(8,128)(2,1)S(1)} all-to-all(bf16[16,224,128]{2,1,0:T(8,128)(2,1)S(1)} %get-tuple-element.19), channel_id=1, replica_groups=mesh['zh'=4,'zl'=2,'xh'=2,'xl'=2,'c'=2,'yh'=4,'yl'=2] {'zl','xh','xl','yl'}, dimensions={0} | all-to-all | bytes 1835008 | tf_op jit(solution)/shard_map/all_to_all | solution.py:319
  107.5 4.3 %collective-permute-start.1 = (bf16[16,224,128]{2,1,0:T(8,128)(2,1)S(1)}, bf16[16,224,128]{2,1,0:T(8,128)(2,1)S(1)}, u32[]{:S(2)}, u32[]{:S(2)}) collective-permute-start(bf16[16,224,128]{2,1,0:T(8,128)(2,1)S(1)} %all_to_all.29.w_ref), channel_id=1, source_target_pairs={{0,8},{8,0},{1,9},{9,1},{2,10},{10,2},{3,11},{11,3},{4,12},{12,4},... | collective-permute-start | bytes 2752520 | tf_op jit(solution)/shard_map/ppermute | solution.py:323
  111.8 1.3 %shard_map.94 = (f32[16,128]{1,0:T(8,128)}, f32[16,128]{1,0:T(8,128)}) custom-call(s32[18]{0:T(128)S(1)} %pad_add_fusion.tab_ref, f32[1,128]{1,0:T(1,128)S(1)} %get-tuple-element.23.t_ref, f32[16,128]{1,0:T(8,128)S(1)} %get-tuple-element.24.h_ref, f32[16,128]{1,0:T(8,128)S(1)} %get-tuple-element.25.m_ref, f32[16,128]{1,0:T(8,128)S(1)} %get-tuple-element.26.v_ref), custom_call_target="tpu_custom_call" | custom-call | tf_op jit(solution)/shard_map/pallas_call | solution.py:354
  113.1 0.4 shard_map.92
  113.6 0.3 collective-permute-done.1.w_ref
  113.9 1.4 %shard_map.93 = (f32[6672,128]{1,0:T(8,128)S(1)}, f32[72,128]{1,0:T(8,128)S(1)}, bf16[6664,128]{1,0:T(8,128)(2,1)}) custom-call(bf16[16,224,128]{2,1,0:T(8,128)(2,1)S(1)} %collective-permute-done.1.w_ref, f32[6672,128]{1,0:T(8,128)S(1)} %get-tuple-element.20.rows_in, ...), custom_call_target="tpu_custom_call", output_to_operand_aliasing={{0}: (1, {}), {1}: (2, {})} | custom-call | tf_op jit(solution)/shard_map/pallas_call | solution.py:357
  (2 shorter events, 0.1 us)
Async XLA Ops:
  0.6 4.0 %copy-start.2 = (s32[6]{0:T(128)S(1)}, s32[6]{0:T(128)}, u32[]{:S(2)}) copy-start(s32[6]{0:T(128)} %param.11) | copy-start | bytes 76
  0.6 4.0 %copy-start.3 = (s32[6]{0:T(128)S(1)}, s32[6]{0:T(128)}, u32[]{:S(2)}) copy-start(s32[6]{0:T(128)} %param.10) | copy-start | bytes 76
  0.7 4.0 %copy-start.4 = (s32[6]{0:T(128)S(1)}, s32[6]{0:T(128)}, u32[]{:S(2)}) copy-start(s32[6]{0:T(128)} %param.9) | copy-start | bytes 76
  35.3 27.4 %copy-start = (f32[1666]{0:T(1024)S(1)}, f32[1666]{0:T(1024)}, u32[]{:S(2)}) copy-start(f32[1666]{0:T(1024)} %mf_ref.1) | copy-start | bytes 19996
  35.3 27.4 %copy-start.1 = (f32[1666]{0:T(1024)S(1)}, f32[1666]{0:T(1024)}, u32[]{:S(2)}) copy-start(f32[1666]{0:T(1024)} %vf_ref.1) | copy-start | bytes 19996
  35.4 3.4 %collective-permute-start = (f32[448,128]{1,0:T(8,128)S(1)}, f32[448,128]{1,0:T(8,128)S(1)}, u32[]{:S(2)}, u32[]{:S(2)}) collective-permute-start(f32[448,128]{1,0:T(8,128)S(1)} %shard_map.87), channel_id=1, source_target_pairs={{0,8},{8,0},{1,9},{9,1},{2,10},{10,2},{3,11},{11,3},{4,12},{12,4},... | collective-permute-start | bytes 688136 | tf_op jit(solution)/shard_map/ppermute | solution.py:323
  107.5 6.4 %collective-permute-start.1 = (bf16[16,224,128]{2,1,0:T(8,128)(2,1)S(1)}, bf16[16,224,128]{2,1,0:T(8,128)(2,1)S(1)}, u32[]{:S(2)}, u32[]{:S(2)}) collective-permute-start(bf16[16,224,128]{2,1,0:T(8,128)(2,1)S(1)} %all_to_all.29.w_ref), channel_id=1, source_target_pairs={{0,8},{8,0},{1,9},{9,1},{2,10},{10,2},{3,11},{11,3},{4,12},{12,4},... | collective-permute-start | bytes 2752520 | tf_op jit(solution)/shard_map/ppermute | solution.py:323

commit v10 on v9

--- a/solution.py
+++ b/solution.py
@@ -148,8 +148,9 @@
 def spread_kernel(a_ref, b_ref, o_ref, rows):
     rows[:HALF_ROWS, :] = a_ref[...] + b_ref[...]
     for k in range(N_WIDE):
-        o_ref[k, :TOUCHED, :] = rows[k * TOUCHED : (k + 1) * TOUCHED, :]
-        o_ref[k, TOUCHED:, :] = jnp.zeros((SLOT - TOUCHED, LANES), f32)
+        for r in range(TOUCHED):
+            at = k * TOUCHED + r
+            o_ref[k, :, r * LANES : (r + 1) * LANES] = rows[at : at + 1, :]
 
 
 def slot_positions():
@@ -186,9 +187,13 @@
 def owner_kernel(tab_ref, r_ref, mf_ref, vf_ref, o_ref, h_ref, m_ref, v_ref, turn):
     m_ref[...] = placed(mf_ref, turn)
     v_ref[...] = placed(vf_ref, turn)
-    g = r_ref[0]
+    flat = r_ref[0]
     for k in range(1, N_WIDE):
-        g = g + r_ref[k]
+        flat = flat + r_ref[k]
+    turn[TOUCHED:SLOT, :] = jnp.zeros((SLOT - TOUCHED, LANES), f32)
+    for r in range(TOUCHED):
+        turn[r : r + 1, :] = flat[:, r * LANES : (r + 1) * LANES]
+    g = turn[:SLOT, :]
     pos, valid = slot_positions()
     g = jnp.where(valid, g * (1.0 / 512.0), 0.0)
     m = m_ref[...]
@@ -325,13 +330,13 @@
 
 def shards(grads, master, velocity, layer_offsets, layer_sizes, lars_skip):
     tab = jnp.concatenate([layer_offsets, layer_sizes, lars_skip])
-    near, far, slot = (NEAR_ROWS, LANES), (SLOT, LANES), shape(SLOT, LANES)
+    near, slot = (NEAR_ROWS, LANES), shape(SLOT, LANES)
     sending, tab = lax.optimization_barrier((packed(grads), tab))
     received = lax.all_to_all(sending, AXES, 0, 0, axis_index_groups=cubes(), tiled=True)
     half = (HALF_ROWS, LANES)
     give = swapped(call(functools.partial(half_kernel, False), shape(*half), [VMEM])(received))
     keep = call(functools.partial(half_kernel, True), shape(*half), [VMEM])(received)
-    spread = call(spread_kernel, shape(N_WIDE, *far), [VMEM, VMEM], [(HALF_ROWS + SPARE, LANES)])(keep, give)
+    spread = call(spread_kernel, shape(N_WIDE, 1, TOUCHED * LANES), [VMEM, VMEM], [(HALF_ROWS + SPARE, LANES)])(keep, give)
     shared, h, m, v = call(
         owner_kernel,
         (shape(N_FAR, 2 * SLOT, LANES), slot, slot, slot),

time: 116 us -> 115 us (level)
  no operation moved by 1% of the time
where the time goes in v10:
time: 115 us
  blocking collectives  96.8 us (84%)
  Pallas kernels  9.22 us (8%)
  starting transfers between devices  6.19 us (5%)
  waiting for transfers between devices  1.67 us (1%)
    all_to_all x4, blocking collectives, sent(): return lax.all_to_all(x, axes, 0, 0, tiled=True)  66.3 us
    all_to_all x1, blocking collectives, shards(): lax.all_to_all(sending, AXES, 0, 0, axis_index_groups=cubes(), tiled=True)  30.5 us
    ppermute x2, starting transfers between devices, swapped(): return lax.ppermute(x, 'c', [(0, 1), (1, 0)])  6.19 us
    pallas_call x1, Pallas kernels, packed(): pl.pallas_call(pack_kernel, out_shape=shape(N_CUBE, NC * HALF_ROWS, LANES...  3.98 us
  transfers between devices with their start and end apart: 2, of which 2 were waited for; matrix products, arithmetic and copies ran while one was open for 0% of the time, Pallas kernels for 2%

profile of v10, /device:TPU:1, one launch (start us, length us, event | category | flops | bytes accessed | tf_op | source)
XLA Modules:
  0.0 114.7 jit_solution(16552757475009445360)
XLA Ops:
  0.6 0.0 copy-start.2
  0.6 0.0 copy-start.3
  0.7 0.0 copy-start.4
  0.7 4.0 %shard_map.85 = bf16[8,896,128]{2,1,0:T(8,128)(2,1)S(1)} custom-call(bf16[6664,1,128]{2,1,0:T(2,128)(2,1)} %bitcast.6), custom_call_target="tpu_custom_call" | custom-call | tf_op jit(solution)/shard_map/pallas_call | solution.py:104
  4.6 0.0 copy-done.2
  4.7 0.0 copy-done.3
  4.7 0.0 copy-done.4
  4.7 0.1 pad_add_fusion.tab_ref
  4.8 30.5 %all_to_all.25.r_ref = bf16[8,896,128]{2,1,0:T(8,128)(2,1)S(1)} all-to-all(bf16[8,896,128]{2,1,0:T(8,128)(2,1)S(1)} %shard_map.85), channel_id=1, replica_groups={{2,1,18,17,66,65,82,81},{4,3,20,19,68,67,84,83},{6,5,22,21,70,69,86,85}..., dimensions={0} | all-to-all | bytes 3670016 | tf_op jit(solution)/shard_map/all_to_all | solution.py:335
  35.3 0.0 copy-start
  35.3 0.0 copy-start.1
  35.3 0.1 shard_map.87
  35.4 1.9 %collective-permute-start = (f32[448,128]{1,0:T(8,128)S(1)}, f32[448,128]{1,0:T(8,128)S(1)}, u32[]{:S(2)}, u32[]{:S(2)}) collective-permute-start(f32[448,128]{1,0:T(8,128)S(1)} %shard_map.87), channel_id=1, source_target_pairs={{0,8},{8,0},{1,9},{9,1},{2,10},{10,2},{3,11},{11,3},{4,12},{12,4},... | collective-permute-start | bytes 688136 | tf_op jit(solution)/shard_map/ppermute | solution.py:328
  37.3 0.1 shard_map.86.a_ref
  37.5 1.3 %collective-permute-done.b_ref = f32[448,128]{1,0:T(8,128)S(1)} collective-permute-done((f32[448,128]{1,0:T(8,128)S(1)}, f32[448,128]{1,0:T(8,128)S(1)}, u32[]{:S(2)}, u32[]{:S(2)}) %collective-permute-start) | collective-permute-done | bytes 229408 | tf_op jit(solution)/shard_map/ppermute | solution.py:328
  38.8 0.2 shard_map.88
  39.0 23.5 %all_to_all.26.r_ref = f32[32,1,1792]{2,1,0:T(1,128)S(1)} all-to-all(f32[32,1,1792]{2,1,0:T(1,128)S(1)} %shard_map.88), channel_id=1, replica_groups=mesh['zh'=4,'zl'=2,'xh'=2,'xl'=2,'c'=2,'yh'=4,'yl'=2] {'zh','xh','yh'}, dimensions={0} | all-to-all | bytes 458752 | tf_op jit(solution)/shard_map/all_to_all | solution.py:324
  62.5 0.0 copy-done
  62.5 0.0 copy-done.1
  62.5 0.7 shard_map.89
  63.2 15.7 %all_to_all.27.s_ref = f32[16,32,128]{2,1,0:T(8,128)S(1)} all-to-all(f32[16,32,128]{2,1,0:T(8,128)S(1)} %get-tuple-element.18), channel_id=1, replica_groups=mesh['zh'=4,'zl'=2,'xh'=2,'xl'=2,'c'=2,'yh'=4,'yl'=2] {'zh','yh'}, dimensions={0} | all-to-all | bytes 524288 | tf_op jit(solution)/shard_map/all_to_all | solution.py:324
  79.0 11.7 %all_to_all.28.n_ref = f32[32,1,128]{2,1,0:T(1,128)S(1)} all-to-all(f32[32,1,128]{2,1,0:T(1,128)S(1)} %shard_map.90), channel_id=1, replica_groups=mesh['zh'=4,'zl'=2,'xh'=2,'xl'=2,'c'=2,'yh'=4,'yl'=2] {'zl','xh','xl','c..., dimensions={0} | all-to-all | bytes 32768 | tf_op jit(solution)/shard_map/all_to_all | solution.py:324
  90.7 0.9 shard_map.91
  91.6 15.4 %all_to_all.29.w_ref = bf16[16,224,128]{2,1,0:T(8,128)(2,1)S(1)} all-to-all(bf16[16,224,128]{2,1,0:T(8,128)(2,1)S(1)} %get-tuple-element.19), channel_id=1, replica_groups=mesh['zh'=4,'zl'=2,'xh'=2,'xl'=2,'c'=2,'yh'=4,'yl'=2] {'zl','xh','xl','yl'}, dimensions={0} | all-to-all | bytes 1835008 | tf_op jit(solution)/shard_map/all_to_all | solution.py:324
  107.0 4.3 %collective-permute-start.1 = (bf16[16,224,128]{2,1,0:T(8,128)(2,1)S(1)}, bf16[16,224,128]{2,1,0:T(8,128)(2,1)S(1)}, u32[]{:S(2)}, u32[]{:S(2)}) collective-permute-start(bf16[16,224,128]{2,1,0:T(8,128)(2,1)S(1)} %all_to_all.29.w_ref), channel_id=1, source_target_pairs={{0,8},{8,0},{1,9},{9,1},{2,10},{10,2},{3,11},{11,3},{4,12},{12,4},... | collective-permute-start | bytes 2752520 | tf_op jit(solution)/shard_map/ppermute | solution.py:328
  111.3 1.3 %shard_map.94 = (f32[16,128]{1,0:T(8,128)}, f32[16,128]{1,0:T(8,128)}) custom-call(s32[18]{0:T(128)S(1)} %pad_add_fusion.tab_ref, f32[1,128]{1,0:T(1,128)S(1)} %get-tuple-element.23.t_ref, f32[16,128]{1,0:T(8,128)S(1)} %get-tuple-element.24.h_ref, f32[16,128]{1,0:T(8,128)S(1)} %get-tuple-element.25.m_ref, f32[16,128]{1,0:T(8,128)S(1)} %get-tuple-element.26.v_ref), custom_call_target="tpu_custom_call" | custom-call | tf_op jit(solution)/shard_map/pallas_call | solution.py:359
  112.6 0.4 shard_map.92
  113.0 0.3 collective-permute-done.1.w_ref
  113.3 1.4 %shard_map.93 = (f32[6672,128]{1,0:T(8,128)S(1)}, f32[72,128]{1,0:T(8,128)S(1)}, bf16[6664,128]{1,0:T(8,128)(2,1)}) custom-call(bf16[16,224,128]{2,1,0:T(8,128)(2,1)S(1)} %collective-permute-done.1.w_ref, f32[6672,128]{1,0:T(8,128)S(1)} %get-tuple-element.20.rows_in, ...), custom_call_target="tpu_custom_call", output_to_operand_aliasing={{0}: (1, {}), {1}: (2, {})} | custom-call | tf_op jit(solution)/shard_map/pallas_call | solution.py:362
  (1 shorter events, 0.0 us)
Async XLA Ops:
  0.6 4.0 %copy-start.2 = (s32[6]{0:T(128)S(1)}, s32[6]{0:T(128)}, u32[]{:S(2)}) copy-start(s32[6]{0:T(128)} %param.11) | copy-start | bytes 76
  0.6 4.0 %copy-start.3 = (s32[6]{0:T(128)S(1)}, s32[6]{0:T(128)}, u32[]{:S(2)}) copy-start(s32[6]{0:T(128)} %param.10) | copy-start | bytes 76
  0.7 4.0 %copy-start.4 = (s32[6]{0:T(128)S(1)}, s32[6]{0:T(128)}, u32[]{:S(2)}) copy-start(s32[6]{0:T(128)} %param.9) | copy-start | bytes 76
  35.3 27.2 %copy-start = (f32[1666]{0:T(1024)S(1)}, f32[1666]{0:T(1024)}, u32[]{:S(2)}) copy-start(f32[1666]{0:T(1024)} %mf_ref.1) | copy-start | bytes 19996
  35.3 27.2 %copy-start.1 = (f32[1666]{0:T(1024)S(1)}, f32[1666]{0:T(1024)}, u32[]{:S(2)}) copy-start(f32[1666]{0:T(1024)} %vf_ref.1) | copy-start | bytes 19996
  35.4 3.4 %collective-permute-start = (f32[448,128]{1,0:T(8,128)S(1)}, f32[448,128]{1,0:T(8,128)S(1)}, u32[]{:S(2)}, u32[]{:S(2)}) collective-permute-start(f32[448,128]{1,0:T(8,128)S(1)} %shard_map.87), channel_id=1, source_target_pairs={{0,8},{8,0},{1,9},{9,1},{2,10},{10,2},{3,11},{11,3},{4,12},{12,4},... | collective-permute-start | bytes 688136 | tf_op jit(solution)/shard_map/ppermute | solution.py:328
  107.0 6.4 %collective-permute-start.1 = (bf16[16,224,128]{2,1,0:T(8,128)(2,1)S(1)}, bf16[16,224,128]{2,1,0:T(8,128)(2,1)S(1)}, u32[]{:S(2)}, u32[]{:S(2)}) collective-permute-start(bf16[16,224,128]{2,1,0:T(8,128)(2,1)S(1)} %all_to_all.29.w_ref), channel_id=1, source_target_pairs={{0,8},{8,0},{1,9},{9,1},{2,10},{10,2},{3,11},{11,3},{4,12},{12,4},... | collective-permute-start | bytes 2752520 | tf_op jit(solution)/shard_map/ppermute | solution.py:328
